TPU v7x, 32 devices: a whole 2x2x4 slice. The times are simulated.
32 devices in a mesh: dp: 4 (over z), seq: 8 (over y, x, core).
Axes of the slice: x: 2, y: 2, z: 4, core: 2. Of those that a mesh axis runs over, the one named last changes fastest.
Arguments:
- inputs: bfloat16 [32, 2048, 512], P('dp', 'seq'), may hold values from -6 to 6
- segments: int32 [32, 2048], P('dp'), may hold values from 0 to 7, never falling along the last dimension, each value on 1 to 1024 neighbouring positions
- w_qkv: bfloat16 [2, 512, 1536], P(None, ('dp', 'seq')), may hold values from -0.25 to 0.25
- w_out: bfloat16 [2, 512, 512], P(None, ('dp', 'seq')), may hold values from -1 to 1
- w_up: bfloat16 [2, 512, 2048], P(None, ('dp', 'seq')), may hold values from -0.25 to 0.25
- w_down: bfloat16 [2, 2048, 512], P(None, ('dp', 'seq')), may hold values from -0.125 to 0.125
- gain_attn: bfloat16 [2, 512], P(None, ('dp', 'seq')), may hold values from 0.5 to 1.5
- gain_mlp: bfloat16 [2, 512], P(None, ('dp', 'seq')), may hold values from 0.5 to 1.5
- cotangent: bfloat16 [32, 2048, 512], P('dp', 'seq'), may hold values from -6 to 6
Outputs:
- outputs: bfloat16 [32, 2048, 512], P('dp', 'seq')
- input_grad: float32 [32, 2048, 512], P('dp', 'seq')
- grad_qkv: float32 [2, 512, 1536], P(None, ('dp', 'seq'))
- grad_out: float32 [2, 512, 512], P(None, ('dp', 'seq'))
- grad_up: float32 [2, 512, 2048], P(None, ('dp', 'seq'))
- grad_down: float32 [2, 2048, 512], P(None, ('dp', 'seq'))
- grad_gain_attn: float32 [2, 512], P(None, ('dp', 'seq'))
- grad_gain_mlp: float32 [2, 512], P(None, ('dp', 'seq'))
Inputs may be any that keep to these rules, and one draw needn't show every extreme that they name: `segments`: in each sequence the ids never fall, each document has 1 to 1024 tokens, and one has exactly 1024.
All inputs are finite; a program needn't handle non-finite values.
Results may differ from a plain program's by a relative error of at most 0.017.
Values may be sent and summed in bfloat16 or wider, within the bound.
A program may use at most 256 MiB of HBM per device.

v0:
```python
import jax
import jax.numpy as jnp
from jax import lax
from jax.sharding import PartitionSpec as P

D = 512
HEADS = 8
HEAD = 64
SPAN = 128
MB = 2
SEQ_MB = 4


EPS = 1e-05
NEG = -1000000000.0


def layer_norm(values, gain):
    mean = jnp.mean(values, -1, keepdims=True)
    centred = values - mean
    var = jnp.mean(centred * centred, -1, keepdims=True)
    return centred * lax.rsqrt(var + EPS) * gain


def gelu(values):
    return (
        0.5
        * values
        * (1.0 + jnp.tanh(0.7978845608 * (values + 0.044715 * values * values * values)))
    )


def fetch_each(w_qkv, w_out, w_up, w_down, gain_attn, gain_mlp, layer):
    return (
        lax.all_gather(w_qkv[layer], ("dp", "seq"), axis=0, tiled=True),
        lax.all_gather(w_out[layer], ("dp", "seq"), axis=0, tiled=True),
        lax.all_gather(w_up[layer], ("dp", "seq"), axis=0, tiled=True),
        lax.all_gather(w_down[layer], ("dp", "seq"), axis=0, tiled=True),
        lax.all_gather(gain_attn[layer], ("dp", "seq"), axis=0, tiled=True),
        lax.all_gather(gain_mlp[layer], ("dp", "seq"), axis=0, tiled=True),
    )


def make_masks(seg_rows, stretch):
    batch = seg_rows.shape[0]
    spans_all = seg_rows.shape[1] // SPAN
    spans_own = stretch // SPAN
    rank = lax.axis_index("seq")
    local_seg = lax.dynamic_slice_in_dim(seg_rows, rank * stretch, stretch, 1).reshape(
        batch, spans_own, SPAN
    )
    ends = seg_rows.reshape(batch, spans_all, SPAN)[:, :, SPAN - 1]
    pos = jnp.arange(SPAN)
    near = (local_seg[..., :, None] == local_seg[..., None, :]) & (pos[:, None] >= pos[None, :])
    span_ids = rank * spans_own + jnp.arange(spans_own)
    far = (jnp.arange(spans_all)[None, None, None, :] < span_ids[None, :, None, None]) & (
        ends[:, None, None, :] == local_seg[..., None]
    )
    return (near[:, :, None], far[:, :, None])


def split_qkv(qkv):
    batch, stretch, _ = qkv.shape
    shape = (batch, stretch // SPAN, SPAN, HEADS, HEAD)
    return (
        qkv[..., :D].reshape(shape),
        qkv[..., D : 2 * D].reshape(shape),
        qkv[..., 2 * D :].reshape(shape),
    )


def raw_scores(query, keys, key_all, seg_rows, stretch):
    batch = query.shape[0]
    scale = HEAD ** (-0.5)
    key_wide = key_all.reshape(batch, -1, HEADS, HEAD)
    near = jnp.einsum("spqhe,spkhe->sphqk", query, keys, preferred_element_type=jnp.float32) * scale
    far = (
        jnp.einsum("spqhe,smhe->sphqm", query, key_wide, preferred_element_type=jnp.float32) * scale
    )
    near_mask, far_mask = make_masks(seg_rows, stretch)
    return (jnp.where(near_mask, near, NEG), jnp.where(far_mask, far, NEG))


def attend_forward(qkv, seg_rows):
    batch, stretch, _ = qkv.shape
    spans_own = stretch // SPAN
    query, keys, values = split_qkv(qkv)
    key_mean = jnp.mean(
        qkv[..., D : 2 * D].astype(jnp.float32).reshape(batch, spans_own, SPAN, D), 2
    ).astype(jnp.bfloat16)
    value_mean = jnp.mean(
        qkv[..., 2 * D :].astype(jnp.float32).reshape(batch, spans_own, SPAN, D), 2
    ).astype(jnp.bfloat16)
    key_all, value_all = (
        lax.all_gather(key_mean, "seq", axis=1, tiled=True),
        lax.all_gather(value_mean, "seq", axis=1, tiled=True),
    )
    near, far = raw_scores(query, keys, key_all, seg_rows, stretch)
    top = jnp.maximum(jnp.max(near, -1), jnp.max(far, -1))
    near_exp = jnp.exp(near - top[..., None])
    far_exp = jnp.exp(far - top[..., None])
    total = jnp.sum(near_exp, -1) + jnp.sum(far_exp, -1)
    lse = top + jnp.log(total)
    near_prob = (near_exp / total[..., None]).astype(jnp.bfloat16)
    far_prob = (far_exp / total[..., None]).astype(jnp.bfloat16)
    out = jnp.einsum("sphqk,spkhe->spqhe", near_prob, values, preferred_element_type=jnp.float32)
    out = out + jnp.einsum(
        "sphqm,smhe->spqhe",
        far_prob,
        value_all.reshape(batch, -1, HEADS, HEAD),
        preferred_element_type=jnp.float32,
    )
    return (out.reshape(batch, stretch, D).astype(jnp.bfloat16), key_all, value_all, lse)


def attend_backward(qkv, key_all, value_all, lse, seg_rows, dout):
    batch, stretch, _ = qkv.shape
    spans_own = stretch // SPAN
    scale = HEAD ** (-0.5)
    query, keys, values = split_qkv(qkv)
    key_wide = key_all.reshape(batch, -1, HEADS, HEAD)
    value_wide = value_all.reshape(batch, -1, HEADS, HEAD)
    near, far = raw_scores(query, keys, key_all, seg_rows, stretch)
    near_p = jnp.exp(near - lse[..., None])
    far_p = jnp.exp(far - lse[..., None])
    near_pb = near_p.astype(jnp.bfloat16)
    far_pb = far_p.astype(jnp.bfloat16)
    dout_r = dout.reshape(batch, spans_own, SPAN, HEADS, HEAD)
    dnear = jnp.einsum("spqhe,spkhe->sphqk", dout_r, values, preferred_element_type=jnp.float32)
    dfar = jnp.einsum("spqhe,smhe->sphqm", dout_r, value_wide, preferred_element_type=jnp.float32)
    rowdot = jnp.sum(near_p * dnear, -1) + jnp.sum(far_p * dfar, -1)
    gnear = (near_p * (dnear - rowdot[..., None])).astype(jnp.bfloat16)
    gfar = (far_p * (dfar - rowdot[..., None])).astype(jnp.bfloat16)
    dquery = jnp.einsum("sphqk,spkhe->spqhe", gnear, keys, preferred_element_type=jnp.float32)
    dquery = (
        dquery + jnp.einsum("sphqm,smhe->spqhe", gfar, key_wide, preferred_element_type=jnp.float32)
    ) * scale
    dkeys = (
        jnp.einsum("sphqk,spqhe->spkhe", gnear, query, preferred_element_type=jnp.float32) * scale
    )
    dvalues = jnp.einsum("sphqk,spqhe->spkhe", near_pb, dout_r, preferred_element_type=jnp.float32)
    dkey_all = (
        jnp.einsum("sphqm,spqhe->smhe", gfar, query, preferred_element_type=jnp.float32) * scale
    ).reshape(batch, -1, D)
    dvalue_all = jnp.einsum(
        "sphqm,spqhe->smhe", far_pb, dout_r, preferred_element_type=jnp.float32
    ).reshape(batch, -1, D)
    dkey_mean, dvalue_mean = (
        lax.psum_scatter(
            dkey_all.astype(jnp.bfloat16), "seq", scatter_dimension=1, tiled=True
        ).astype(jnp.float32),
        lax.psum_scatter(
            dvalue_all.astype(jnp.bfloat16), "seq", scatter_dimension=1, tiled=True
        ).astype(jnp.float32),
    )
    dkeys = dkeys.reshape(batch, spans_own, SPAN, D) + dkey_mean[:, :, None, :] * (1.0 / SPAN)
    dvalues = dvalues.reshape(batch, spans_own, SPAN, D) + dvalue_mean[:, :, None, :] * (1.0 / SPAN)
    joined = jnp.concatenate(
        [
            dquery.reshape(batch, stretch, D),
            dkeys.reshape(batch, stretch, D),
            dvalues.reshape(batch, stretch, D),
        ],
        -1,
    )
    return joined.astype(jnp.bfloat16)


def layer_forward(resid, seg_rows, weights):
    wq, wo, wu, wd, g_one, g_two = weights
    n_one = layer_norm(resid, g_one.astype(jnp.float32)).astype(jnp.bfloat16)
    qkv = jnp.dot(n_one, wq, preferred_element_type=jnp.float32).astype(jnp.bfloat16)
    attn_out, key_all, value_all, lse = attend_forward(qkv, seg_rows)
    hidden = resid + jnp.dot(attn_out, wo, preferred_element_type=jnp.float32)
    n_two = layer_norm(hidden, g_two.astype(jnp.float32)).astype(jnp.bfloat16)
    upper = jnp.dot(n_two, wu, preferred_element_type=jnp.float32)
    active = gelu(upper).astype(jnp.bfloat16)
    result = hidden + jnp.dot(active, wd, preferred_element_type=jnp.float32)
    return (
        result,
        (resid, n_one, qkv, key_all, value_all, lse, attn_out, hidden, n_two, upper, active),
    )


def layer_backward(dresult, seg_rows, weights, kept):
    wq, wo, wu, wd, g_one, g_two = weights
    resid, n_one, qkv, key_all, value_all, lse, attn_out, hidden, n_two, upper, active = kept
    ddown = dresult.astype(jnp.bfloat16)
    grad_wd = jnp.einsum("sci,sco->io", active, ddown, preferred_element_type=jnp.float32)
    dactive = jnp.einsum("sco,io->sci", ddown, wd, preferred_element_type=jnp.float32)
    _, pull = jax.vjp(gelu, upper)
    dupper = pull(dactive)[0].astype(jnp.bfloat16)
    grad_wu = jnp.einsum("sci,sco->io", n_two, dupper, preferred_element_type=jnp.float32)
    dn_two = jnp.einsum("sco,io->sci", dupper, wu, preferred_element_type=jnp.float32)
    _, pull = jax.vjp(layer_norm, hidden, g_two.astype(jnp.float32))
    dhidden_norm, grad_g_two = pull(dn_two)
    dhidden = dresult + dhidden_norm
    dattn = dhidden.astype(jnp.bfloat16)
    grad_wo = jnp.einsum("sci,sco->io", attn_out, dattn, preferred_element_type=jnp.float32)
    dout = jnp.einsum("sco,io->sci", dattn, wo, preferred_element_type=jnp.float32).astype(
        jnp.bfloat16
    )
    dqkv = attend_backward(qkv, key_all, value_all, lse, seg_rows, dout)
    grad_wq = jnp.einsum("sci,sco->io", n_one, dqkv, preferred_element_type=jnp.float32)
    dn_one = jnp.einsum("sco,io->sci", dqkv, wq, preferred_element_type=jnp.float32)
    _, pull = jax.vjp(layer_norm, resid, g_one.astype(jnp.float32))
    dresid_norm, grad_g_one = pull(dn_one)
    return (dhidden + dresid_norm, (grad_wq, grad_wo, grad_wu, grad_wd, grad_g_one, grad_g_two))


def add_trees(first, second):
    if first is None:
        return second
    return jax.tree.map(lambda left, right: left + right, first, second)


def on_device(inputs, segments, w_qkv, w_out, w_up, w_down, gain_attn, gain_mlp, cotangent):
    layers = w_qkv.shape[0]
    sums = [None] * layers
    results = []
    igrads = []
    for micro in range(MB):
        resid = inputs[micro * SEQ_MB : (micro + 1) * SEQ_MB].astype(jnp.float32)
        seg_rows = segments[micro * SEQ_MB : (micro + 1) * SEQ_MB]
        stored = []
        for index in range(layers):
            weights = fetch_each(w_qkv, w_out, w_up, w_down, gain_attn, gain_mlp, index)
            resid, kept = layer_forward(resid, seg_rows, weights)
            stored.append(kept)
        results.append(resid.astype(jnp.bfloat16))
        dresult = cotangent[micro * SEQ_MB : (micro + 1) * SEQ_MB].astype(jnp.float32)
        for index in reversed(range(layers)):
            weights = fetch_each(w_qkv, w_out, w_up, w_down, gain_attn, gain_mlp, index)
            dresult, wgrads = layer_backward(dresult, seg_rows, weights, stored[index])
            shares = (
                lax.psum_scatter(wgrads[0], ("dp", "seq"), scatter_dimension=0, tiled=True),
                lax.psum_scatter(wgrads[1], ("dp", "seq"), scatter_dimension=0, tiled=True),
                lax.psum_scatter(wgrads[2], ("dp", "seq"), scatter_dimension=0, tiled=True),
                lax.psum_scatter(wgrads[3], ("dp", "seq"), scatter_dimension=0, tiled=True),
                lax.psum_scatter(wgrads[4], ("dp", "seq"), scatter_dimension=0, tiled=True),
                lax.psum_scatter(wgrads[5], ("dp", "seq"), scatter_dimension=0, tiled=True),
            )
            sums[index] = add_trees(sums[index], tuple(shares))
        igrads.append(dresult)
    stacked = [jnp.stack([sums[index][member] for index in range(layers)]) for member in range(6)]
    return (
        jnp.concatenate(results, 0),
        jnp.concatenate(igrads, 0),
        stacked[0],
        stacked[1],
        stacked[2],
        stacked[3],
        stacked[4],
        stacked[5],
    )


def solution(mesh):
    in_specs = (
        P("dp", "seq", None),
        P("dp", None),
        P(None, ("dp", "seq"), None),
        P(None, ("dp", "seq"), None),
        P(None, ("dp", "seq"), None),
        P(None, ("dp", "seq"), None),
        P(None, ("dp", "seq")),
        P(None, ("dp", "seq")),
        P("dp", "seq", None),
    )
    out_specs = (
        P("dp", "seq", None),
        P("dp", "seq", None),
        P(None, ("dp", "seq"), None),
        P(None, ("dp", "seq"), None),
        P(None, ("dp", "seq"), None),
        P(None, ("dp", "seq"), None),
        P(None, ("dp", "seq")),
        P(None, ("dp", "seq")),
    )
    return jax.shard_map(
        on_device, mesh=mesh, in_specs=in_specs, out_specs=out_specs, check_vma=False
    )
```

profile of v0, /device:TPU:0, one launch (start us, length us, event | category | flops | bytes accessed | tf_op | source)
XLA Modules:
  0.0 1837.8 jit_solution(7540262130890583277)
XLA Ops:
  16.3 42.1 %all-reduce.17 = (bf16[512]{0:T(512)(128)(2,1)S(1)}, bf16[512]{0:T(512)(128)(2,1)S(1)}, bf16[512]{0:T(512)(128)(2,1)S(1)}, bf16[512]{0:T(512)(128)(2,1)S(1)}) all-reduce(bf16[512]{0:T(512)(128)(2,1)S(1)} %dynamic-update-slice, bf16[512]{0:T(512)(128)(2,1)S(1)} %dynamic-update-slice.1, ...), channel_id=2, replica_groups=mesh['dp'=4,'seq'=8] {'dp','seq'}, use_global_device_ids=true, to_apply=%add | all-reduce | flops 2048 | bytes 8192
  63.9 44.5 %all-gather.8 = bf16[1,512,512]{2,1,0:T(8,128)(2,1)} all-gather(bf16[1,16,512]{2,1,0:T(8,128)(2,1)S(1)} %get-tuple-element.101), channel_id=10, replica_groups=mesh['dp'=4,'seq'=8] {'dp','seq'}, dimensions={1}, use_global_device_ids=true | all-gather | bytes 540672 | tf_op jit(solution)/shard_map/all_gather | solution.py:36
  108.4 41.2 %all-gather.2 = bf16[1,512,512]{2,1,0:T(8,128)(2,1)} all-gather(bf16[1,16,512]{2,1,0:T(8,128)(2,1)S(1)} %get-tuple-element.102), channel_id=4, replica_groups=mesh['dp'=4,'seq'=8] {'dp','seq'}, dimensions={1}, use_global_device_ids=true | all-gather | bytes 540672 | tf_op jit(solution)/shard_map/all_gather | solution.py:36
  164.5 9.1 all_gather.112
  174.3 8.6 all_gather.113
  205.0 9.1 all_gather.42
  214.8 8.4 all_gather.43
  269.3 8.0 fusion.117
  277.4 7.5 fusion.347
  307.9 9.1 all_gather.114
  317.6 8.4 all_gather.115
  357.1 9.1 all_gather.50
  366.8 8.4 all_gather.51
  377.0 4.3 reshape.830
  411.7 8.0 fusion.96
  419.7 5.8 fusion.98
  425.5 10.9 fusion.15
  436.4 12.1 fusion.7
  483.5 5.2 fusion.130
  510.5 4.8 reshape.802
  519.1 5.0 reshape.812
  524.1 6.0 multiply_convert_fusion.5
  530.9 4.6 multiply_bitcast_fusion.1
  538.2 4.0 reshape.809
  546.0 4.8 reshape.810
  550.8 6.0 multiply_convert_fusion.7
  557.6 4.6 multiply_bitcast_fusion.3
  565.0 4.1 reshape.799
  572.8 4.9 reshape.800
  580.8 48.8 %all-reduce.25.cloned.1.call-done = (bf16[4,16,512]{2,0,1:T(4,128)(2,1)}, bf16[4,16,512]{2,0,1:T(4,128)(2,1)}, bf16[4,16,512]{2,0,1:T(4,128)(2,1)}, bf16[4,16,512]{2,0,1:T(4,128)(2,1)}) async-done(((bf16[4,16,512]{2,0,1:T(4,128)(2,1)}, bf16[4,16,512]{2,0,1:T(4,128)(2,1)}, bf16[4,16,512]{2,0,1:T(4,128)(2,1)}, bf16[4,16,512]{2,0,1:T(4,128)(2,1)}), (bf16[4,16,512]{2,0,1:T(4,128)(2,1)}, ...) | async-done | bytes 262160
  652.1 8.7 fusion.11
  660.8 11.8 fusion.3
  705.5 5.6 multiply_reduce_fusion
  734.0 5.6 fusion.133
  739.6 5.0 multiply_convert_fusion.4
  752.2 5.1 fusion.139
  757.3 4.2 copy.1019
  761.5 4.9 reshape.807
  769.2 4.8 reshape.817
  781.7 4.1 reshape.814
  792.5 4.8 reshape.815
  798.1 4.7 multiply_convert_fusion.6
  805.6 4.1 reshape.804
  812.6 4.0 copy.1017
  816.6 5.0 reshape.805
  837.0 6.0 fusion.235
  843.0 9.4 bitcast_add_fusion
  852.5 6.7 fusion.253
  859.2 9.6 bitcast_add_fusion.1
  869.5 5.5 fusion.287
  875.1 4.5 bitcast_add_fusion.2
  880.2 5.5 fusion.286
  885.7 4.6 bitcast_add_fusion.3
  891.0 7.6 add_convert_fusion
  898.6 6.3 add_convert_fusion.1
  914.6 39.4 %all-reduce.16 = (f32[512]{0:T(512)S(1)}, f32[512]{0:T(512)S(1)}, f32[512]{0:T(512)S(1)}, f32[512]{0:T(512)S(1)}) all-reduce(f32[512]{0:T(512)S(1)} %add.614, f32[512]{0:T(512)S(1)} %add.613, f32[512]{0:T(512)S(1)} %add.616, f32[512]{0:T(512)S(1)} %add.615), channel_id=43, replica_groups=mesh['dp'=4,'seq'=8] {'dp','seq'}, use_global_device_ids=true, to_apply=%region_93.94.clone | all-reduce | flops 2048 | bytes 16384
  955.4 5.8 add_add_fusion.12
  963.7 89.2 %reduce-scatter.13.cloned.1.call-done = f32[16,512]{1,0:T(8,128)} async-done(((f32[512,512]{1,0:T(8,128)}), f32[16,512]{1,0:T(8,128)}) %reduce-scatter.13.cloned.1.call-update) | async-done | bytes 32784 | tf_op jit(solution)/shard_map/reduce_scatter | solution.py:237
  1054.3 102.1 %reduce-scatter.11.cloned.1.call-done = f32[16,1536]{1,0:T(8,128)} async-done(((f32[512,1536]{1,0:T(8,128)}), f32[16,1536]{1,0:T(8,128)}) %reduce-scatter.11.cloned.1.call-update) | async-done | bytes 98320 | tf_op jit(solution)/shard_map/reduce_scatter | solution.py:236
  1156.4 106.5 %reduce-scatter.9.cloned.1.call-done = f32[16,1536]{1,0:T(8,128)} async-done(((f32[512,1536]{1,0:T(8,128)}), f32[16,1536]{1,0:T(8,128)}) %reduce-scatter.9.cloned.1.call-update) | async-done | bytes 98320 | tf_op jit(solution)/shard_map/reduce_scatter | solution.py:236
  1264.6 142.4 %reduce-scatter.23.cloned.1.call-done = f32[64,512]{1,0:T(8,128)} async-done(((f32[2048,512]{1,0:T(8,128)}), f32[64,512]{1,0:T(8,128)}) %reduce-scatter.23.cloned.1.call-update) | async-done | bytes 131088 | tf_op jit(solution)/shard_map/reduce_scatter | solution.py:239
  1407.0 140.9 %reduce-scatter.21.cloned.1.call-done = f32[64,512]{1,0:T(8,128)} async-done(((f32[2048,512]{1,0:T(8,128)}), f32[64,512]{1,0:T(8,128)}) %reduce-scatter.21.cloned.1.call-update) | async-done | bytes 131088 | tf_op jit(solution)/shard_map/reduce_scatter | solution.py:239
  1549.6 139.0 %reduce-scatter.19.cloned.1.call-done = f32[16,2048]{1,0:T(8,128)} async-done(((f32[512,2048]{1,0:T(8,128)}), f32[16,2048]{1,0:T(8,128)}) %reduce-scatter.19.cloned.1.call-update) | async-done | bytes 131088 | tf_op jit(solution)/shard_map/reduce_scatter | solution.py:238
  1688.6 140.8 %reduce-scatter.17.cloned.1.call-done = f32[16,2048]{1,0:T(8,128)} async-done(((f32[512,2048]{1,0:T(8,128)}), f32[16,2048]{1,0:T(8,128)}) %reduce-scatter.17.cloned.1.call-update) | async-done | bytes 131088 | tf_op jit(solution)/shard_map/reduce_scatter | solution.py:238
  (896 shorter events, 407.9 us)
Async XLA Ops:
  7.2 55.0 %copy-start.8 = (bf16[8,256,512]{2,1,0:T(8,128)(2,1)S(1)}, bf16[8,256,512]{2,1,0:T(8,128)(2,1)}, u32[]{:S(2)}) copy-start(bf16[8,256,512]{2,1,0:T(8,128)(2,1)} %param.9) | copy-start | bytes 6291460
  7.2 144.6 %all-gather.19.cloned.1.call-start = ((), (), s32[]{:S(2)}) async-start(), calls=%async_computation.8 | async-start | bytes 1622016 | tf_op jit(solution)/shard_map/all_gather | solution.py:35
  8.9 260.4 %all-gather.21.cloned.1.call-start = ((), (), s32[]{:S(2)}) async-start(), calls=%async_computation.9 | async-start | bytes 2162688 | tf_op jit(solution)/shard_map/all_gather | solution.py:37
  10.5 266.9 %all-gather.23.cloned.1.call-start = ((), (), s32[]{:S(2)}) async-start(), calls=%async_computation.10 | async-start | bytes 2162688 | tf_op jit(solution)/shard_map/all_gather | solution.py:38
  12.1 273.3 %all-gather.25.cloned.1.call-start = ((), (), s32[]{:S(2)}) async-start(), calls=%async_computation.11 | async-start | bytes 1622016 | tf_op jit(solution)/shard_map/all_gather | solution.py:35
  12.6 399.0 %all-gather.27.cloned.1.call-start = ((), (), s32[]{:S(2)}) async-start(), calls=%async_computation.12 | async-start | bytes 2162688 | tf_op jit(solution)/shard_map/all_gather | solution.py:37
  13.2 412.3 %all-gather.29.cloned.1.call-start = ((), (), s32[]{:S(2)}) async-start(), calls=%async_computation.13 | async-start | bytes 2162688 | tf_op jit(solution)/shard_map/all_gather | solution.py:38
  13.8 615.8 %all-reduce.25.cloned.1.call-start = ((), (), s32[]{:S(2)}) async-start(), calls=%async_computation.23 | async-start | bytes 524288
  58.4 98.6 %copy-start.233 = (f32[512]{0:T(512)}, f32[512]{0:T(512)S(1)}, u32[]{:S(2)}) copy-start(f32[512]{0:T(512)S(1)} %convert_element_type.478) | copy-start | bytes 6148
  62.1 87.4 %copy-start.259 = (u32[32]{0:T(128)S(1)}, u32[32]{0:T(128)}, u32[]{:S(2)}) copy-start(u32[32]{0:T(128)} %constant.103) | copy-start | bytes 388
  62.1 89.7 %copy-start.195 = (f32[4,256]{1,0:T(4,128)}, f32[4,256]{1,0:T(4,128)S(1)}, u32[]{:S(2)}) copy-start(f32[4,256]{1,0:T(4,128)S(1)} %get-tuple-element.169) | copy-start | bytes 12292
  62.1 94.9 %copy-start.197 = (f32[4,256]{1,0:T(4,128)}, f32[4,256]{1,0:T(4,128)S(1)}, u32[]{:S(2)}) copy-start(f32[4,256]{1,0:T(4,128)S(1)} %get-tuple-element.170) | copy-start | bytes 12292
  63.1 93.9 %copy-start.202 = (f32[4,256]{1,0:T(4,128)}, f32[4,256]{1,0:T(4,128)S(1)}, u32[]{:S(2)}) copy-start(f32[4,256]{1,0:T(4,128)S(1)} %fusion.316) | copy-start | bytes 12292
  63.1 88.7 %copy-start.204 = (f32[4,256]{1,0:T(4,128)}, f32[4,256]{1,0:T(4,128)S(1)}, u32[]{:S(2)}) copy-start(f32[4,256]{1,0:T(4,128)S(1)} %fusion.320) | copy-start | bytes 12292
  151.8 89.0 %copy-start.177 = (pred[4,2,128,16]{2,3,1,0:T(8,128)(4,1)}, pred[4,2,128,16]{2,3,1,0:T(8,128)(4,1)S(1)}, u32[]{:S(2)}) copy-start(pred[4,2,128,16]{2,3,1,0:T(8,128)(4,1)S(1)} %get-tuple-element.113) | copy-start | bytes 49156
  164.5 92.8 %copy-start.39 = (bf16[4,2,128,8,64]{2,1,4,3,0:T(2,128)(2,1)}, bf16[4,2,128,8,64]{2,1,4,3,0:T(2,128)(2,1)S(1)}, u32[]{:S(2)}) copy-start(bf16[4,2,128,8,64]{2,1,4,3,0:T(2,128)(2,1)S(1)} %reshape.669) | copy-start | bytes 3145732
  184.8 71.8 %copy-start.102 = (bf16[4,16,8,64]{3,2,1,0:T(8,128)(2,1)}, bf16[4,16,8,64]{3,2,1,0:T(8,128)(2,1)S(1)}, u32[]{:S(2)}) copy-start(bf16[4,16,8,64]{3,2,1,0:T(8,128)(2,1)S(1)} %reshape.674) | copy-start | bytes 196612
  256.0 35.3 %copy-start.161 = (f32[4,256]{1,0:T(4,128)}, f32[4,256]{1,0:T(4,128)S(1)}, u32[]{:S(2)}) copy-start(f32[4,256]{1,0:T(4,128)S(1)} %broadcast_multiply_fusion.6) | copy-start | bytes 12292
  256.5 34.8 %copy-start.169 = (f32[4,256]{1,0:T(4,128)}, f32[4,256]{1,0:T(4,128)S(1)}, u32[]{:S(2)}) copy-start(f32[4,256]{1,0:T(4,128)S(1)} %fusion.317) | copy-start | bytes 12292
  267.5 9.8 copy-start.163
  269.2 8.1 copy-start.218
  269.2 8.1 copy-start.171
  406.1 49.8 %copy-start.165 = (f32[4,256]{1,0:T(4,128)}, f32[4,256]{1,0:T(4,128)S(1)}, u32[]{:S(2)}) copy-start(f32[4,256]{1,0:T(4,128)S(1)} %broadcast_multiply_fusion) | copy-start | bytes 12292
  409.2 46.6 %copy-start.167 = (f32[4,256]{1,0:T(4,128)}, f32[4,256]{1,0:T(4,128)S(1)}, u32[]{:S(2)}) copy-start(f32[4,256]{1,0:T(4,128)S(1)} %broadcast_multiply_fusion.4) | copy-start | bytes 12292
  411.6 44.3 %copy-start.173 = (f32[4,256]{1,0:T(4,128)}, f32[4,256]{1,0:T(4,128)S(1)}, u32[]{:S(2)}) copy-start(f32[4,256]{1,0:T(4,128)S(1)} %fusion.323) | copy-start | bytes 12292
  411.6 44.3 %copy-start.175 = (f32[4,256]{1,0:T(4,128)}, f32[4,256]{1,0:T(4,128)S(1)}, u32[]{:S(2)}) copy-start(f32[4,256]{1,0:T(4,128)S(1)} %fusion.319) | copy-start | bytes 12292
  411.6 8.1 copy-start.14
  411.6 8.1 copy-start.189
  411.7 8.0 copy-start.253
  425.5 10.9 copy-start.66
  425.5 10.9 copy-start.247
  436.4 14.5 copy-start.82
  436.4 12.1 copy-start.254
  467.0 5.7 copy-start.81
  524.1 6.0 copy-start.184
  550.8 6.0 copy-start.183
  550.8 6.8 copy-start.43
  577.8 243.9 %all-reduce.23.cloned.1.call-start = ((), (), s32[]{:S(2)}) async-start(), calls=%async_computation.22 | async-start | bytes 524288
  634.5 6.1 copy-start.116
  644.7 7.2 slice-start
  651.9 8.9 copy-start.20
  651.9 30.8 %copy-start.23 = (f32[4,256,512]{2,1,0:T(8,128)}, f32[4,256,512]{2,1,0:T(8,128)S(1)}, u32[]{:S(2)}) copy-start(f32[4,256,512]{2,1,0:T(8,128)S(1)} %get-tuple-element.88) | copy-start | bytes 6291460
  660.8 14.3 copy-start.85
  660.8 11.8 copy-start.250
  688.6 6.8 copy-start.46
  701.8 9.2 copy-start.44
  726.0 237.7 %reduce-scatter.15.cloned.1.call-start = ((), (), s32[]{:S(2)}) async-start(), calls=%async_computation.17 | async-start | bytes 1081344 | tf_op jit(solution)/shard_map/reduce_scatter | solution.py:237
  729.6 323.2 %reduce-scatter.13.cloned.1.call-start = ((), (), s32[]{:S(2)}) async-start(), calls=%async_computation.16 | async-start | bytes 1081344 | tf_op jit(solution)/shard_map/reduce_scatter | solution.py:237
  733.9 422.5 %reduce-scatter.11.cloned.1.call-start = ((), (), s32[]{:S(2)}) async-start(), calls=%async_computation.15 | async-start | bytes 3244032 | tf_op jit(solution)/shard_map/reduce_scatter | solution.py:236
  751.0 512.0 %reduce-scatter.9.cloned.1.call-start = ((), (), s32[]{:S(2)}) async-start(), calls=%async_computation.14 | async-start | bytes 3244032 | tf_op jit(solution)/shard_map/reduce_scatter | solution.py:236
  816.6 8.0 copy-start.75
  825.0 8.2 copy-start.128
  836.9 570.1 %reduce-scatter.23.cloned.1.call-start = ((), (), s32[]{:S(2)}) async-start(), calls=%async_computation.21 | async-start | bytes 4325376 | tf_op jit(solution)/shard_map/reduce_scatter | solution.py:239
  837.0 6.1 copy-start.68
  852.4 695.4 %reduce-scatter.21.cloned.1.call-start = ((), (), s32[]{:S(2)}) async-start(), calls=%async_computation.20 | async-start | bytes 4325376 | tf_op jit(solution)/shard_map/reduce_scatter | solution.py:239
  852.5 6.7 copy-start.22
  868.8 6.2 copy-start.166
  868.9 6.2 copy-start.174
  868.9 819.7 %reduce-scatter.19.cloned.1.call-start = ((), (), s32[]{:S(2)}) async-start(), calls=%async_computation.19 | async-start | bytes 4325376 | tf_op jit(solution)/shard_map/reduce_scatter | solution.py:238
  879.6 949.7 %reduce-scatter.17.cloned.1.call-start = ((), (), s32[]{:S(2)}) async-start(), calls=%async_computation.18 | async-start | bytes 4325376 | tf_op jit(solution)/shard_map/reduce_scatter | solution.py:238
  891.0 7.6 copy-start.16
  891.0 7.6 copy-start.248
  912.0 43.4 %copy-start.229 = (f32[4,256]{1,0:T(4,128)S(1)}, f32[4,256]{1,0:T(4,128)}, u32[]{:S(2)}) copy-start(f32[4,256]{1,0:T(4,128)} %copy-done.228) | copy-start | bytes 12292
  912.0 43.4 %copy-start.231 = (f32[4,256]{1,0:T(4,128)S(1)}, f32[4,256]{1,0:T(4,128)}, u32[]{:S(2)}) copy-start(f32[4,256]{1,0:T(4,128)} %copy-done.230) | copy-start | bytes 12292
  (215 other events, 633.6 us)
Sparse Core Ops, SparseCore 0:
  11.4 57.6 all-gather.18
  72.0 55.7 all-gather.20
  131.2 55.8 all-gather.22
  189.8 53.7 all-gather.24
  246.3 55.1 all-gather.26
  304.3 55.0 all-gather.28
  577.9 51.6 all-reduce.24
  726.1 53.7 all-reduce.22
  782.2 136.0 reduce-scatter.14
  920.3 132.5 reduce-scatter.12
  1058.3 98.0 reduce-scatter.10
  1161.7 101.2 reduce-scatter.8
  1265.3 141.6 reduce-scatter.22
  1409.1 138.6 reduce-scatter.20
  1550.0 138.5 reduce-scatter.18
  1690.7 138.5 reduce-scatter.16
where the time goes:
time: 1850 us; the launch traced here: 1840 us
  waiting for transfers between devices  912 us (49%)
  matrix products  311 us (17%)
  local copies, waits for them, and re-layouts  272 us (15%)
  blocking collectives  237 us (13%)
  other arithmetic  86 us (5%)
    reduce_scatter x2, waiting for transfers between devices, on_device(): lax.psum_scatter(wgrads[3], ('dp', 'seq'), scatter_dimension=0, tiled=True)  283 us
    reduce_scatter x2, waiting for transfers between devices, on_device(): lax.psum_scatter(wgrads[2], ('dp', 'seq'), scatter_dimension=0, tiled=True)  280 us
    reduce_scatter x2, waiting for transfers between devices, on_device(): lax.psum_scatter(wgrads[0], ('dp', 'seq'), scatter_dimension=0, tiled=True)  209 us
    reduce_scatter x2, waiting for transfers between devices, on_device(): lax.psum_scatter(wgrads[1], ('dp', 'seq'), scatter_dimension=0, tiled=True)  89.2 us
    all_gather x2, blocking collectives, fetch_each(): lax.all_gather(w_out[layer], ('dp', 'seq'), axis=0, tiled=True)  85.6 us
    unnamed x2, blocking collectives  81.5 us
    unnamed x18, waiting for transfers between devices  50.6 us
    dot_general x4, matrix products, layer_backward(): jnp.einsum('sco,io->sci', ddown, wd, preferred_element_type=jnp.float32)  43.5 us
  transfers between devices with their start and end apart: 16, of which 8 were waited for; matrix products, arithmetic and copies ran while one was open for 22% of the time, Pallas kernels for 0%

commit v1 on v0

v1 whole, which is shorter than its diff:
```python
import functools

import jax
import jax.numpy as jnp
from jax import lax
from jax.experimental import pallas as pl
from jax.experimental.pallas import tpu as pltpu
from jax.sharding import PartitionSpec as P

D = 512
HEADS = 8
HEAD = 64
SPAN = 128
PAIRS = HEADS // 2
EPS = 1e-05
NEG = -1000000000.0
SCALE = HEAD ** (-0.5)
F32 = jnp.float32
BF16 = jnp.bfloat16
CHUNK = 512
VMEM_LIMIT = 60 * 1024 * 1024

NN = (((1,), (0,)), ((), ()))
NT = (((1,), (1,)), ((), ()))
TN = (((0,), (0,)), ((), ()))


def dot(left, right, dims=NN):
    return lax.dot_general(left, right, dims, preferred_element_type=F32)


def normed(values):
    mean = jnp.mean(values, -1, keepdims=True)
    centred = values - mean
    var = jnp.mean(centred * centred, -1, keepdims=True)
    rstd = lax.rsqrt(var + EPS)
    return centred * rstd, rstd


def norm_backward(dnorm, unit, rstd, gain):
    grad_gain = jnp.sum(dnorm * unit, 0, keepdims=True)
    scaled = dnorm * gain
    first = jnp.mean(scaled, -1, keepdims=True)
    second = jnp.mean(scaled * unit, -1, keepdims=True)
    return rstd * (scaled - first - unit * second), grad_gain


def project_qkv(x32, gain, wq_ref, qkv_ref, sums_ref):
    unit, _ = normed(x32)
    n_one = (unit * gain).astype(BF16)
    spans = x32.shape[0] // SPAN
    for part in range(3):
        block = dot(n_one, wq_ref[:, part * D : (part + 1) * D]).astype(BF16)
        qkv_ref[0, :, part * D : (part + 1) * D] = block
        if part > 0:
            wide = block.astype(F32)
            for span in range(spans):
                mean = jnp.sum(wide[span * SPAN : (span + 1) * SPAN], 0, keepdims=True) * (1.0 / SPAN)
                sums_ref[0, span : span + 1, (part - 1) * D : part * D] = mean.astype(BF16)


def lane_halves():
    lane = lax.broadcasted_iota(jnp.int32, (1, 2 * HEAD), 1)
    low = lane < HEAD
    return low


def head_stack(block, low, factor):
    one = jnp.where(low, factor, 0.0).astype(BF16)
    two = jnp.where(low, 0.0, factor).astype(BF16)
    return jnp.concatenate([block * one, block * two], 0)


def pair_operands(qkv_ref, sums_ref, span, pair):
    rows = slice(span * SPAN, (span + 1) * SPAN)
    lanes = slice(pair * 128, (pair + 1) * 128)
    keys = jnp.concatenate(
        [qkv_ref[0, rows, D + pair * 128 : D + (pair + 1) * 128], sums_ref[0, :, lanes]], 0
    )
    values = jnp.concatenate(
        [
            qkv_ref[0, rows, 2 * D + pair * 128 : 2 * D + (pair + 1) * 128],
            sums_ref[0, :, D + pair * 128 : D + (pair + 1) * 128],
        ],
        0,
    )
    query = qkv_ref[0, rows, lanes]
    return query, keys, values


def attention_forward(qkv_ref, sums_ref, bias_ref, prob_ref, o_ref):
    low = lane_halves()
    spans = qkv_ref.shape[1] // SPAN
    for span in range(spans):
        bias = bias_ref[0, span]
        bias = jnp.concatenate([bias, bias], 1)
        for pair in range(PAIRS):
            query, keys, values = pair_operands(qkv_ref, sums_ref, span, pair)
            scores = dot(keys, head_stack(query, low, SCALE), NT) + bias
            top = jnp.max(scores, 0, keepdims=True)
            exps = jnp.exp(scores - top)
            total = jnp.sum(exps, 0, keepdims=True)
            prob = (exps * (1.0 / total)).astype(BF16)
            prob_ref[0, span, pair] = prob
            both = dot(prob, values, TN)
            o_ref[0, span * SPAN : (span + 1) * SPAN, pair * 128 : (pair + 1) * 128] = jnp.where(
                low, both[:SPAN], both[SPAN:]
            ).astype(BF16)


def attention_backward(qkv_ref, sums_ref, prob_ref, dout, dqkv_ref, dsums_ref):
    low = lane_halves()
    spans = qkv_ref.shape[1] // SPAN
    for pair in range(PAIRS):
        lanes = slice(pair * 128, (pair + 1) * 128)
        klanes = slice(D + pair * 128, D + (pair + 1) * 128)
        vlanes = slice(2 * D + pair * 128, 2 * D + (pair + 1) * 128)
        dksum = dvsum = 0.0
        for span in range(spans):
            rows = slice(span * SPAN, (span + 1) * SPAN)
            query, keys, values = pair_operands(qkv_ref, sums_ref, span, pair)
            q_stack = head_stack(query, low, SCALE)
            do_stack = head_stack(dout[rows, lanes], low, 1.0)
            prob = prob_ref[0, span, pair]
            wide = prob.astype(F32)
            dprob = dot(values, do_stack, NT)
            rowdot = jnp.sum(wide * dprob, 0, keepdims=True)
            dscore = (wide * (dprob - rowdot)).astype(BF16)
            dboth = dot(dscore, keys, TN)
            dquery = jnp.where(low, dboth[:SPAN], dboth[SPAN:]) * SCALE
            dkeys = dot(dscore, q_stack)
            dvalues = dot(prob, do_stack)
            dqkv_ref[0, rows, lanes] = dquery.astype(BF16)
            dqkv_ref[0, rows, klanes] = dkeys[:SPAN].astype(BF16)
            dqkv_ref[0, rows, vlanes] = dvalues[:SPAN].astype(BF16)
            dksum = dksum + dkeys[SPAN:]
            dvsum = dvsum + dvalues[SPAN:]
        dsums_ref[0, :, pair * 128 : (pair + 1) * 128] = dksum.astype(BF16)
        dsums_ref[0, :, D + pair * 128 : D + (pair + 1) * 128] = dvsum.astype(BF16)


G0 = 0.7978845608
G1 = 0.7978845608 * 0.044715


def gelu(values):
    squared = values * values
    slope = jnp.tanh(values * (G0 + G1 * squared))
    half = 0.5 * values
    return half + half * slope


def gelu_both(values):
    squared = values * values
    slope = jnp.tanh(values * (G0 + G1 * squared))
    half = 0.5 * values
    rise = 0.5 + 0.5 * slope
    inner = G0 + (3.0 * G1) * squared
    return values * rise, rise + half * (1.0 - slope * slope) * inner


def mlp_forward(h32, gain, wu_ref, wd_ref, u_ref):
    unit, _ = normed(h32)
    n_two = (unit * gain).astype(BF16)
    total = h32
    for start in range(0, wu_ref.shape[1], CHUNK):
        upper = dot(n_two, wu_ref[:, start : start + CHUNK])
        u_ref[0, :, start : start + CHUNK] = upper.astype(BF16)
        total = total + dot(gelu(upper).astype(BF16), wd_ref[start : start + CHUNK, :])
    return total


def first_kernel(x_ref, gain_ref, wq_ref, qkv_ref, sums_ref):
    project_qkv(x_ref[0].astype(F32), gain_ref[...], wq_ref, qkv_ref, sums_ref)


def layer_kernel(last, *refs):
    if last:
        (x_ref, qkv_ref, sums_ref, bias_ref, gain_ref, wo_ref, wu_ref, wd_ref,
         prob_ref, o_ref, h_ref, u_ref, next_ref) = refs
    else:
        (x_ref, qkv_ref, sums_ref, bias_ref, gain_ref, wo_ref, wu_ref, wd_ref, gain_next_ref, wq_ref,
         prob_ref, o_ref, h_ref, u_ref, next_ref, qkv_next_ref, sums_next_ref) = refs
    attention_forward(qkv_ref, sums_ref, bias_ref, prob_ref, o_ref)
    hidden = x_ref[0].astype(F32) + dot(o_ref[0], wo_ref[...])
    h_ref[0] = hidden
    result = mlp_forward(hidden, gain_ref[...], wu_ref, wd_ref, u_ref)
    next_ref[0] = result.astype(next_ref.dtype)
    if not last:
        project_qkv(result, gain_next_ref[...], wq_ref, qkv_next_ref, sums_next_ref)


def accumulate(ref, index, value, first):
    @pl.when(first)
    def _():
        ref[index] = value

    @pl.when(jnp.logical_not(first))
    def _():
        ref[index] = ref[index] + value


def mlp_attention_backward(dy32, u_ref, h_ref, o_ref, prob_ref, qkv_ref, sums_ref, gain_ref,
                           wo_ref, wu_ref, wd_ref, dh_ref, dqkv_ref, dsums_ref, gd_ref, gu_ref,
                           go_ref, gg_ref):
    ddown = dy32.astype(BF16)
    unit, rstd = normed(h_ref[0])
    n_two = (unit * gain_ref[...]).astype(BF16)
    dn_two = 0.0
    for start in range(0, wu_ref.shape[1], CHUNK):
        cols = slice(start, start + CHUNK)
        dactive = dot(ddown, wd_ref[cols, :], NT)
        active, slope = gelu_both(u_ref[0, :, cols].astype(F32))
        gd_ref[cols, :] += dot(active.astype(BF16), ddown, TN)
        dupper = (dactive * slope).astype(BF16)
        gu_ref[:, cols] += dot(n_two, dupper, TN)
        dn_two = dn_two + dot(dupper, wu_ref[:, cols], NT)
    dnorm, grad_gain = norm_backward(dn_two, unit, rstd, gain_ref[...])
    gg_ref[...] += grad_gain
    dhidden = dy32 + dnorm
    dh_ref[0] = dhidden
    dattn = dhidden.astype(BF16)
    go_ref[...] += dot(o_ref[0], dattn, TN)
    dout = dot(dattn, wo_ref[...], NT).astype(BF16)
    attention_backward(qkv_ref, sums_ref, prob_ref, dout, dqkv_ref, dsums_ref)


def back_kernel(dy_ref, u_ref, h_ref, o_ref, prob_ref, qkv_ref, sums_ref, gain_ref,
                wo_ref, wu_ref, wd_ref, dh_ref, dqkv_ref, dsums_ref, gd_out, gu_out, go_out,
                gg_ref, gd_ref, gu_ref, go_ref):
    step = pl.program_id(0)

    @pl.when(step == 0)
    def _():
        gd_ref[...] = jnp.zeros_like(gd_ref)
        gu_ref[...] = jnp.zeros_like(gu_ref)
        go_ref[...] = jnp.zeros_like(go_ref)
        gg_ref[...] = jnp.zeros_like(gg_ref)

    mlp_attention_backward(dy_ref[0].astype(F32), u_ref, h_ref, o_ref, prob_ref, qkv_ref, sums_ref,
                           gain_ref, wo_ref, wu_ref, wd_ref, dh_ref, dqkv_ref, dsums_ref, gd_ref,
                           gu_ref, go_ref, gg_ref)

    @pl.when(step == pl.num_programs(0) - 1)
    def _():
        gd_out[...] = gd_ref[...].astype(BF16)
        gu_out[...] = gu_ref[...].astype(BF16)
        go_out[...] = go_ref[...].astype(BF16)


def qkv_backward(x32, gain, near_ref, dsums_ref, dh, wq_ref, gq_ref, gg_ref):
    unit, rstd = normed(x32)
    n_one = (unit * gain).astype(BF16)
    dn_one = 0.0
    tokens = x32.shape[0]
    for part in range(3):
        cols = slice(part * D, (part + 1) * D)
        block = near_ref[0, :, cols]
        if part > 0:
            pieces = []
            for span in range(tokens // SPAN):
                share = dsums_ref[0, span : span + 1, (part - 1) * D : part * D].astype(F32) * (1.0 / SPAN)
                pieces.append(block[span * SPAN : (span + 1) * SPAN].astype(F32) + share)
            block = jnp.concatenate(pieces, 0).astype(BF16)
        gq_ref[:, cols] += dot(n_one, block, TN)
        dn_one = dn_one + dot(block, wq_ref[:, cols], NT)
    dnorm, grad_gain = norm_backward(dn_one, unit, rstd, gain)
    gg_ref[...] += grad_gain
    return dh + dnorm


def last_kernel(x_ref, gain_ref, near_ref, dsums_ref, dh_ref, wq_ref, dx_ref, gq_out, gg_ref, gq_ref):
    step = pl.program_id(0)

    @pl.when(step == 0)
    def _():
        gq_ref[...] = jnp.zeros_like(gq_ref)
        gg_ref[...] = jnp.zeros_like(gg_ref)

    dx_ref[0] = qkv_backward(x_ref[0].astype(F32), gain_ref[...], near_ref, dsums_ref, dh_ref[0], wq_ref,
                             gq_ref, gg_ref)

    @pl.when(step == pl.num_programs(0) - 1)
    def _():
        gq_out[...] = gq_ref[...].astype(BF16)


def per_seq(shape):
    rest = len(shape) - 1
    return pl.BlockSpec((1,) + tuple(shape[1:]), lambda b: (b,) + (0,) * rest)


def whole(shape):
    rank = len(shape)
    return pl.BlockSpec(tuple(shape), lambda b: (0,) * rank, pipeline_mode=pl.Buffered(1))


def sds(shape, dtype):
    return jax.ShapeDtypeStruct(tuple(shape), dtype)


def params():
    return pltpu.CompilerParams(dimension_semantics=("arbitrary",), vmem_limit_bytes=VMEM_LIMIT)


def call_first(x, gain, wq):
    batch, tokens, _ = x.shape
    spans = tokens // SPAN
    outs = (sds((batch, tokens, 3 * D), BF16), sds((batch, spans, 2 * D), BF16))
    return pl.pallas_call(
        first_kernel,
        grid=(batch,),
        in_specs=[per_seq(x.shape), whole(gain.shape), whole(wq.shape)],
        out_specs=[per_seq(o.shape) for o in outs],
        out_shape=outs,
        compiler_params=params(),
        name="first",
    )(x, gain, wq)


def call_layer(x, qkv, sums, bias, gain, wo, wu, wd, gain_next=None, wq=None):
    batch, tokens, _ = x.shape
    spans = tokens // SPAN
    last = wq is None
    keys = SPAN + sums.shape[1]
    outs = [
        sds((batch, spans, PAIRS, keys, 2 * SPAN), BF16),
        sds((batch, tokens, D), BF16),
        sds((batch, tokens, D), F32),
        sds((batch, tokens, wu.shape[1]), BF16),
        sds((batch, tokens, D), BF16 if last else F32),
    ]
    args = [x, qkv, sums, bias, gain, wo, wu, wd]
    if not last:
        outs += [sds((batch, tokens, 3 * D), BF16), sds((batch, spans, 2 * D), BF16)]
        args += [gain_next, wq]
    specs = [per_seq(a.shape) for a in args[:4]] + [whole(a.shape) for a in args[4:]]
    return pl.pallas_call(
        functools.partial(layer_kernel, last),
        grid=(batch,),
        in_specs=specs,
        out_specs=[per_seq(o.shape) for o in outs],
        out_shape=outs,
        compiler_params=params(),
        name="layer",
    )(*args)


def call_back(dy, u, h, o, prob, qkv, sums, gain, wo, wu, wd):
    batch, tokens, _ = dy.shape
    args = [dy, u, h, o, prob, qkv, sums, gain, wo, wu, wd]
    specs = [per_seq(a.shape) for a in args[:7]] + [whole(a.shape) for a in args[7:]]
    outs = [sds(h.shape, F32), sds(qkv.shape, BF16), sds(sums.shape, BF16),
            sds(wd.shape, BF16), sds(wu.shape, BF16), sds(wo.shape, BF16), sds((1, D), F32)]
    return pl.pallas_call(
        back_kernel,
        grid=(batch,),
        in_specs=specs,
        out_specs=[per_seq(o.shape) for o in outs[:3]] + [whole(o.shape) for o in outs[3:]],
        out_shape=outs,
        scratch_shapes=[pltpu.VMEM(wd.shape, F32), pltpu.VMEM(wu.shape, F32), pltpu.VMEM(wo.shape, F32)],
        compiler_params=params(),
        name="back",
    )(*args)


def call_last(x, gain, near, dsums, dh, wq):
    batch, tokens, _ = x.shape
    outs = [sds((batch, tokens, D), F32), sds(wq.shape, BF16), sds((1, D), F32)]
    return pl.pallas_call(
        last_kernel,
        grid=(batch,),
        in_specs=[per_seq(x.shape), whole(gain.shape), per_seq(near.shape), per_seq(dsums.shape),
                  per_seq(dh.shape), whole(wq.shape)],
        out_specs=[per_seq(outs[0].shape), whole(outs[1].shape), whole(outs[2].shape)],
        out_shape=outs,
        scratch_shapes=[pltpu.VMEM(wq.shape, F32)],
        compiler_params=params(),
        name="last",
    )(x, gain, near, dsums, dh, wq)


def mask_bias(segments, stretch):
    batch, length = segments.shape
    rank = lax.axis_index("seq")
    own = lax.dynamic_slice_in_dim(segments, rank * stretch, stretch, 1).reshape(batch, -1, SPAN)
    ends = segments.reshape(batch, -1, SPAN)[:, :, SPAN - 1]
    spans = own.shape[1]
    pos = jnp.arange(SPAN)
    near = (own[:, :, :, None] == own[:, :, None, :]) & (pos[:, None] <= pos[None, :])
    ids = rank * spans + jnp.arange(spans)
    before = jnp.arange(ends.shape[1])[None, :] < ids[:, None]
    far = (ends[:, None, :, None] == own[:, :, None, :]) & before[None, :, :, None]
    return jnp.where(jnp.concatenate([near, far], 2), 0.0, NEG).astype(F32)


def gather(shard):
    return lax.all_gather(shard, ("dp", "seq"), axis=0, tiled=True)


def scatter(grad):
    return lax.psum_scatter(grad, ("dp", "seq"), scatter_dimension=0, tiled=True)


def on_device(inputs, segments, w_qkv, w_out, w_up, w_down, gain_attn, gain_mlp, cotangent):
    layers = w_qkv.shape[0]
    stretch = inputs.shape[1]
    gains = lax.all_gather(
        jnp.concatenate([gain_attn, gain_mlp], 0), ("dp", "seq"), axis=1, tiled=True
    ).astype(F32)
    g_one = [gains[l : l + 1] for l in range(layers)]
    g_two = [gains[layers + l : layers + l + 1] for l in range(layers)]
    wq = [gather(w_qkv[l]) for l in range(layers)]
    wo = [gather(w_out[l]) for l in range(layers)]
    wu = [gather(w_up[l]) for l in range(layers)]
    wd = [gather(w_down[l]) for l in range(layers)]
    bias = mask_bias(segments, stretch)

    def spread(sums):
        return lax.all_gather(sums, "seq", axis=1, tiled=True)

    def collect(dsums):
        return lax.psum_scatter(dsums, "seq", scatter_dimension=1, tiled=True)

    x = inputs
    qkv, own = call_first(x, g_one[0], wq[0])
    kept = []
    for l in range(layers):
        sums = spread(own)
        if l + 1 < layers:
            prob, o, h, u, x_next, qkv_next, own = call_layer(
                x, qkv, sums, bias, g_two[l], wo[l], wu[l], wd[l], g_one[l + 1], wq[l + 1]
            )
        else:
            prob, o, h, u, x_next = call_layer(x, qkv, sums, bias, g_two[l], wo[l], wu[l], wd[l])
            qkv_next = None
        kept.append((x, qkv, sums, prob, o, h, u))
        x, qkv = x_next, qkv_next
    outputs = x
    dy = cotangent
    shares = [None] * layers
    for l in reversed(range(layers)):
        x, qkv, sums, prob, o, h, u = kept[l]
        dh, near, dsums, gd, gu, go, gg_two = call_back(
            dy, u, h, o, prob, qkv, sums, g_two[l], wo[l], wu[l], wd[l]
        )
        dy, gq, gg_one = call_last(x, g_one[l], near, collect(dsums), dh, wq[l])
        shares[l] = (scatter(gq), scatter(go), scatter(gu), scatter(gd), gg_one, gg_two)
    gain_grads = jnp.concatenate(
        [shares[l][4] for l in range(layers)] + [shares[l][5] for l in range(layers)], 0
    )
    gain_grads = lax.psum_scatter(gain_grads, ("dp", "seq"), scatter_dimension=1, tiled=True)
    stacked = [jnp.stack([shares[l][m] for l in range(layers)]).astype(F32) for m in range(4)]
    return (outputs, dy, *stacked, gain_grads[:layers], gain_grads[layers:])


def solution(mesh):
    weights = P(None, ("dp", "seq"), None)
    gains = P(None, ("dp", "seq"))
    rows = P("dp", "seq", None)
    return jax.shard_map(
        on_device,
        mesh=mesh,
        in_specs=(rows, P("dp", None), weights, weights, weights, weights, gains, gains, rows),
        out_specs=(rows, rows, weights, weights, weights, weights, gains, gains),
        check_vma=False,
    )
```

time: 1850 us -> 1780 us (0.962)
  waiting for transfers between devices: 912 us -> 1360 us
  matrix products: 311 us -> 0 us
  local copies, waits for them, and re-layouts: 272 us -> 19.9 us
  Pallas kernels: 0 us -> 234 us
  blocking collectives: 237 us -> 145 us
  other arithmetic: 86 us -> 9.17 us
    dot_general x96 -> x0, matrix products: 311 us -> none  [the longest x4 43.5 us: layer_backward(): jnp.einsum('sco,io->sci', ddown, wd, preferred_element_type=jnp.float32)]
    pallas_call x0 -> x7, Pallas kernels: none -> 234 us  [the longest x2 116 us: call_back(): pl.pallas_call(back_kernel, grid=(batch,), in_specs=specs, out_specs=[per...]
    reduce_scatter x8 -> x10, waiting for transfers between devices: 861 us -> 1080 us  [the longest x8 1010 us: scatter(): lax.psum_scatter(grad, ('dp', 'seq'), scatter_dimension=0, tiled=True)]
    reshape x57 -> x0, local copies, waits for them, and re-layouts: 173 us -> none  [the longest x8 34.9 us: attend_backward(): dkeys.reshape(batch, spans_own, SPAN, D)]
    all_gather x6, waiting for transfers between devices: 0.09 us -> 144 us  [gather(): return lax.all_gather(shard, ('dp', 'seq'), axis=0, tiled=True)]
    unnamed x18, waiting for transfers between devices: 50.6 us -> 137 us
    unnamed x2 -> x0, blocking collectives: 81.5 us -> none
    unnamed x540 -> x12, local copies, waits for them, and re-layouts: 38.7 us -> 3.01 us
  transfers between devices with their start and end apart: 16 -> 17, of which waited for: 8 -> 15; matrix products, arithmetic and copies ran while one was open for 22% -> 1% of each run, Pallas kernels for 0% -> 3%
where the time goes in v1:
time: 1780 us
  waiting for transfers between devices  1360 us (76%)
  Pallas kernels  234 us (13%)
  blocking collectives  145 us (8%)
  local copies, waits for them, and re-layouts  19.9 us (1%)
    reduce_scatter x8, waiting for transfers between devices, scatter(): lax.psum_scatter(grad, ('dp', 'seq'), scatter_dimension=0, tiled=True)  1010 us
    all_gather x6, waiting for transfers between devices, gather(): return lax.all_gather(shard, ('dp', 'seq'), axis=0, tiled=True)  144 us
    unnamed x18, waiting for transfers between devices  137 us
    pallas_call x2, Pallas kernels, call_back(): pl.pallas_call(back_kernel, grid=(batch,), in_specs=specs, out_specs=[per...  116 us
    all_gather x2, blocking collectives, gather(): return lax.all_gather(shard, ('dp', 'seq'), axis=0, tiled=True)  83.5 us
    pallas_call x2, Pallas kernels, call_layer(): pl.pallas_call(functools.partial(layer_kernel, last), grid=(batch,), in_s...  76.3 us
    reduce_scatter x2, waiting for transfers between devices, collect(): return lax.psum_scatter(dsums, 'seq', scatter_dimension=1, tiled=True)  66.2 us
    all_gather x1, blocking collectives, on_device(): lax.all_gather(jnp.concatenate([gain_attn, gain_mlp], 0), ('dp', 'seq'),...  43.3 us
  transfers between devices with their start and end apart: 17, of which 15 were waited for; matrix products, arithmetic and copies ran while one was open for 1% of the time, Pallas kernels for 3%

profile of v1, /device:TPU:0, one launch (start us, length us, event | category | flops | bytes accessed | tf_op | source)
XLA Modules:
  0.0 1779.4 jit_solution(13751645703108994192)
XLA Ops:
  7.2 1.5 fusion.2
  8.8 0.7 all-gather.22.cloned.1.call-update
  9.5 1.5 fusion.1
  11.1 1.5 fusion
  12.7 0.5 all-gather.24.cloned.1.call-update
  13.3 0.5 all-gather.26.cloned.1.call-update
  13.9 0.7 constant_dynamic-slice_fusion
  14.6 0.7 maximum_bitcast_fusion
  15.3 43.3 %all-gather.8 = bf16[32,16,4]{1,2,0:T(4,128)(2,1)S(1)} all-gather(bf16[1,16,4]{1,2,0:T(4,128)(2,1)S(1)} %maximum_bitcast_fusion), channel_id=1, replica_groups=mesh['dp'=4,'seq'=8] {'dp','seq'}, dimensions={0}, use_global_device_ids=true | all-gather | bytes 4224 | tf_op jit(solution)/shard_map/all_gather | solution.py:408
  58.9 0.9 copy.49
  60.3 0.3 compare_and_fusion
  60.6 1.2 add_select_fusion.refs_3_
  61.8 0.6 fusion.5
  62.4 40.8 %all-gather.5 = bf16[1,512,512]{2,1,0:T(8,128)(2,1)} all-gather(bf16[1,16,512]{2,1,0:T(8,128)(2,1)S(1)} %get-tuple-element.82), channel_id=7, replica_groups=mesh['dp'=4,'seq'=8] {'dp','seq'}, dimensions={1}, use_global_device_ids=true | all-gather | bytes 540672 | tf_op jit(solution)/shard_map/all_gather | solution.py:398
  103.2 42.7 %all-gather.1 = bf16[1,512,512]{2,1,0:T(8,128)(2,1)} all-gather(bf16[1,16,512]{2,1,0:T(8,128)(2,1)S(1)} %get-tuple-element.83), channel_id=3, replica_groups=mesh['dp'=4,'seq'=8] {'dp','seq'}, dimensions={1}, use_global_device_ids=true | all-gather | bytes 540672 | tf_op jit(solution)/shard_map/all_gather | solution.py:398
  145.9 9.9 first.1
  155.9 0.8 copy.33
  156.6 8.1 all_gather.35
  164.8 0.9 copy.34.refs_2_.sums_ref
  165.6 20.4 %all-gather.18.cloned.1.call-done = bf16[1,512,2048]{2,1,0:T(8,128)(2,1)} async-done(((bf16[1,16,2048]{2,1,0:T(8,128)(2,1)}), bf16[1,512,2048]{2,1,0:T(8,128)(2,1)}) %all-gather.18.cloned.1.call-update) | async-done | bytes 2097168 | tf_op jit(solution)/shard_map/all_gather | solution.py:398
  186.1 58.4 %all-gather.20.cloned.1.call-done = bf16[1,2048,512]{2,1,0:T(8,128)(2,1)} async-done(((bf16[1,64,512]{2,1,0:T(8,128)(2,1)}), bf16[1,2048,512]{2,1,0:T(8,128)(2,1)}) %all-gather.20.cloned.1.call-update) | async-done | bytes 2097168 | tf_op jit(solution)/shard_map/all_gather | solution.py:398
  244.4 41.0 %layer.2 = (bf16[8,2,4,144,256]{4,3,2,1,0:T(8,128)(2,1)}, bf16[8,256,512]{2,1,0:T(8,128)(2,1)}, f32[8,256,512]{2,1,0:T(8,128)}, bf16[8,256,2048]{2,1,0:T(8,128)(...) custom-call(bf16[8,256,512]{2,1,0:T(8,128)(2,1)} %x_ref.3, ...), custom_call_target="tpu_custom_call" | custom-call | tf_op jit(solution)/shard_map/layer/pallas_call | solution.py:338
  285.5 0.8 copy.35
  286.2 9.9 all_gather.40
  296.1 0.9 copy.36.refs_2_.sums_ref
  297.0 6.3 all-gather.24.cloned.1.call-done
  303.3 58.7 %all-gather.26.cloned.1.call-done = bf16[1,2048,512]{2,1,0:T(8,128)(2,1)} async-done(((bf16[1,64,512]{2,1,0:T(8,128)(2,1)}), bf16[1,2048,512]{2,1,0:T(8,128)(2,1)}) %all-gather.26.cloned.1.call-update) | async-done | bytes 2097168 | tf_op jit(solution)/shard_map/all_gather | solution.py:398
  362.0 35.3 %layer.3 = (bf16[8,2,4,144,256]{4,3,2,1,0:T(8,128)(2,1)}, bf16[8,256,512]{2,1,0:T(8,128)(2,1)}, f32[8,256,512]{2,1,0:T(8,128)}, bf16[8,256,2048]{2,1,0:T(8,128)(2,1)}, bf16[8,256,512]{2,1,0:T(8,128)(2,1)}) custom-call(f32[8,256,512]{2,1,0:T(8,128)} %get-tuple-element.44.refs_0_.x_ref, bf16[8,256,1536]{2,1,0:T(8,128)(2,1)} %get-tuple-element.45.refs_1_.qkv_ref, ...), custom_call_target="tpu_custom_call" | custom-call | tf_op jit(solution)/shard_map/layer/pallas_call | solution.py:338
  397.3 58.0 %back.2 = (f32[8,256,512]{2,1,0:T(8,128)}, bf16[8,256,1536]{2,1,0:T(8,128)(2,1)}, bf16[8,16,1024]{2,1,0:T(8,128)(2,1)}, bf16[2048,512]{1,0:T(8,128)(2,1)}, bf16[...) custom-call(bf16[8,256,512]{2,1,0:T(8,128)(2,1)} %dy_ref.1, ...), custom_call_target="tpu_custom_call" | custom-call | tf_op jit(solution)/shard_map/back/pallas_call | solution.py:355
  455.3 1.8 copy.38
  457.4 32.4 %reduce-scatter.14.cloned.1.call-done = bf16[8,2,1024]{2,0,1:T(8,128)(2,1)} async-done(((bf16[8,16,1024]{2,0,1:T(8,128)(2,1)}), bf16[8,2,1024]{2,0,1:T(8,128)(2,1)}) %reduce-scatter.14.cloned.1.call-update) | async-done | bytes 32784 | tf_op jit(solution)/shard_map/reduce_scatter | solution.py:423
  489.8 1.4 copy.39.dsums_ref
  491.2 15.9 last.2
  507.1 57.9 %back.3 = (f32[8,256,512]{2,1,0:T(8,128)}, bf16[8,256,1536]{2,1,0:T(8,128)(2,1)}, bf16[8,16,1024]{2,1,0:T(8,128)(2,1)}, bf16[2048,512]{1,0:T(8,128)(2,1)}, bf16[...) custom-call(f32[8,256,512]{2,1,0:T(8,128)} %get-tuple-element.55.dy_ref, ...), custom_call_target="tpu_custom_call" | custom-call | tf_op jit(solution)/shard_map/back/pallas_call | solution.py:355
  565.0 1.8 copy.41
  566.9 33.8 %reduce-scatter.16.cloned.1.call-done = bf16[8,2,1024]{2,0,1:T(8,128)(2,1)} async-done(((bf16[8,16,1024]{2,0,1:T(8,128)(2,1)}), bf16[8,2,1024]{2,0,1:T(8,128)(2,1)}) %reduce-scatter.16.cloned.1.call-update) | async-done | bytes 32784 | tf_op jit(solution)/shard_map/reduce_scatter | solution.py:423
  600.7 1.4 copy.42.dsums_ref
  602.1 15.6 last.3
  617.7 0.7 pad_maximum_fusion
  618.4 0.9 copy.43
  619.3 0.5 reduce-scatter.24.cloned.1.call-update
  619.9 0.7 reduce-scatter.22.cloned.1.call-update
  620.7 0.5 reduce-scatter.20.cloned.1.call-update
  621.2 0.7 reduce-scatter.18.cloned.1.call-update
  622.0 0.5 reduce-scatter.32.cloned.1.call-update
  622.6 0.5 reduce-scatter.30.cloned.1.call-update
  623.1 0.5 reduce-scatter.28.cloned.1.call-update
  623.7 0.5 reduce-scatter.26.cloned.1.call-update
  624.3 130.8 %reduce-scatter.34.cloned.1.call-done = f32[16,4]{1,0:T(8,128)} async-done(((f32[512,4]{1,0:T(8,128)}), f32[16,4]{1,0:T(8,128)}) %reduce-scatter.34.cloned.1.call-update) | async-done | bytes 272
  755.1 0.8 fusion.4
  755.9 0.6 copy.46
  756.5 0.6 copy.45
  757.2 131.6 %reduce-scatter.24.cloned.1.call-done = bf16[16,512]{1,0:T(8,128)(2,1)} async-done(((bf16[512,512]{1,0:T(8,128)(2,1)}), bf16[16,512]{1,0:T(8,128)(2,1)}) %reduce-scatter.24.cloned.1.call-update) | async-done | bytes 16400 | tf_op jit(solution)/shard_map/reduce_scatter | solution.py:402
  888.8 133.5 %reduce-scatter.22.cloned.1.call-done = bf16[16,512]{1,0:T(8,128)(2,1)} async-done(((bf16[512,512]{1,0:T(8,128)(2,1)}), bf16[16,512]{1,0:T(8,128)(2,1)}) %reduce-scatter.22.cloned.1.call-update) | async-done | bytes 16400 | tf_op jit(solution)/shard_map/reduce_scatter | solution.py:402
  1022.3 1.4 maximum_convert_fusion.3
  1023.7 97.6 %reduce-scatter.20.cloned.1.call-done = bf16[16,1536]{1,0:T(8,128)(2,1)} async-done(((bf16[512,1536]{1,0:T(8,128)(2,1)}), bf16[16,1536]{1,0:T(8,128)(2,1)}) %reduce-scatter.20.cloned.1.call-update) | async-done | bytes 49168 | tf_op jit(solution)/shard_map/reduce_scatter | solution.py:402
  1121.3 102.2 %reduce-scatter.18.cloned.1.call-done = bf16[16,1536]{1,0:T(8,128)(2,1)} async-done(((bf16[512,1536]{1,0:T(8,128)(2,1)}), bf16[16,1536]{1,0:T(8,128)(2,1)}) %reduce-scatter.18.cloned.1.call-update) | async-done | bytes 49168 | tf_op jit(solution)/shard_map/reduce_scatter | solution.py:402
  1223.5 1.5 maximum_convert_fusion.2
  1225.0 137.8 %reduce-scatter.32.cloned.1.call-done = bf16[64,512]{1,0:T(8,128)(2,1)} async-done(((bf16[2048,512]{1,0:T(8,128)(2,1)}), bf16[64,512]{1,0:T(8,128)(2,1)}) %reduce-scatter.32.cloned.1.call-update) | async-done | bytes 65552 | tf_op jit(solution)/shard_map/reduce_scatter | solution.py:402
  1362.8 136.1 %reduce-scatter.30.cloned.1.call-done = bf16[64,512]{1,0:T(8,128)(2,1)} async-done(((bf16[2048,512]{1,0:T(8,128)(2,1)}), bf16[64,512]{1,0:T(8,128)(2,1)}) %reduce-scatter.30.cloned.1.call-update) | async-done | bytes 65552 | tf_op jit(solution)/shard_map/reduce_scatter | solution.py:402
  1499.0 1.6 maximum_convert_fusion.1
  1500.6 134.6 %reduce-scatter.28.cloned.1.call-done = bf16[16,2048]{1,0:T(8,128)(2,1)} async-done(((bf16[512,2048]{1,0:T(8,128)(2,1)}), bf16[16,2048]{1,0:T(8,128)(2,1)}) %reduce-scatter.28.cloned.1.call-update) | async-done | bytes 65552 | tf_op jit(solution)/shard_map/reduce_scatter | solution.py:402
  1635.1 136.1 %reduce-scatter.26.cloned.1.call-done = bf16[16,2048]{1,0:T(8,128)(2,1)} async-done(((bf16[512,2048]{1,0:T(8,128)(2,1)}), bf16[16,2048]{1,0:T(8,128)(2,1)}) %reduce-scatter.26.cloned.1.call-update) | async-done | bytes 65552 | tf_op jit(solution)/shard_map/reduce_scatter | solution.py:402
  1771.3 1.6 maximum_convert_fusion
  (43 shorter events, 1.8 us)
Async XLA Ops:
  7.2 55.2 %copy-start = (bf16[2,16,512]{2,1,0:T(8,128)(2,1)S(1)}, bf16[2,16,512]{2,1,0:T(8,128)(2,1)}, u32[]{:S(2)}) copy-start(bf16[2,16,512]{2,1,0:T(8,128)(2,1)} %param.12) | copy-start | bytes 98308
  7.2 138.8 %all-gather.16.cloned.1.call-start = ((), (), s32[]{:S(2)}) async-start(), calls=%async_computation.21 | async-start | bytes 1622016 | tf_op jit(solution)/shard_map/all_gather | solution.py:398
  8.7 156.9 %all-gather.22.cloned.1.call-start = ((), (), s32[]{:S(2)}) async-start(), calls=%async_computation.24 | async-start | bytes 1622016 | tf_op jit(solution)/shard_map/all_gather | solution.py:398
  9.5 176.6 %all-gather.18.cloned.1.call-start = ((), (), s32[]{:S(2)}) async-start(), calls=%async_computation.22 | async-start | bytes 2162688 | tf_op jit(solution)/shard_map/all_gather | solution.py:398
  11.1 233.4 %all-gather.20.cloned.1.call-start = ((), (), s32[]{:S(2)}) async-start(), calls=%async_computation.23 | async-start | bytes 2162688 | tf_op jit(solution)/shard_map/all_gather | solution.py:398
  12.7 290.6 %all-gather.24.cloned.1.call-start = ((), (), s32[]{:S(2)}) async-start(), calls=%async_computation.25 | async-start | bytes 2162688 | tf_op jit(solution)/shard_map/all_gather | solution.py:398
  13.3 348.7 %all-gather.26.cloned.1.call-start = ((), (), s32[]{:S(2)}) async-start(), calls=%async_computation.26 | async-start | bytes 2162688 | tf_op jit(solution)/shard_map/all_gather | solution.py:398
  13.8 475.9 %reduce-scatter.14.cloned.1.call-start = ((), (), s32[]{:S(2)}) async-start(), calls=%async_computation.11 | async-start | bytes 294912 | tf_op jit(solution)/shard_map/reduce_scatter | solution.py:423
  457.1 143.5 %reduce-scatter.16.cloned.1.call-start = ((), (), s32[]{:S(2)}) async-start(), calls=%async_computation.12 | async-start | bytes 294912 | tf_op jit(solution)/shard_map/reduce_scatter | solution.py:423
  566.8 188.2 %reduce-scatter.34.cloned.1.call-start = ((), (), s32[]{:S(2)}) async-start(), calls=%async_computation.27 | async-start | bytes 270336
  602.1 15.6 copy-start.1
  602.1 15.6 copy-start.2
  602.1 15.6 copy-start.3
  619.3 269.5 %reduce-scatter.24.cloned.1.call-start = ((), (), s32[]{:S(2)}) async-start(), calls=%async_computation.16 | async-start | bytes 540672 | tf_op jit(solution)/shard_map/reduce_scatter | solution.py:402
  619.9 402.5 %reduce-scatter.22.cloned.1.call-start = ((), (), s32[]{:S(2)}) async-start(), calls=%async_computation.15 | async-start | bytes 540672 | tf_op jit(solution)/shard_map/reduce_scatter | solution.py:402
  620.6 500.7 %reduce-scatter.20.cloned.1.call-start = ((), (), s32[]{:S(2)}) async-start(), calls=%async_computation.14 | async-start | bytes 1622016 | tf_op jit(solution)/shard_map/reduce_scatter | solution.py:402
  621.2 602.3 %reduce-scatter.18.cloned.1.call-start = ((), (), s32[]{:S(2)}) async-start(), calls=%async_computation.13 | async-start | bytes 1622016 | tf_op jit(solution)/shard_map/reduce_scatter | solution.py:402
  621.9 740.9 %reduce-scatter.32.cloned.1.call-start = ((), (), s32[]{:S(2)}) async-start(), calls=%async_computation.20 | async-start | bytes 2162688 | tf_op jit(solution)/shard_map/reduce_scatter | solution.py:402
  622.5 876.5 %reduce-scatter.30.cloned.1.call-start = ((), (), s32[]{:S(2)}) async-start(), calls=%async_computation.19 | async-start | bytes 2162688 | tf_op jit(solution)/shard_map/reduce_scatter | solution.py:402
  623.1 1012.0 %reduce-scatter.28.cloned.1.call-start = ((), (), s32[]{:S(2)}) async-start(), calls=%async_computation.18 | async-start | bytes 2162688 | tf_op jit(solution)/shard_map/reduce_scatter | solution.py:402
  623.7 1147.6 %reduce-scatter.26.cloned.1.call-start = ((), (), s32[]{:S(2)}) async-start(), calls=%async_computation.17 | async-start | bytes 2162688 | tf_op jit(solution)/shard_map/reduce_scatter | solution.py:402
Sparse Core Ops, SparseCore 0:
  11.4 57.6 all-gather.15
  72.6 54.7 all-gather.21
  130.8 55.2 all-gather.17
  189.4 55.0 all-gather.19
  247.7 55.5 all-gather.23
  306.6 55.3 all-gather.25
  457.2 32.5 reduce-scatter.13
  567.0 33.6 reduce-scatter.15
  619.4 135.6 reduce-scatter.33
  757.1 131.6 reduce-scatter.23
  891.0 131.2 reduce-scatter.21
  1027.4 93.8 reduce-scatter.19
  1126.5 96.9 reduce-scatter.17
  1225.6 137.1 reduce-scatter.31
  1365.0 133.9 reduce-scatter.29
  1501.1 133.9 reduce-scatter.27
  1637.2 133.9 reduce-scatter.25

commit v2 on v1

--- a/solution.py
+++ b/solution.py
@@ -393,40 +393,350 @@
     far = (ends[:, None, :, None] == own[:, :, None, :]) & before[None, :, :, None]
     return jnp.where(jnp.concatenate([near, far], 2), 0.0, NEG).astype(F32)
 
-
-def gather(shard):
-    return lax.all_gather(shard, ("dp", "seq"), axis=0, tiled=True)
-
-
-def scatter(grad):
-    return lax.psum_scatter(grad, ("dp", "seq"), scatter_dimension=0, tiled=True)
+MESH = pl.DeviceIdType.MESH
+CORES = 2
+
+
+def place():
+    nz, nseq = lax.axis_size("dp"), lax.axis_size("seq")
+    z, s = lax.axis_index("dp"), lax.axis_index("seq")
+    return nz, nseq // CORES, z, s // CORES, lax.rem(s, CORES)
+
+
+def modulo(value, size):
+    return lax.rem(value + size, size)
+
+
+def peers_of():
+    nz, nchip, z, chip, core = place()
+    seq = chip * CORES + core
+    out = [(modulo(z + d, nz), seq) for d in range(1, nz)]
+    out += [(z, modulo(chip + d, nchip) * CORES + core) for d in range(1, nchip)]
+    out.append((z, chip * CORES + 1 - core))
+    return out
+
+
+def greet(peers):
+    barrier = pltpu.get_barrier_semaphore()
+    for peer in peers:
+        pl.semaphore_signal(barrier, inc=1, device_id=peer, device_id_type=MESH)
+    pl.semaphore_wait(barrier, len(peers))
+
+
+def remote(src, dst, send, recv, peer):
+    return pltpu.make_async_remote_copy(
+        src_ref=src, dst_ref=dst, send_sem=send, recv_sem=recv, device_id=peer, device_id_type=MESH
+    )
+
+
+class Gather:
+    def __init__(self, shards, fulls, sems):
+        self.shards, self.fulls = shards, fulls
+        self.own, self.zs, self.zr, self.ps, self.pr, self.cs, self.cr = sems
+        self.nz, self.nchip, self.z, self.chip, self.core = place()
+        self.seq = self.chip * CORES + self.core
+
+    @staticmethod
+    def scratch(count):
+        nz, nchip = lax.axis_size("dp"), lax.axis_size("seq") // CORES
+        dma = pltpu.SemaphoreType.DMA
+        return [dma((count,)), dma((count, nz - 1)), dma((count, nz - 1)), dma((count, nchip - 1)),
+                dma((count, nchip - 1)), dma((count, nchip)), dma((count, nchip))]
+
+    def local(self, t):
+        return pltpu.make_async_copy(self.shards[t], self.fulls[t].at[self.z, self.seq], self.own.at[t])
+
+    def line(self, t, d):
+        peer = (modulo(self.z + d, self.nz), self.seq)
+        return remote(self.shards[t], self.fulls[t].at[self.z, self.seq], self.zs.at[t, d - 1],
+                      self.zr.at[t, d - 1], peer)
+
+    def plane(self, t, d):
+        block = self.fulls[t].at[:, self.seq]
+        peer = (self.z, modulo(self.chip + d, self.nchip) * CORES + self.core)
+        return remote(block, block, self.ps.at[t, d - 1], self.pr.at[t, d - 1], peer)
+
+    def cross(self, t, d):
+        block = self.fulls[t].at[:, modulo(self.chip - d, self.nchip) * CORES + self.core]
+        peer = (self.z, self.chip * CORES + 1 - self.core)
+        return remote(block, block, self.cs.at[t, d], self.cr.at[t, d], peer)
+
+    def start(self, t):
+        self.local(t).start()
+        for d in range(1, self.nz):
+            self.line(t, d).start()
+
+    def spread(self, t):
+        self.local(t).wait()
+        for d in range(1, self.nz):
+            self.line(t, d).wait_recv()
+        for d in range(1, self.nchip):
+            self.plane(t, d).start()
+        self.cross(t, 0).start()
+
+    def share(self, t):
+        for d in range(1, self.nchip):
+            self.plane(t, d).wait_recv()
+            self.cross(t, d).start()
+
+    def finish(self, t):
+        for d in range(self.nchip):
+            self.cross(t, d).wait_recv()
+
+    def drain(self, t):
+        for d in range(1, self.nz):
+            self.line(t, d).wait_send()
+        for d in range(1, self.nchip):
+            self.plane(t, d).wait_send()
+        for d in range(self.nchip):
+            self.cross(t, d).wait_send()
+
+
+def gather_kernel(count, *refs):
+    work = Gather(refs[:count], refs[count : 2 * count], refs[2 * count :])
+    greet(peers_of())
+    for stage in (work.start, work.spread, work.share, work.finish, work.drain):
+        for t in range(count):
+            stage(t)
+
+
+def call_gather(shards, collective_id):
+    nz, nseq = lax.axis_size("dp"), lax.axis_size("seq")
+    count = len(shards)
+    outs = [sds((nz, nseq) + a.shape, a.dtype) for a in shards]
+    return pl.pallas_call(
+        functools.partial(gather_kernel, count),
+        in_specs=[pl.BlockSpec(memory_space=pltpu.VMEM)] * count,
+        out_specs=[pl.BlockSpec(memory_space=pl.ANY)] * count,
+        out_shape=outs,
+        scratch_shapes=Gather.scratch(count),
+        compiler_params=pltpu.CompilerParams(
+            collective_id=collective_id, has_side_effects=True, vmem_limit_bytes=VMEM_LIMIT
+        ),
+        name="gather",
+    )(*shards)
+
+
+class Reduce:
+    def __init__(self, parts, outs, bufs, sems):
+        self.parts, self.outs = parts, outs
+        count = len(parts)
+        self.mine, self.cross_in, self.plane_in, self.col, self.line_in = (
+            bufs[i * count : (i + 1) * count] for i in range(5)
+        )
+        self.own, self.cs, self.cr, self.ps, self.pr, self.zs, self.zr = sems
+        self.nz, self.nchip, self.z, self.chip, self.core = place()
+        self.seq = self.chip * CORES + self.core
+
+    @staticmethod
+    def scratch(parts):
+        nz, nchip = lax.axis_size("dp"), lax.axis_size("seq") // CORES
+        dma = pltpu.SemaphoreType.DMA
+        count = len(parts)
+        bufs = []
+        for lead in ((nchip, nz), (nchip, nz), (nchip - 1, nz), (nz,), (nz - 1,)):
+            bufs += [pltpu.VMEM(lead + a.shape[3:], a.dtype) for a in parts]
+        return bufs + [dma((count, nchip)), dma((count, nchip)), dma((count, nchip)), dma((count, nchip - 1)),
+                       dma((count, nchip - 1)), dma((count, nz - 1)), dma((count, nz - 1))]
+
+    def local(self, t, d):
+        chip = modulo(self.chip + d, self.nchip)
+        return pltpu.make_async_copy(self.parts[t].at[:, chip, self.core], self.mine[t].at[d], self.own.at[t, d])
+
+    def cross(self, t, d):
+        chip = modulo(self.chip + d, self.nchip)
+        peer = (self.z, self.chip * CORES + 1 - self.core)
+        return remote(self.parts[t].at[:, chip, 1 - self.core], self.cross_in[t].at[d], self.cs.at[t, d],
+                      self.cr.at[t, d], peer)
+
+    def plane(self, t, d):
+        peer = (self.z, modulo(self.chip + d, self.nchip) * CORES + self.core)
+        return remote(self.mine[t].at[d], self.plane_in[t].at[d - 1], self.ps.at[t, d - 1],
+                      self.pr.at[t, d - 1], peer)
+
+    def line(self, t, d):
+        z = modulo(self.z + d, self.nz)
+        return remote(self.col[t].at[z], self.line_in[t].at[d - 1], self.zs.at[t, d - 1],
+                      self.zr.at[t, d - 1], (z, self.seq))
+
+    def order(self):
+        return list(range(1, self.nchip)) + [0]
+
+    def start(self, t):
+        for d in self.order():
+            self.cross(t, d).start()
+            self.local(t, d).start()
+
+    def combine(self, t):
+        for d in self.order():
+            self.local(t, d).wait()
+            self.cross(t, d).wait_recv()
+
+            def add(i, carry):
+                total = self.mine[t][d, i].astype(F32) + self.cross_in[t][d, i].astype(F32)
+                self.mine[t][d, i] = total.astype(self.mine[t].dtype)
+                return carry
+
+            lax.fori_loop(0, self.nz, add, 0)
+            if d > 0:
+                self.plane(t, d).start()
+
+    def column(self, t):
+        for d in range(1, self.nchip):
+            self.plane(t, d).wait_recv()
+
+        def add(i, carry):
+            total = self.mine[t][0, i].astype(F32)
+            for d in range(self.nchip - 1):
+                total = total + self.plane_in[t][d, i].astype(F32)
+            self.col[t][i] = total.astype(self.col[t].dtype)
+            return carry
+
+        lax.fori_loop(0, self.nz, add, 0)
+        for d in range(1, self.nz):
+            self.line(t, d).start()
+
+    def finish(self, t):
+        total = self.col[t][self.z].astype(F32)
+        for d in range(1, self.nz):
+            self.line(t, d).wait_recv()
+        for d in range(self.nz - 1):
+            total = total + self.line_in[t][d].astype(F32)
+        self.outs[t][...] = total
+
+    def drain(self, t):
+        for d in self.order():
+            self.cross(t, d).wait_send()
+        for d in range(1, self.nchip):
+            self.plane(t, d).wait_send()
+        for d in range(1, self.nz):
+            self.line(t, d).wait_send()
+
+
+def reduce_kernel(count, *refs):
+    work = Reduce(refs[:count], refs[count : 2 * count], refs[2 * count : 7 * count], refs[7 * count :])
+    greet(peers_of())
+    for stage in (work.start, work.combine, work.column, work.finish, work.drain):
+        for t in range(count):
+            stage(t)
+
+
+def call_reduce(parts, collective_id):
+    nz, nseq = lax.axis_size("dp"), lax.axis_size("seq")
+    count = len(parts)
+    parts = [a.reshape((nz, nseq // CORES, CORES, a.shape[0] // (nz * nseq)) + a.shape[1:]) for a in parts]
+    outs = [sds(a.shape[3:], F32) for a in parts]
+    return pl.pallas_call(
+        functools.partial(reduce_kernel, count),
+        in_specs=[pl.BlockSpec(memory_space=pl.ANY)] * count,
+        out_specs=[pl.BlockSpec(memory_space=pltpu.VMEM)] * count,
+        out_shape=outs,
+        scratch_shapes=Reduce.scratch(parts),
+        compiler_params=pltpu.CompilerParams(
+            collective_id=collective_id, has_side_effects=True, vmem_limit_bytes=VMEM_LIMIT
+        ),
+        name="reduce",
+    )(*parts)
+
+
+def seq_peers():
+    nseq = lax.axis_size("seq")
+    z, s = lax.axis_index("dp"), lax.axis_index("seq")
+    return [(d, (z, modulo(s + d, nseq))) for d in range(1, nseq)]
+
+
+def spread_kernel(own_ref, all_ref, send, recv):
+    s = lax.axis_index("seq")
+    peers = seq_peers()
+    greet([peer for _, peer in peers])
+    copies = [remote(own_ref, all_ref.at[s], send.at[d - 1], recv.at[d - 1], peer) for d, peer in peers]
+    for copy in copies:
+        copy.start()
+    all_ref[s] = own_ref[...]
+    for copy in copies:
+        copy.wait()
+
+
+def call_spread(own, collective_id):
+    nseq = lax.axis_size("seq")
+    return pl.pallas_call(
+        spread_kernel,
+        in_specs=[pl.BlockSpec(memory_space=pltpu.VMEM)],
+        out_specs=pl.BlockSpec(memory_space=pltpu.VMEM),
+        out_shape=sds((nseq,) + own.shape, own.dtype),
+        scratch_shapes=[pltpu.SemaphoreType.DMA((nseq - 1,)),
+                        pltpu.SemaphoreType.DMA((nseq - 1,))],
+        compiler_params=pltpu.CompilerParams(
+            collective_id=collective_id, has_side_effects=True, vmem_limit_bytes=VMEM_LIMIT
+        ),
+        name="spread",
+    )(own)
+
+
+def collect_kernel(part_ref, out_ref, slots, send, recv):
+    s = lax.axis_index("seq")
+    nseq = lax.axis_size("seq")
+    peers = seq_peers()
+    greet([peer for _, peer in peers])
+    copies = [remote(part_ref.at[modulo(s + d, nseq)], slots.at[d - 1], send.at[d - 1], recv.at[d - 1], peer)
+              for d, peer in peers]
+    for copy in copies:
+        copy.start()
+    total = part_ref[s].astype(F32)
+    for d, _ in peers:
+        copies[d - 1].wait()
+    for d in range(nseq - 1):
+        total = total + slots[d].astype(F32)
+    out_ref[...] = total
+
+
+def call_collect(part, collective_id):
+    nseq = part.shape[0]
+    return pl.pallas_call(
+        collect_kernel,
+        in_specs=[pl.BlockSpec(memory_space=pltpu.VMEM)],
+        out_specs=pl.BlockSpec(memory_space=pltpu.VMEM),
+        out_shape=sds(part.shape[1:], F32),
+        scratch_shapes=[pltpu.VMEM((nseq - 1,) + part.shape[1:], part.dtype),
+                        pltpu.SemaphoreType.DMA((nseq - 1,)), pltpu.SemaphoreType.DMA((nseq - 1,))],
+        compiler_params=pltpu.CompilerParams(
+            collective_id=collective_id, has_side_effects=True, vmem_limit_bytes=VMEM_LIMIT
+        ),
+        name="collect",
+    )(part)
 
 
 def on_device(inputs, segments, w_qkv, w_out, w_up, w_down, gain_attn, gain_mlp, cotangent):
     layers = w_qkv.shape[0]
-    stretch = inputs.shape[1]
-    gains = lax.all_gather(
-        jnp.concatenate([gain_attn, gain_mlp], 0), ("dp", "seq"), axis=1, tiled=True
-    ).astype(F32)
+    batch, stretch, _ = inputs.shape
+    nz, nseq = lax.axis_size("dp"), lax.axis_size("seq")
+    spans = stretch // SPAN
+    slots = gain_attn.shape[1]
+    gain_shard = jnp.pad(
+        jnp.concatenate([gain_attn, gain_mlp], 0).astype(F32), ((0, 8 - 2 * layers), (0, 128 - slots))
+    )
+    shards = []
+    for l in range(layers):
+        shards += [w_qkv[l], w_out[l], w_up[l], w_down[l]]
+    fulls = call_gather(shards + [gain_shard], 0)
+    gains = fulls[-1][:, :, : 2 * layers, :slots].transpose(2, 0, 1, 3).reshape(2 * layers, D)
     g_one = [gains[l : l + 1] for l in range(layers)]
     g_two = [gains[layers + l : layers + l + 1] for l in range(layers)]
-    wq = [gather(w_qkv[l]) for l in range(layers)]
-    wo = [gather(w_out[l]) for l in range(layers)]
-    wu = [gather(w_up[l]) for l in range(layers)]
-    wd = [gather(w_down[l]) for l in range(layers)]
+    flat = [a.reshape((-1, a.shape[-1])) for a in fulls[:-1]]
+    wq, wo, wu, wd = (flat[m::4] for m in range(4))
     bias = mask_bias(segments, stretch)
 
-    def spread(sums):
-        return lax.all_gather(sums, "seq", axis=1, tiled=True)
-
-    def collect(dsums):
-        return lax.psum_scatter(dsums, "seq", scatter_dimension=1, tiled=True)
+    def spread(sums, index):
+        return call_spread(sums, index).transpose(1, 0, 2, 3).reshape(batch, nseq * spans, 2 * D)
+
+    def collect(dsums, index):
+        return call_collect(dsums.reshape(batch, nseq, spans, 2 * D).transpose(1, 0, 2, 3), index)
 
     x = inputs
     qkv, own = call_first(x, g_one[0], wq[0])
     kept = []
     for l in range(layers):
-        sums = spread(own)
+        sums = spread(own, 1)
         if l + 1 < layers:
             prob, o, h, u, x_next, qkv_next, own = call_layer(
                 x, qkv, sums, bias, g_two[l], wo[l], wu[l], wd[l], g_one[l + 1], wq[l + 1]
@@ -438,20 +748,26 @@
         x, qkv = x_next, qkv_next
     outputs = x
     dy = cotangent
-    shares = [None] * layers
+    grads = [None] * layers
     for l in reversed(range(layers)):
         x, qkv, sums, prob, o, h, u = kept[l]
         dh, near, dsums, gd, gu, go, gg_two = call_back(
             dy, u, h, o, prob, qkv, sums, g_two[l], wo[l], wu[l], wd[l]
         )
-        dy, gq, gg_one = call_last(x, g_one[l], near, collect(dsums), dh, wq[l])
-        shares[l] = (scatter(gq), scatter(go), scatter(gu), scatter(gd), gg_one, gg_two)
-    gain_grads = jnp.concatenate(
-        [shares[l][4] for l in range(layers)] + [shares[l][5] for l in range(layers)], 0
-    )
-    gain_grads = lax.psum_scatter(gain_grads, ("dp", "seq"), scatter_dimension=1, tiled=True)
-    stacked = [jnp.stack([shares[l][m] for l in range(layers)]).astype(F32) for m in range(4)]
-    return (outputs, dy, *stacked, gain_grads[:layers], gain_grads[layers:])
+        dy, gq, gg_one = call_last(x, g_one[l], near, collect(dsums, 2), dh, wq[l])
+        grads[l] = (gq, go, gu, gd, gg_one, gg_two)
+    gain_grads = jnp.concatenate([grads[l][4] for l in range(layers)] + [grads[l][5] for l in range(layers)], 0)
+    gain_grads = jnp.pad(
+        gain_grads.reshape(2 * layers, nz * nseq, slots).transpose(1, 0, 2),
+        ((0, 0), (0, 8 - 2 * layers), (0, 128 - slots)),
+    ).reshape(-1, 128)
+    parts = []
+    for l in range(layers):
+        parts += list(grads[l][:4])
+    shares = call_reduce(parts + [gain_grads], 3)
+    stacked = [jnp.stack(shares[m : 4 * layers : 4]) for m in range(4)]
+    gain_share = shares[-1][: 2 * layers, :slots]
+    return (outputs, dy, *stacked, gain_share[:layers], gain_share[layers:])
 
 
 def solution(mesh):

time: 1780 us -> 471 us (0.26)
  waiting for transfers between devices: 1360 us -> 0 us
  Pallas kernels: 234 us -> 437 us
  blocking collectives: 145 us -> 0 us
    reduce_scatter x10 -> x0, waiting for transfers between devices: 1080 us -> none  [the longest x8 1010 us: scatter(): lax.psum_scatter(grad, ('dp', 'seq'), scatter_dimension=0, tiled=True)]
    pallas_call x0 -> x6, Pallas kernels: none -> 202 us  [the longest x1 86.2 us: call_reduce(): pl.pallas_call(functools.partial(reduce_kernel, count), in_specs=[pl.Bloc...]
    all_gather x5 -> x0, blocking collectives: 145 us -> none  [the longest x2 83.5 us: gather(): return lax.all_gather(shard, ('dp', 'seq'), axis=0, tiled=True)]
    all_gather x6 -> x0, waiting for transfers between devices: 144 us -> none  [gather(): return lax.all_gather(shard, ('dp', 'seq'), axis=0, tiled=True)]
    unnamed x18 -> x0, waiting for transfers between devices: 137 us -> none
  transfers between devices with their start and end apart: 17 -> 0, of which waited for: 15 -> 0; matrix products, arithmetic and copies ran while one was open for 1% -> 0% of each run, Pallas kernels for 3% -> 0%
where the time goes in v2:
time: 471 us; the launch traced here: 469 us
  Pallas kernels  437 us (93%)
  local copies, waits for them, and re-layouts  21.5 us (5%)
  other arithmetic  10.1 us (2%)
    pallas_call x2, Pallas kernels, call_back(): pl.pallas_call(back_kernel, grid=(batch,), in_specs=specs, out_specs=[per...  116 us
    pallas_call x1, Pallas kernels, call_reduce(): pl.pallas_call(functools.partial(reduce_kernel, count), in_specs=[pl.Bloc...  86.2 us
    pallas_call x1, Pallas kernels, call_gather(): pl.pallas_call(functools.partial(gather_kernel, count), in_specs=[pl.Bloc...  84.7 us
    pallas_call x2, Pallas kernels, call_layer(): pl.pallas_call(functools.partial(layer_kernel, last), grid=(batch,), in_s...  76.3 us
    pallas_call x2, Pallas kernels, call_last(): pl.pallas_call(last_kernel, grid=(batch,), in_specs=[per_seq(x.shape), wh...  31.5 us
    pallas_call x2, Pallas kernels, call_collect(): pl.pallas_call(collect_kernel, in_specs=[pl.BlockSpec(memory_space=pltpu....  16.1 us
    pallas_call x2, Pallas kernels, call_spread(): pl.pallas_call(spread_kernel, in_specs=[pl.BlockSpec(memory_space=pltpu.V...  15.4 us
    pallas_call x1, Pallas kernels, call_first(): pl.pallas_call(first_kernel, grid=(batch,), in_specs=[per_seq(x.shape), w...  9.93 us

profile of v2, /device:TPU:0, one launch (start us, length us, event | category | flops | bytes accessed | tf_op | source)
XLA Modules:
  0.0 468.9 jit_solution(2404537212361728624)
XLA Ops:
  0.6 0.1 iota_compare_fusion.3
  0.7 1.3 fusion.6.refs_8_
  2.0 0.7 constant_dynamic-slice_fusion
  2.7 1.3 slice_bitcast_fusion.7
  4.1 0.9 copy.41
  4.9 0.3 slice_reduce_fusion
  5.2 0.1 compare_and_fusion.1
  5.3 1.5 slice_bitcast_fusion.5
  6.8 1.5 slice_bitcast_fusion.2
  8.3 1.5 slice_bitcast_fusion.1
  9.8 0.3 compare_and_fusion
  10.2 1.2 add_select_fusion.refs_3_
  11.4 84.7 %gather.1 = (bf16[4,8,16,1536]{3,2,1,0:T(8,128)(2,1)}, bf16[4,8,16,512]{3,2,1,0:T(8,128)(2,1)}, bf16[4,8,16,2048]{3,2,1,0:T(8,128)(2,1)}, bf16[4,8,64,512]{3,2,1...) custom-call(bf16[16,1536]{1,0:T(8,128)(2,1)} %get-tuple-element.121., ...), custom_call_target="tpu_custom_call" | custom-call | tf_op jit(solution)/shard_map/gather/pallas_call | solution.py:507
  96.0 0.9 slice_bitcast_fusion
  97.0 0.2 slice_reduce_fusion.1
  97.1 0.7 slice.80.refs_4_.gain_ref
  97.8 0.6 slice.78.refs_8_.gain_ref
  98.4 0.6 slice.76.refs_4_.gain_ref
  99.1 0.7 slice.73.gain_ref
  99.7 9.9 %first.1 = (bf16[8,256,1536]{2,1,0:T(8,128)(2,1)}, bf16[8,2,1024]{2,1,0:T(2,128)(2,1)}) custom-call(bf16[8,256,512]{2,1,0:T(8,128)(2,1)} %x_ref.3, f32[1,512]{1,0:T(1,128)} %slice.73.gain_ref, bf16[512,1536]{1,0:T(8,128)(2,1)} %bitcast.68), custom_call_target="tpu_custom_call" | custom-call | tf_op jit(solution)/shard_map/first/pallas_call | solution.py:310
  109.6 7.7 %spread.2 = bf16[8,8,2,1024]{3,2,1,0:T(2,128)(2,1)} custom-call(bf16[8,2,1024]{2,1,0:T(2,128)(2,1)} %get-tuple-element.63.own_ref), custom_call_target="tpu_custom_call" | custom-call | tf_op jit(solution)/shard_map/spread/pallas_call | solution.py:662
  117.4 1.1 copy.27
  118.5 0.8 reshape.129.refs_2_.sums_ref
  119.3 41.0 %layer.2 = (bf16[8,2,4,144,256]{4,3,2,1,0:T(8,128)(2,1)}, bf16[8,256,512]{2,1,0:T(8,128)(2,1)}, f32[8,256,512]{2,1,0:T(8,128)}, bf16[8,256,2048]{2,1,0:T(8,128)(...) custom-call(bf16[8,256,512]{2,1,0:T(8,128)(2,1)} %x_ref.3, ...), custom_call_target="tpu_custom_call" | custom-call | tf_op jit(solution)/shard_map/layer/pallas_call | solution.py:338
  160.3 7.7 %spread.3 = bf16[8,8,2,1024]{3,2,1,0:T(2,128)(2,1)} custom-call(bf16[8,2,1024]{2,1,0:T(2,128)(2,1)} %get-tuple-element.70.own_ref), custom_call_target="tpu_custom_call" | custom-call | tf_op jit(solution)/shard_map/spread/pallas_call | solution.py:662
  168.0 1.1 copy.28
  169.1 0.8 reshape.135.refs_2_.sums_ref
  169.9 35.3 %layer.3 = (bf16[8,2,4,144,256]{4,3,2,1,0:T(8,128)(2,1)}, bf16[8,256,512]{2,1,0:T(8,128)(2,1)}, f32[8,256,512]{2,1,0:T(8,128)}, bf16[8,256,2048]{2,1,0:T(8,128)(2,1)}, bf16[8,256,512]{2,1,0:T(8,128)(2,1)}) custom-call(f32[8,256,512]{2,1,0:T(8,128)} %get-tuple-element.68.refs_0_.x_ref, bf16[8,256,1536]{2,1,0:T(8,128)(2,1)} %get-tuple-element.69.refs_1_.qkv_ref, ...), custom_call_target="tpu_custom_call" | custom-call | tf_op jit(solution)/shard_map/layer/pallas_call | solution.py:338
  205.3 58.2 %back.2 = (f32[8,256,512]{2,1,0:T(8,128)}, bf16[8,256,1536]{2,1,0:T(8,128)(2,1)}, bf16[8,16,1024]{2,1,0:T(8,128)(2,1)}, bf16[2048,512]{1,0:T(8,128)(2,1)}, bf16[...) custom-call(bf16[8,256,512]{2,1,0:T(8,128)(2,1)} %dy_ref.1, ...), custom_call_target="tpu_custom_call" | custom-call | tf_op jit(solution)/shard_map/back/pallas_call | solution.py:355
  263.5 1.1 copy.29
  264.6 1.0 copy.40
  265.5 8.0 %collect.2.dsums_ref = f32[8,2,1024]{2,1,0:T(2,128)} custom-call(bf16[8,8,2,1024]{3,2,1,0:T(2,128)(2,1)} %bitcast.80), custom_call_target="tpu_custom_call" | custom-call | tf_op jit(solution)/shard_map/collect/pallas_call | solution.py:695
  273.6 15.9 %last.2 = (f32[8,256,512]{2,1,0:T(8,128)}, bf16[512,1536]{1,0:T(8,128)(2,1)}, f32[1,512]{1,0:T(1,128)}) custom-call(f32[8,256,512]{2,1,0:T(8,128)} %get-tuple-element.68.refs_0_.x_ref, f32[1,512]{1,0:T(1,128)} %slice.78.refs_8_.gain_ref, bf16[8,256,1536]{2,1,0:T(8,128)(2,1)} %get-tuple-element.79.near_ref, f32[8,2,1024]{2,1,0:T(2,128)} %collect.2.dsums_ref, ...), custom_call_target="tpu_custom_call" | custom-call | tf_op jit(solution)/shard_map/last/pallas_call | solution.py:370
  289.5 58.1 %back.3 = (f32[8,256,512]{2,1,0:T(8,128)}, bf16[8,256,1536]{2,1,0:T(8,128)(2,1)}, bf16[8,16,1024]{2,1,0:T(8,128)(2,1)}, bf16[2048,512]{1,0:T(8,128)(2,1)}, bf16[...) custom-call(f32[8,256,512]{2,1,0:T(8,128)} %get-tuple-element.82.dy_ref, ...), custom_call_target="tpu_custom_call" | custom-call | tf_op jit(solution)/shard_map/back/pallas_call | solution.py:355
  347.6 1.1 copy.31
  348.7 1.0 copy.39
  349.7 8.1 %collect.3.dsums_ref = f32[8,2,1024]{2,1,0:T(2,128)} custom-call(bf16[8,8,2,1024]{3,2,1,0:T(2,128)(2,1)} %bitcast.81), custom_call_target="tpu_custom_call" | custom-call | tf_op jit(solution)/shard_map/collect/pallas_call | solution.py:695
  357.8 0.0 copy-start
  357.8 0.0 copy-start.1
  357.8 0.0 copy-start.2
  357.8 15.6 %last.3 = (f32[8,256,512]{2,1,0:T(8,128)}, bf16[512,1536]{1,0:T(8,128)(2,1)}, f32[1,512]{1,0:T(1,128)}) custom-call(bf16[8,256,512]{2,1,0:T(8,128)(2,1)} %x_ref.3, f32[1,512]{1,0:T(1,128)} %slice.73.gain_ref, bf16[8,256,1536]{2,1,0:T(8,128)(2,1)} %get-tuple-element.87.near_ref, f32[8,2,1024]{2,1,0:T(2,128)} %collect.3.dsums_ref, ...), custom_call_target="tpu_custom_call" | custom-call | tf_op jit(solution)/shard_map/last/pallas_call | solution.py:370
  373.5 0.0 copy-done
  373.5 0.0 copy-done.1
  373.5 0.0 copy-done.2
  373.5 0.7 pad_maximum_fusion.4
  374.2 0.1 reshape.149
  374.3 0.7 pad.12.clone
  375.0 86.2 %reduce.19 = (f32[16,1536]{1,0:T(8,128)}, f32[16,512]{1,0:T(8,128)}, f32[16,2048]{1,0:T(8,128)}, f32[64,512]{1,0:T(8,128)}, f32[16,1536]{1,0:T(8,128)}, /*index=...) custom-call(bf16[4,4,2,16,1536]{4,3,2,1,0:T(8,128)(2,1)} %bitcast.79, ...), custom_call_target="tpu_custom_call" | custom-call | tf_op jit(solution)/shard_map/reduce/pallas_call | solution.py:629
  461.2 1.6 pad_maximum_fusion.2
  462.9 1.3 fusion.7
  464.2 1.4 pad_maximum_fusion.3
  465.6 1.7 pad_maximum_fusion
  467.3 1.7 pad_maximum_fusion.1
  (4 shorter events, 0.1 us)
Async XLA Ops:
  357.8 15.7 %copy-start = (f32[1,512]{1,0:T(1,128)S(1)}, f32[1,512]{1,0:T(1,128)}, u32[]{:S(2)}) copy-start(f32[1,512]{1,0:T(1,128)} %get-tuple-element.102) | copy-start | bytes 6148
  357.8 15.7 %copy-start.1 = (f32[1,512]{1,0:T(1,128)S(1)}, f32[1,512]{1,0:T(1,128)}, u32[]{:S(2)}) copy-start(f32[1,512]{1,0:T(1,128)} %get-tuple-element.100) | copy-start | bytes 6148
  357.8 15.7 %copy-start.2 = (f32[1,512]{1,0:T(1,128)S(1)}, f32[1,512]{1,0:T(1,128)}, u32[]{:S(2)}) copy-start(f32[1,512]{1,0:T(1,128)} %get-tuple-element.101) | copy-start | bytes 6148

commit v3 on v2

--- a/solution.py
+++ b/solution.py
@@ -770,12 +770,963 @@
     return (outputs, dy, *stacked, gain_share[:layers], gain_share[layers:])
 
 
+class Spot:
+    def __init__(self):
+        self.nz, self.nseq = lax.axis_size("dp"), lax.axis_size("seq")
+        self.z, self.seq = lax.axis_index("dp"), lax.axis_index("seq")
+        self.chip, self.core = lax.div(self.seq, CORES), lax.rem(self.seq, CORES)
+        row, col = lax.div(self.chip, 2), lax.rem(self.chip, 2)
+        across, along = row * 2 + 1 - col, (1 - row) * 2 + col
+        self.first = (1 - self.core) * across + self.core * along
+        self.second = (1 - self.core) * along + self.core * across
+        self.diagonal = (1 - row) * 2 + 1 - col
+
+    def at_chip(self, chip):
+        return (self.z, chip * CORES + self.core)
+
+    def twin(self):
+        return (self.z, self.chip * CORES + 1 - self.core)
+
+    def on_line(self, d):
+        return (modulo(self.z + d, self.nz), self.seq)
+
+    def signal(self):
+        barrier = pltpu.get_barrier_semaphore()
+        for peer in self.peers():
+            pl.semaphore_signal(barrier, inc=1, device_id=peer, device_id_type=MESH)
+
+    def meet(self):
+        pl.semaphore_wait(pltpu.get_barrier_semaphore(), len(self.peers()))
+
+    def peers(self):
+        out = [self.on_line(d) for d in range(1, self.nz)]
+        return out + [(self.z, modulo(self.seq + d, self.nseq)) for d in range(1, self.nseq)]
+
+
+def dma(*shape):
+    return pltpu.SemaphoreType.DMA(shape)
+
+
+class Fetch:
+    def __init__(self, spot, shards, fulls, sems):
+        self.spot, self.shards, self.fulls = spot, shards, fulls
+        self.own, self.zs, self.zr, self.hs, self.hr, self.cs, self.cr = sems
+
+    @staticmethod
+    def scratch(count, nz):
+        return [dma(count), dma(count, nz - 1), dma(count, nz - 1), dma(count, 3), dma(count, 3),
+                dma(count, 4), dma(count, 4)]
+
+    def local(self, t):
+        return pltpu.make_async_copy(
+            self.shards[t], self.fulls[t].at[self.spot.z, self.spot.seq], self.own.at[t])
+
+    def line(self, t, d):
+        return remote(self.shards[t], self.fulls[t].at[self.spot.z, self.spot.seq], self.zs.at[t, d - 1],
+                      self.zr.at[t, d - 1], self.spot.on_line(d))
+
+    def hop(self, t, k):
+        spot = self.spot
+        chip = (spot.chip, spot.chip, spot.first)[k]
+        target = (spot.first, spot.second, spot.second)[k]
+        block = self.fulls[t].at[:, chip * CORES + spot.core]
+        return remote(block, block, self.hs.at[t, k], self.hr.at[t, k], spot.at_chip(target))
+
+    def cross(self, t, k):
+        spot = self.spot
+        chip = (spot.chip, spot.first, spot.second, spot.diagonal)[k]
+        block = self.fulls[t].at[:, chip * CORES + spot.core]
+        return remote(block, block, self.cs.at[t, k], self.cr.at[t, k], spot.twin())
+
+    def start(self, t):
+        self.local(t).start()
+        for d in range(1, self.spot.nz):
+            self.line(t, d).start()
+
+    def spread(self, t):
+        self.local(t).wait()
+        for d in range(1, self.spot.nz):
+            self.line(t, d).wait_recv()
+        self.hop(t, 0).start()
+        self.hop(t, 1).start()
+        self.cross(t, 0).start()
+
+    def relay(self, t):
+        self.hop(t, 0).wait_recv()
+        self.hop(t, 2).start()
+        self.cross(t, 1).start()
+
+    def share(self, t):
+        self.hop(t, 1).wait_recv()
+        self.cross(t, 2).start()
+
+    def close(self, t):
+        self.hop(t, 2).wait_recv()
+        self.cross(t, 3).start()
+
+    def finish(self, t):
+        for k in range(4):
+            self.cross(t, k).wait_recv()
+
+    def drain(self, t):
+        for d in range(1, self.spot.nz):
+            self.line(t, d).wait_send()
+        for k in range(3):
+            self.hop(t, k).wait_send()
+        for k in range(4):
+            self.cross(t, k).wait_send()
+
+
+class Fold:
+    def __init__(self, spot, parts, outs, bufs, sems):
+        self.spot, self.parts, self.outs = spot, parts, outs
+        count = len(parts)
+        self.mine, self.twin_in, self.first_in, self.second_in, self.col, self.line_in = (
+            bufs[i * count : (i + 1) * count] for i in range(6)
+        )
+        self.own, self.cs, self.cr, self.hs, self.hr, self.zs, self.zr = sems
+
+    @staticmethod
+    def buffers(shapes, nz):
+        out = []
+        for lead in ((4, nz), (4, nz), (2, nz), (nz,), (nz,), (nz - 1,)):
+            out += [pltpu.VMEM(lead + tuple(shape), BF16) for shape in shapes]
+        return out
+
+    @staticmethod
+    def sems(count, nz):
+        return [dma(count, 4), dma(count, 4), dma(count, 4), dma(count, 3), dma(count, 3),
+                dma(count, nz - 1), dma(count, nz - 1)]
+
+    def local(self, t, k):
+        spot = self.spot
+        chip = (spot.chip, spot.first, spot.second, spot.diagonal)[k]
+        return pltpu.make_async_copy(self.parts[t].at[:, chip, spot.core], self.mine[t].at[k], self.own.at[t, k])
+
+    def cross(self, t, k):
+        spot = self.spot
+        chip = (spot.chip, spot.second, spot.first, spot.diagonal)[k]
+        return remote(self.parts[t].at[:, chip, 1 - spot.core], self.twin_in[t].at[k], self.cs.at[t, k],
+                      self.cr.at[t, k], spot.twin())
+
+    def hop(self, t, k):
+        spot = self.spot
+        source = self.mine[t].at[(1, 3, 2)[k]]
+        target = (self.first_in[t].at[0], self.first_in[t].at[1], self.second_in[t])[k]
+        chip = (spot.first, spot.first, spot.second)[k]
+        return remote(source, target, self.hs.at[t, k], self.hr.at[t, k], spot.at_chip(chip))
+
+    def line(self, t, d):
+        z = modulo(self.spot.z + d, self.spot.nz)
+        return remote(self.col[t].at[z], self.line_in[t].at[d - 1], self.zs.at[t, d - 1], self.zr.at[t, d - 1],
+                      self.spot.on_line(d))
+
+    def start(self, t):
+        for k in (3, 1, 2, 0):
+            self.cross(t, k).start()
+            self.local(t, k).start()
+
+    def combine(self, t):
+        mine, twin_in = self.mine[t], self.twin_in[t]
+        for k in (3, 1, 2, 0):
+            self.local(t, k).wait()
+            self.cross(t, k).wait_recv()
+
+            def add(i, carry):
+                mine[k, i] = (mine[k, i].astype(F32) + twin_in[k, i].astype(F32)).astype(BF16)
+                return carry
+
+            lax.fori_loop(0, self.spot.nz, add, 0)
+            if k == 3:
+                self.hop(t, 1).start()
+            elif k == 1:
+                self.hop(t, 0).start()
+
+    def middle(self, t):
+        mine, first_in = self.mine[t], self.first_in[t]
+        self.hop(t, 1).wait_recv()
+
+        def add(i, carry):
+            mine[2, i] = (mine[2, i].astype(F32) + first_in[1, i].astype(F32)).astype(BF16)
+            return carry
+
+        lax.fori_loop(0, self.spot.nz, add, 0)
+        self.hop(t, 2).start()
+
+    def column(self, t):
+        mine, first_in, second_in, col = self.mine[t], self.first_in[t], self.second_in[t], self.col[t]
+        self.hop(t, 0).wait_recv()
+        self.hop(t, 2).wait_recv()
+
+        def add(i, carry):
+            total = mine[0, i].astype(F32) + first_in[0, i].astype(F32) + second_in[i].astype(F32)
+            col[i] = total.astype(BF16)
+            return carry
+
+        lax.fori_loop(0, self.spot.nz, add, 0)
+        for d in range(1, self.spot.nz):
+            self.line(t, d).start()
+
+    def finish(self, t):
+        total = self.col[t][self.spot.z].astype(F32)
+        for d in range(1, self.spot.nz):
+            self.line(t, d).wait_recv()
+        for d in range(self.spot.nz - 1):
+            total = total + self.line_in[t][d].astype(F32)
+        self.outs[t][...] = total
+
+    def drain(self, t):
+        for k in range(4):
+            self.cross(t, k).wait_send()
+        for k in range(3):
+            self.hop(t, k).wait_send()
+        for d in range(1, self.spot.nz):
+            self.line(t, d).wait_send()
+
+
+class AllSum:
+    def __init__(self, spot, source, bufs):
+        self.spot, self.source = spot, source
+        self.twin_in, self.pair, self.plane_in, self.col, self.line_in, self.ss, self.rs = bufs
+
+    @staticmethod
+    def scratch(shape, nz):
+        return [pltpu.VMEM(shape, F32), pltpu.VMEM(shape, F32), pltpu.VMEM((3,) + shape, F32),
+                pltpu.VMEM(shape, F32), pltpu.VMEM((nz - 1,) + shape, F32), dma(3 + nz), dma(3 + nz)]
+
+    def cross(self):
+        return remote(self.source, self.twin_in, self.ss.at[0], self.rs.at[0], self.spot.twin())
+
+    def hop(self, k):
+        chip = (self.spot.first, self.spot.second, self.spot.diagonal)[k]
+        return remote(self.pair, self.plane_in.at[k], self.ss.at[1 + k], self.rs.at[1 + k],
+                      self.spot.at_chip(chip))
+
+    def line(self, d):
+        return remote(self.col, self.line_in.at[d - 1], self.ss.at[3 + d], self.rs.at[3 + d],
+                      self.spot.on_line(d))
+
+    def start(self):
+        self.cross().start()
+
+    def plane(self):
+        self.cross().wait_recv()
+        self.pair[...] = self.source[...] + self.twin_in[...]
+        for k in range(3):
+            self.hop(k).start()
+
+    def column(self):
+        for k in range(3):
+            self.hop(k).wait_recv()
+        self.col[...] = self.pair[...] + self.plane_in[0] + self.plane_in[1] + self.plane_in[2]
+        for d in range(1, self.spot.nz):
+            self.line(d).start()
+
+    def total(self):
+        out = self.col[...]
+        for d in range(1, self.spot.nz):
+            self.line(d).wait_recv()
+        for d in range(self.spot.nz - 1):
+            out = out + self.line_in[d]
+        return out
+
+    def drain(self):
+        self.cross().wait_send()
+        for k in range(3):
+            self.hop(k).wait_send()
+        for d in range(1, self.spot.nz):
+            self.line(d).wait_send()
+
+
+class Exchange:
+    def __init__(self, spot, ss, rs):
+        self.spot, self.ss, self.rs = spot, ss, rs
+
+    def copies(self, source, target):
+        spot = self.spot
+        out = []
+        for d in range(1, spot.nseq):
+            s = modulo(spot.seq + d, spot.nseq)
+            out.append(remote(source(s), target(d), self.ss.at[d - 1], self.rs.at[d - 1], (spot.z, s)))
+        return out
+
+    def spread(self, own, land):
+        return self.copies(lambda s: own, lambda d: land.at[self.spot.seq])
+
+    def collect(self, parts, land):
+        return self.copies(lambda s: parts.at[s], lambda d: land.at[d - 1])
+
+
+def begin(copies):
+    for copy in copies:
+        copy.start()
+
+
+def complete(copies):
+    for copy in copies:
+        copy.wait()
+
+
+def when(condition, *actions):
+    @pl.when(condition)
+    def _():
+        for action in actions:
+            action()
+
+
+def does(method, *args):
+    return lambda: method(*args)
+
+
+def log2(value):
+    assert value & (value - 1) == 0
+    return value.bit_length() - 1
+
+
+def row_picker(b, batch, spans, nseq):
+    shape = (nseq * spans, nseq * batch * spans)
+    r = lax.broadcasted_iota(jnp.int32, shape, 0)
+    c = lax.broadcasted_iota(jnp.int32, shape, 1)
+    shift = log2(spans)
+    place_of = (r >> shift) * (batch * spans) + b * spans + (r & (spans - 1))
+    return jnp.where(c == place_of, 1.0, 0.0).astype(BF16)
+
+
+def span_adder(b, batch, spans, tokens):
+    shape = (batch * spans, tokens)
+    r = lax.broadcasted_iota(jnp.int32, shape, 0)
+    t = lax.broadcasted_iota(jnp.int32, shape, 1)
+    return jnp.where(r == b * spans + (t >> log2(SPAN)), 1.0, 0.0).astype(BF16)
+
+
+def whole_weight(ref, cols):
+    block = ref[:, :, :, cols]
+    return block.reshape((-1, block.shape[-1]))
+
+
+def enter_kernel(counts, *refs):
+    batch, spans = counts
+    (x_ref, bias_ref, gain_own, wq_sh, wo_sh, wu_sh, wd_sh,
+     qkv_ref, sums_ref, prob_ref, o_ref, gains_ref, fq, fo, fu, fd, fq_next,
+     qkv_all, own_acc, own_low, land, wq_in, wq_sem, ex_s, ex_r) = refs[:25]
+    rest = refs[25:]
+    spot = Spot()
+    fetch = Fetch(spot, [wq_sh.at[0], wo_sh.at[0], wu_sh.at[0], wd_sh.at[0], wq_sh.at[1]],
+                  [fq, fo, fu, fd, fq_next], rest[:7])
+    adder = AllSum(spot, gain_own, rest[7:])
+    exchange = Exchange(spot, ex_s, ex_r).spread(own_low, land)
+    q0, o0, u0, d0, q1 = range(5)
+    step = pl.program_id(0)
+    tokens = x_ref.shape[1]
+
+    @pl.when(step == 0)
+    def _():
+        spot.signal()
+        own_acc[...] = jnp.zeros_like(own_acc)
+        spot.meet()
+        adder.start()
+        for t in range(5):
+            fetch.start(t)
+        fetch.spread(q0)
+        adder.plane()
+        fetch.spread(o0)
+        adder.column()
+        fetch.relay(q0)
+        gains_ref[...] = adder.total()
+        fetch.share(q0)
+        fetch.spread(u0)
+        fetch.close(q0)
+        fetch.relay(o0)
+        fetch.finish(q0)
+        copy = pltpu.make_async_copy(fq, wq_in, wq_sem)
+        copy.start()
+        copy.wait()
+
+    when(step == 1, does(fetch.share, o0), does(fetch.spread, d0))
+    when(step == 3, does(fetch.close, o0))
+    when(step == 4, does(fetch.relay, u0), does(fetch.finish, o0))
+    when(step == 5, does(fetch.share, u0))
+    when(step == 6, does(fetch.spread, q1))
+
+    @pl.when(step < batch)
+    def _():
+        unit, _ = normed(x_ref[0].astype(F32))
+        n_one = (unit * gains_ref[0:1]).astype(BF16)
+        pick = span_adder(step, batch, spans, tokens)
+        for part in range(3):
+            cols = slice(part * D, (part + 1) * D)
+            block = dot(n_one, whole_weight(wq_in, cols)).astype(BF16)
+            qkv_ref[0, :, cols] = block
+            qkv_all[step, :, cols] = block
+            if part > 0:
+                own_acc[:, (part - 1) * D : part * D] += dot(pick, block)
+
+    @pl.when(step == batch - 1)
+    def _():
+        own_low[...] = (own_acc[...] * (1.0 / SPAN)).astype(BF16)
+        begin(exchange)
+        land[spot.seq] = own_low[...]
+
+    when(step == batch, does(complete, exchange))
+    when(step == batch + 1, does(fetch.close, u0), does(fetch.relay, d0))
+    when(step == batch + 2, does(fetch.share, d0))
+    when(step == batch + 3, does(fetch.finish, u0))
+    when(step == batch + 4, does(fetch.relay, q1))
+    when(step == batch + 5, does(fetch.close, d0), does(fetch.share, q1))
+    when(step == batch + 6, does(fetch.finish, d0))
+    when(step == batch + 7, does(fetch.close, q1))
+
+    @pl.when(step >= batch)
+    def _():
+        b = step - batch
+        every = land[...].reshape((-1, land.shape[-1]))
+        sums_ref[0] = dot(row_picker(b, batch, spans, spot.nseq), every).astype(BF16)
+        attention_forward(qkv_all.at[pl.ds(b, 1)], sums_ref, bias_ref, prob_ref, o_ref)
+
+    @pl.when(step == 2 * batch - 1)
+    def _():
+        fetch.finish(q1)
+        for t in range(5):
+            fetch.drain(t)
+        adder.drain()
+
+
+def phased(shape, start, count):
+    rest = len(shape) - 1
+    return pl.BlockSpec((1,) + tuple(shape[1:]),
+                        lambda i: (jnp.clip(i - start, 0, count - 1),) + (0,) * rest)
+
+
+def anywhere():
+    return pl.BlockSpec(memory_space=pl.ANY)
+
+
+def fused_params(collective_id):
+    return pltpu.CompilerParams(dimension_semantics=("arbitrary",), vmem_limit_bytes=VMEM_LIMIT,
+                                collective_id=collective_id, has_side_effects=True)
+
+
+def full_shape(weights):
+    return sds((lax.axis_size("dp"), lax.axis_size("seq")) + weights.shape[1:], weights.dtype)
+
+
+def call_enter(x, bias, gain_own, wq, wo, wu, wd):
+    batch, tokens, _ = x.shape
+    spans = tokens // SPAN
+    nz, nseq = lax.axis_size("dp"), lax.axis_size("seq")
+    rows = batch * spans
+    keys = SPAN + nseq * spans
+    outs = [sds((batch, tokens, 3 * D), BF16), sds((batch, nseq * spans, 2 * D), BF16),
+            sds((batch, spans, PAIRS, keys, 2 * SPAN), BF16), sds((batch, tokens, D), BF16),
+            sds(gain_own.shape, F32)] + [full_shape(w) for w in (wq, wo, wu, wd, wq)]
+    return pl.pallas_call(
+        functools.partial(enter_kernel, (batch, spans)),
+        grid=(2 * batch,),
+        in_specs=[phased(x.shape, 0, batch), phased(bias.shape, batch, batch)]
+        + [whole(a.shape) for a in (gain_own, wq, wo, wu, wd)],
+        out_specs=[phased(outs[0].shape, 0, batch)] + [phased(o.shape, batch, batch) for o in outs[1:4]]
+        + [whole(gain_own.shape)] + [anywhere()] * 5,
+        out_shape=outs,
+        scratch_shapes=[pltpu.VMEM((batch, tokens, 3 * D), BF16), pltpu.VMEM((rows, 2 * D), F32),
+                        pltpu.VMEM((rows, 2 * D), BF16), pltpu.VMEM((nseq, rows, 2 * D), BF16),
+                        pltpu.VMEM(outs[5].shape, BF16), pltpu.SemaphoreType.DMA, dma(nseq - 1), dma(nseq - 1)]
+        + Fetch.scratch(5, nz) + AllSum.scratch(gain_own.shape, nz),
+        compiler_params=fused_params(0),
+        name="enter",
+    )(x, bias, gain_own, wq, wo, wu, wd)
+
+
+def mid_kernel(counts, *refs):
+    batch, spans = counts
+    (x_ref, o_ref, gains_ref, wo_ref, wu_ref, wd_ref, wq_ref, wo_sh, wu_sh, wd_sh,
+     h_ref, u_ref, next_ref, qkv_ref, raw_ref, fo, fu, fd,
+     own_acc, own_low, land, ex_s, ex_r) = refs[:23]
+    spot = Spot()
+    fetch = Fetch(spot, [wu_sh.at[1], wd_sh.at[1], wo_sh.at[1]], [fu, fd, fo], refs[23:])
+    exchange = Exchange(spot, ex_s, ex_r).spread(own_low, land)
+    u1, d1, o1 = range(3)
+    step = pl.program_id(0)
+
+    @pl.when(step == 0)
+    def _():
+        spot.signal()
+        own_acc[...] = jnp.zeros_like(own_acc)
+
+    hidden = x_ref[0].astype(F32) + dot(o_ref[0], wo_ref[...])
+    h_ref[0] = hidden
+
+    @pl.when(step == 0)
+    def _():
+        spot.meet()
+        for t in range(3):
+            fetch.start(t)
+
+    when(step == 2, does(fetch.spread, u1))
+    when(step == 3, does(fetch.spread, d1), does(fetch.spread, o1))
+    when(step == 4, does(fetch.relay, u1), does(fetch.share, u1))
+    when(step == 5, does(fetch.relay, d1), does(fetch.share, d1), does(fetch.relay, o1))
+    when(step == 6, does(fetch.close, u1), does(fetch.share, o1))
+    when(step == 7, does(fetch.close, d1), does(fetch.close, o1), does(fetch.finish, u1))
+
+    result = mlp_forward(hidden, gains_ref[2:3], wu_ref, wd_ref, u_ref)
+    next_ref[0] = result
+    unit, _ = normed(result)
+    n_one = (unit * gains_ref[1:2]).astype(BF16)
+    pick = span_adder(step, batch, spans, x_ref.shape[1])
+    for part in range(3):
+        cols = slice(part * D, (part + 1) * D)
+        block = dot(n_one, wq_ref[:, cols]).astype(BF16)
+        qkv_ref[0, :, cols] = block
+        if part > 0:
+            own_acc[:, (part - 1) * D : part * D] += dot(pick, block)
+
+    @pl.when(step == batch - 1)
+    def _():
+        own_low[...] = (own_acc[...] * (1.0 / SPAN)).astype(BF16)
+        begin(exchange)
+        land[spot.seq] = own_low[...]
+        fetch.finish(d1)
+        fetch.finish(o1)
+        complete(exchange)
+        raw_ref[...] = land[...]
+        for t in range(3):
+            fetch.drain(t)
+
+
+def call_mid(x, o, gains, wo, wu, wd, wq_next, wo_sh, wu_sh, wd_sh):
+    batch, tokens, _ = x.shape
+    spans = tokens // SPAN
+    nz, nseq = lax.axis_size("dp"), lax.axis_size("seq")
+    rows = batch * spans
+    outs = [sds((batch, tokens, D), F32), sds((batch, tokens, wu.shape[1]), BF16), sds((batch, tokens, D), F32),
+            sds((batch, tokens, 3 * D), BF16), sds((nseq, rows, 2 * D), BF16)]
+    outs += [full_shape(w) for w in (wo_sh, wu_sh, wd_sh)]
+    args = [x, o, gains, wo, wu, wd, wq_next, wo_sh, wu_sh, wd_sh]
+    return pl.pallas_call(
+        functools.partial(mid_kernel, (batch, spans)),
+        grid=(batch,),
+        in_specs=[per_seq(a.shape) for a in args[:2]] + [whole(a.shape) for a in args[2:]],
+        out_specs=[per_seq(a.shape) for a in outs[:4]] + [whole(outs[4].shape)] + [anywhere()] * 3,
+        out_shape=outs,
+        scratch_shapes=[pltpu.VMEM((rows, 2 * D), F32), pltpu.VMEM((rows, 2 * D), BF16),
+                        pltpu.VMEM((nseq, rows, 2 * D), BF16), dma(nseq - 1), dma(nseq - 1)]
+        + Fetch.scratch(3, nz),
+        compiler_params=fused_params(1),
+        name="mid",
+    )(*args)
+
+
+def top_kernel(counts, x_ref, qkv_ref, bias_ref, raw_ref, gains_ref, wo_ref, wu_ref, wd_ref,
+               sums_ref, prob_ref, o_ref, h_ref, u_ref, next_ref):
+    batch, spans, nseq = counts
+    every = raw_ref[...].reshape((-1, raw_ref.shape[-1]))
+    sums_ref[0] = dot(row_picker(pl.program_id(0), batch, spans, nseq), every).astype(BF16)
+    attention_forward(qkv_ref, sums_ref, bias_ref, prob_ref, o_ref)
+    hidden = x_ref[0] + dot(o_ref[0], wo_ref[...])
+    h_ref[0] = hidden
+    result = mlp_forward(hidden, gains_ref[3:4], wu_ref, wd_ref, u_ref)
+    next_ref[0] = result.astype(next_ref.dtype)
+
+
+def call_top(x, qkv, bias, raw, gains, wo, wu, wd):
+    batch, tokens, _ = x.shape
+    spans = tokens // SPAN
+    nseq = raw.shape[0]
+    outs = [sds((batch, nseq * spans, 2 * D), BF16),
+            sds((batch, spans, PAIRS, SPAN + nseq * spans, 2 * SPAN), BF16), sds((batch, tokens, D), BF16),
+            sds((batch, tokens, D), F32), sds((batch, tokens, wu.shape[1]), BF16), sds((batch, tokens, D), BF16)]
+    args = [x, qkv, bias, raw, gains, wo, wu, wd]
+    return pl.pallas_call(
+        functools.partial(top_kernel, (batch, spans, nseq)),
+        grid=(batch,),
+        in_specs=[per_seq(a.shape) for a in args[:3]] + [whole(a.shape) for a in args[3:]],
+        out_specs=[per_seq(a.shape) for a in outs],
+        out_shape=outs,
+        compiler_params=params(),
+        name="top",
+    )(*args)
+
+
+def mlp_back(dy32, u_ref, h_ref, o_ref, gain, wo_ref, wu_ref, wd_ref, dh_ref, gd_ref, gu_ref, go_ref, gg_ref):
+    ddown = dy32.astype(BF16)
+    unit, rstd = normed(h_ref[0])
+    n_two = (unit * gain).astype(BF16)
+    dn_two = 0.0
+    for start in range(0, wu_ref.shape[1], CHUNK):
+        cols = slice(start, start + CHUNK)
+        dactive = dot(ddown, wd_ref[cols, :], NT)
+        active, slope = gelu_both(u_ref[0, :, cols].astype(F32))
+        gd_ref[cols, :] += dot(active.astype(BF16), ddown, TN)
+        dupper = (dactive * slope).astype(BF16)
+        gu_ref[:, cols] += dot(n_two, dupper, TN)
+        dn_two = dn_two + dot(dupper, wu_ref[:, cols], NT)
+    dnorm, grad_gain = norm_backward(dn_two, unit, rstd, gain)
+    gg_ref[...] += grad_gain
+    dhidden = dy32 + dnorm
+    dh_ref[0] = dhidden
+    dattn = dhidden.astype(BF16)
+    go_ref[...] += dot(o_ref[0], dattn, TN)
+    return dot(dattn, wo_ref[...], NT).astype(BF16)
+
+
+def pile(b, batch, spans, nseq, dsums_ref, part_acc):
+    part_acc[...] += dot(row_picker(b, batch, spans, nseq), dsums_ref[0], TN)
+
+
+def ship(spot, part_acc, part_low, copies):
+    part_low[...] = part_acc[...].astype(BF16).reshape(part_low.shape)
+    begin(copies)
+
+
+def gathered(spot, part_low, land, copies):
+    total = part_low[spot.seq].astype(F32)
+    complete(copies)
+    for d in range(spot.nseq - 1):
+        total = total + land[d].astype(F32)
+    return total
+
+
+def zero(*refs):
+    for ref in refs:
+        ref[...] = jnp.zeros_like(ref)
+
+
+def base_kernel(counts, *refs):
+    batch, spans = counts
+    (dy_ref, u_ref, h_ref, o_ref, prob_ref, qkv_ref, sums_ref, gains_ref, wo_ref, wu_ref, wd_ref,
+     dh_ref, dqkv_ref, total_ref, gd_out, gu_out, go_out, gg_ref,
+     gd_ref, gu_ref, go_ref, dsums, part_acc, part_low, land, ex_s, ex_r) = refs
+    spot = Spot()
+    exchange = Exchange(spot, ex_s, ex_r).collect(part_low, land)
+    step = pl.program_id(0)
+
+    @pl.when(step == 0)
+    def _():
+        spot.signal()
+        zero(gd_ref, gu_ref, go_ref, gg_ref, part_acc)
+
+    dout = mlp_back(dy_ref[0].astype(F32), u_ref, h_ref, o_ref, gains_ref[3:4], wo_ref, wu_ref, wd_ref,
+                    dh_ref, gd_ref, gu_ref, go_ref, gg_ref)
+    attention_backward(qkv_ref, sums_ref, prob_ref, dout, dqkv_ref, dsums)
+    pile(step, batch, spans, spot.nseq, dsums, part_acc)
+
+    @pl.when(step == batch - 1)
+    def _():
+        spot.meet()
+        ship(spot, part_acc, part_low, exchange)
+        gd_out[...] = gd_ref[...].astype(BF16)
+        gu_out[...] = gu_ref[...].astype(BF16)
+        go_out[...] = go_ref[...].astype(BF16)
+        total_ref[...] = gathered(spot, part_low, land, exchange)
+
+
+def call_base(dy, u, h, o, prob, qkv, sums, gains, wo, wu, wd):
+    batch, tokens, _ = dy.shape
+    spans = tokens // SPAN
+    nseq = lax.axis_size("seq")
+    rows = batch * spans
+    args = [dy, u, h, o, prob, qkv, sums, gains, wo, wu, wd]
+    outs = [sds(h.shape, F32), sds(qkv.shape, BF16), sds((rows, 2 * D), F32), sds(wd.shape, BF16),
+            sds(wu.shape, BF16), sds(wo.shape, BF16), sds((1, D), F32)]
+    return pl.pallas_call(
+        functools.partial(base_kernel, (batch, spans)),
+        grid=(batch,),
+        in_specs=[per_seq(a.shape) for a in args[:7]] + [whole(a.shape) for a in args[7:]],
+        out_specs=[per_seq(a.shape) for a in outs[:2]] + [whole(a.shape) for a in outs[2:]],
+        out_shape=outs,
+        scratch_shapes=[pltpu.VMEM(wd.shape, F32), pltpu.VMEM(wu.shape, F32), pltpu.VMEM(wo.shape, F32),
+                        pltpu.VMEM((1, nseq * spans, 2 * D), BF16), pltpu.VMEM((nseq * rows, 2 * D), F32),
+                        pltpu.VMEM((nseq, rows, 2 * D), BF16), pltpu.VMEM((nseq - 1, rows, 2 * D), BF16),
+                        dma(nseq - 1), dma(nseq - 1)],
+        compiler_params=fused_params(2),
+        name="base",
+    )(*args)
+
+
+def qkv_back(x32, gain, near, share, dh, weight, gq_ref, gg_ref):
+    unit, rstd = normed(x32)
+    n_one = (unit * gain).astype(BF16)
+    dn_one = 0.0
+    for part in range(3):
+        cols = slice(part * D, (part + 1) * D)
+        block = near(cols)
+        if part > 0:
+            pieces = []
+            for span in range(x32.shape[0] // SPAN):
+                row = share(span, slice((part - 1) * D, part * D)) * (1.0 / SPAN)
+                pieces.append(block[span * SPAN : (span + 1) * SPAN].astype(F32) + row)
+            block = jnp.concatenate(pieces, 0).astype(BF16)
+        gq_ref[:, cols] += dot(n_one, block, TN)
+        dn_one = dn_one + dot(block, weight(cols), NT)
+    dnorm, grad_gain = norm_backward(dn_one, unit, rstd, gain)
+    gg_ref[...] += grad_gain
+    return dh + dnorm
+
+
+def turn_kernel(counts, *refs):
+    batch, spans = counts
+    (x_ref, near_ref, dh_ref, u_ref, h_ref, o_ref, total_ref, gains_ref, wq_ref, wo_ref, wu_ref, wd_ref,
+     pd, pu, po,
+     dh_out, dout_out, gd_out, gu_out, go_out, ggq_ref, gg_ref, sd, su, so, sq,
+     dx_all, gq_ref, gd_ref, gu_ref, go_ref, gq_low) = refs[:32]
+    rest = refs[32:]
+    spot = Spot()
+    fold = Fold(spot, [pd, pu, po, gq_low], [sd, su, so, sq], rest[:24], rest[24:])
+    d1, u1, o1, q1 = range(4)
+    step = pl.program_id(0)
+
+    @pl.when(step == 0)
+    def _():
+        spot.signal()
+        zero(gq_ref, gd_ref, gu_ref, go_ref, gg_ref, ggq_ref)
+        spot.meet()
+        for t in range(3):
+            fold.start(t)
+
+    when(step == 2, does(fold.combine, d1))
+    when(step == 3, does(fold.combine, u1))
+    when(step == 4, does(fold.combine, o1))
+    when(step == 6, does(fold.middle, d1))
+
+    @pl.when(step == batch)
+    def _():
+        gq_low[...] = gq_ref[...].astype(BF16).reshape(gq_low.shape)
+        fold.start(q1)
+        fold.middle(u1)
+
+    when(step == batch + 1, does(fold.middle, o1), does(fold.column, d1), does(fold.combine, q1))
+    when(step == batch + 2, does(fold.column, u1), does(fold.column, o1))
+    when(step == batch + 3, does(fold.middle, q1), does(fold.finish, d1))
+    when(step == batch + 4, does(fold.finish, u1), does(fold.finish, o1))
+    when(step == batch + 5, does(fold.column, q1))
+    when(step == batch + 7, does(fold.finish, q1))
+
+    @pl.when(step < batch)
+    def _():
+        dx_all[step] = qkv_back(
+            x_ref[0], gains_ref[1:2], lambda cols: near_ref[0, :, cols],
+            lambda span, cols: total_ref[pl.ds(step * spans + span, 1), cols], dh_ref[0],
+            lambda cols: wq_ref[:, cols], gq_ref, ggq_ref)
+
+    @pl.when(step >= batch)
+    def _():
+        dout_out[0] = mlp_back(dx_all[step - batch], u_ref, h_ref, o_ref, gains_ref[2:3], wo_ref, wu_ref, wd_ref,
+                               dh_out, gd_ref, gu_ref, go_ref, gg_ref)
+
+    @pl.when(step == 2 * batch - 1)
+    def _():
+        gd_out[...] = gd_ref[...].astype(BF16)
+        gu_out[...] = gu_ref[...].astype(BF16)
+        go_out[...] = go_ref[...].astype(BF16)
+        for t in range(4):
+            fold.drain(t)
+
+
+def by_owner(part):
+    nz, nseq = lax.axis_size("dp"), lax.axis_size("seq")
+    return part.reshape((nz, nseq // CORES, CORES, part.shape[0] // (nz * nseq)) + part.shape[1:])
+
+
+def call_turn(x, near, dh, u, h, o, total, gains, wq, wo, wu, wd, pd, pu, po):
+    batch, tokens, _ = x.shape
+    nz = lax.axis_size("dp")
+    parts = [by_owner(a) for a in (pd, pu, po)]
+    owned = by_owner(sds_like(wq))
+    shapes = [a.shape[3:] for a in parts] + [owned.shape[3:]]
+    args = [x, near, dh, u, h, o, total, gains, wq, wo, wu, wd] + parts
+    outs = [sds(h.shape, F32), sds(o.shape, BF16), sds(wd.shape, BF16), sds(wu.shape, BF16), sds(wo.shape, BF16),
+            sds((1, D), F32), sds((1, D), F32)] + [sds(s, F32) for s in shapes]
+    return pl.pallas_call(
+        functools.partial(turn_kernel, (batch, tokens // SPAN)),
+        grid=(2 * batch,),
+        in_specs=[phased(a.shape, 0, batch) for a in args[:3]] + [phased(a.shape, batch, batch) for a in args[3:6]]
+        + [whole(a.shape) for a in args[6:12]] + [anywhere()] * 3,
+        out_specs=[phased(a.shape, batch, batch) for a in outs[:2]] + [whole(a.shape) for a in outs[2:]],
+        out_shape=outs,
+        scratch_shapes=[pltpu.VMEM(x.shape, F32), pltpu.VMEM(wq.shape, F32), pltpu.VMEM(wd.shape, F32),
+                        pltpu.VMEM(wu.shape, F32), pltpu.VMEM(wo.shape, F32), pltpu.VMEM(owned.shape, BF16)]
+        + Fold.buffers(shapes, nz) + Fold.sems(4, nz),
+        compiler_params=fused_params(3),
+        name="turn",
+    )(*args)
+
+
+def sds_like(a):
+    class Shaped:
+        shape = a.shape
+
+        def reshape(self, shape):
+            return sds(shape, a.dtype)
+
+    return Shaped()
+
+
+def leave_kernel(counts, *refs):
+    batch, spans = counts
+    (prob_ref, qkv_ref, sums_ref, dout_ref, x_ref, dh_ref, gains_ref, wq_ref, g_mlp0, g_attn1, g_mlp1,
+     pd, pu, po,
+     dx_ref, gsum_ref, sd, su, so, sq,
+     near_all, gq_ref, gq_low, gg_ref, gain_src, dsums, part_acc, part_low, land, total, ex_s, ex_r) = refs[:32]
+    rest = refs[32:]
+    spot = Spot()
+    fold = Fold(spot, [pd, pu, po, gq_low], [sd, su, so, sq], rest[:24], rest[24:31])
+    adder = AllSum(spot, gain_src, rest[31:])
+    exchange = Exchange(spot, ex_s, ex_r).collect(part_low, land)
+    d0, u0, o0, q0 = range(4)
+    step = pl.program_id(0)
+
+    @pl.when(step == 0)
+    def _():
+        spot.signal()
+        zero(gq_ref, gg_ref, part_acc)
+        spot.meet()
+        for t in range(3):
+            fold.start(t)
+
+    when(step == 2, does(fold.combine, d0))
+    when(step == 3, does(fold.combine, u0))
+    when(step == 4, does(fold.combine, o0))
+    when(step == 6, does(fold.middle, d0))
+
+    @pl.when(step == batch)
+    def _():
+        total[...] = gathered(spot, part_low, land, exchange)
+        fold.middle(u0)
+        fold.middle(o0)
+
+    when(step == batch + 1, does(fold.column, d0))
+    when(step == batch + 3, does(fold.column, u0), does(fold.column, o0))
+    when(step == batch + 5, does(fold.finish, d0))
+    when(step == batch + 6, does(fold.finish, u0), does(fold.finish, o0))
+
+    @pl.when(step < batch)
+    def _():
+        attention_backward(qkv_ref, sums_ref, prob_ref, dout_ref[0], near_all.at[pl.ds(step, 1)], dsums)
+        pile(step, batch, spans, spot.nseq, dsums, part_acc)
+
+    when(step == batch - 1, does(ship, spot, part_acc, part_low, exchange))
+
+    @pl.when(step >= batch)
+    def _():
+        b = step - batch
+        dx_ref[0] = qkv_back(
+            x_ref[0].astype(F32), gains_ref[0:1], lambda cols: near_all[b, :, cols],
+            lambda span, cols: total[pl.ds(b * spans + span, 1), cols], dh_ref[0],
+            lambda cols: wq_ref[:, cols], gq_ref, gg_ref)
+
+    @pl.when(step == 2 * batch - 1)
+    def _():
+        gq_low[...] = gq_ref[...].astype(BF16).reshape(gq_low.shape)
+        fold.start(q0)
+        gain_src[...] = jnp.zeros_like(gain_src)
+        gain_src[0:1] = gg_ref[...]
+        gain_src[1:2] = g_attn1[...]
+        gain_src[2:3] = g_mlp0[...]
+        gain_src[3:4] = g_mlp1[...]
+        adder.start()
+        fold.combine(q0)
+        adder.plane()
+        fold.middle(q0)
+        adder.column()
+        fold.column(q0)
+        gsum_ref[...] = adder.total()
+        fold.finish(q0)
+        for t in range(4):
+            fold.drain(t)
+        adder.drain()
+
+
+def call_leave(prob, qkv, sums, dout, x, dh, gains, wq, g_mlp0, g_attn1, g_mlp1, pd, pu, po):
+    batch, tokens, _ = x.shape
+    spans = tokens // SPAN
+    nz, nseq = lax.axis_size("dp"), lax.axis_size("seq")
+    rows = batch * spans
+    parts = [by_owner(a) for a in (pd, pu, po)]
+    owned = by_owner(sds_like(wq))
+    shapes = [a.shape[3:] for a in parts] + [owned.shape[3:]]
+    args = [prob, qkv, sums, dout, x, dh, gains, wq, g_mlp0, g_attn1, g_mlp1] + parts
+    outs = [sds(dh.shape, F32), sds(gains.shape, F32)] + [sds(s, F32) for s in shapes]
+    return pl.pallas_call(
+        functools.partial(leave_kernel, (batch, spans)),
+        grid=(2 * batch,),
+        in_specs=[phased(a.shape, 0, batch) for a in args[:4]] + [phased(a.shape, batch, batch) for a in args[4:6]]
+        + [whole(a.shape) for a in args[6:11]] + [anywhere()] * 3,
+        out_specs=[phased(outs[0].shape, batch, batch)] + [whole(a.shape) for a in outs[1:]],
+        out_shape=outs,
+        scratch_shapes=[pltpu.VMEM(qkv.shape, BF16), pltpu.VMEM(wq.shape, F32), pltpu.VMEM(owned.shape, BF16),
+                        pltpu.VMEM((1, D), F32), pltpu.VMEM(gains.shape, F32),
+                        pltpu.VMEM((1, nseq * spans, 2 * D), BF16), pltpu.VMEM((nseq * rows, 2 * D), F32),
+                        pltpu.VMEM((nseq, rows, 2 * D), BF16), pltpu.VMEM((nseq - 1, rows, 2 * D), BF16),
+                        pltpu.VMEM((rows, 2 * D), F32), dma(nseq - 1), dma(nseq - 1)]
+        + Fold.buffers(shapes, nz) + Fold.sems(4, nz) + AllSum.scratch(gains.shape, nz),
+        compiler_params=fused_params(4),
+        name="leave",
+    )(*args)
+
+
+def pack_kernel(count, *refs):
+    ins, outs = refs[: 2 * count], refs[2 * count :]
+    for m in range(count):
+        for l in range(2):
+            outs[m][l] = ins[2 * m + l][...]
+
+
+def call_pack(pairs):
+    flat = [a for pair in pairs for a in pair]
+    outs = [sds((2,) + pair[0].shape, F32) for pair in pairs]
+    vmem = pl.BlockSpec(memory_space=pltpu.VMEM)
+    return pl.pallas_call(
+        functools.partial(pack_kernel, len(pairs)),
+        in_specs=[vmem] * len(flat),
+        out_specs=[vmem] * len(pairs),
+        out_shape=outs,
+        name="pack",
+    )(*flat)
+
+
+def fused(inputs, segments, w_qkv, w_out, w_up, w_down, gain_attn, gain_mlp, cotangent):
+    stretch = inputs.shape[1]
+    slots = gain_attn.shape[1]
+    rank = lax.axis_index("dp") * lax.axis_size("seq") + lax.axis_index("seq")
+    own = jnp.concatenate([gain_attn, gain_mlp], 0).astype(F32)
+    own = jnp.pad(own, ((0, 4), (0, 0)))
+    gain_own = lax.dynamic_update_slice(jnp.zeros((8, D), F32), own, (0, rank * slots))
+    bias = mask_bias(segments, stretch)
+
+    def flat(a):
+        return a.reshape((-1, a.shape[-1]))
+
+    qkv0, sums0, prob0, o0, gains, wq0, wo0, wu0, wd0, wq1 = call_enter(
+        inputs, bias, gain_own, w_qkv, w_out, w_up, w_down)
+    wq0, wo0, wu0, wd0, wq1 = (flat(a) for a in (wq0, wo0, wu0, wd0, wq1))
+    h0, u0, x1, qkv1, raw1, wo1, wu1, wd1 = call_mid(
+        inputs, o0, gains, wo0, wu0, wd0, wq1, w_out, w_up, w_down)
+    wo1, wu1, wd1 = flat(wo1), flat(wu1), flat(wd1)
+    sums1, prob1, o1, h1, u1, outputs = call_top(x1, qkv1, bias, raw1, gains, wo1, wu1, wd1)
+    dh1, near1, total1, gd1, gu1, go1, g_mlp1 = call_base(
+        cotangent, u1, h1, o1, prob1, qkv1, sums1, gains, wo1, wu1, wd1)
+    dh0, dout0, gd0, gu0, go0, g_attn1, g_mlp0, sd1, su1, so1, sq1 = call_turn(
+        x1, near1, dh1, u0, h0, o0, total1, gains, wq1, wo0, wu0, wd0, gd1, gu1, go1)
+    dx, gsum, sd0, su0, so0, sq0 = call_leave(
+        prob0, qkv0, sums0, dout0, inputs, dh0, gains, wq0, g_mlp0, g_attn1, g_mlp1, gd0, gu0, go0)
+    gq, go, gu, gd = call_pack([(sq0, sq1), (so0, so1), (su0, su1), (sd0, sd1)])
+    gain_share = lax.dynamic_slice(gsum, (0, rank * slots), (4, slots))
+    return outputs, dx, gq, go, gu, gd, gain_share[:2], gain_share[2:]
+
+
+def choose(*args):
+    square = lax.axis_size("seq") == 4 * CORES
+    if square and args[2].shape[1] % 16 == 0 and args[2].shape[0] == 2:
+        return fused(*args)
+    return on_device(*args)
+
+
 def solution(mesh):
     weights = P(None, ("dp", "seq"), None)
     gains = P(None, ("dp", "seq"))
     rows = P("dp", "seq", None)
     return jax.shard_map(
-        on_device,
+        choose,
         mesh=mesh,
         in_specs=(rows, P("dp", None), weights, weights, weights, weights, gains, gains, rows),
         out_specs=(rows, rows, weights, weights, weights, weights, gains, gains),

time: 471 us -> 367 us (0.78)
  Pallas kernels: 437 us -> 355 us
  local copies, waits for them, and re-layouts: 21.5 us -> 8.08 us
  other arithmetic: 10.1 us -> 2.43 us
    pallas_call x13 -> x7, Pallas kernels: 437 us -> 355 us  [the longest x1 71.9 us: call_enter(): pl.pallas_call(functools.partial(enter_kernel, (batch, spans)), grid=(2 *...]
    another operation x4 -> x0, other arithmetic: 6.41 us -> none  [on_device(): stacked = [jnp.stack(shares[m:4 * layers:4]) for m in range(4)]]
    squeeze x4 -> x0, local copies, waits for them, and re-layouts: 5.86 us -> none  [on_device(): shards += [w_qkv[l], w_out[l], w_up[l], w_down[l]]]
where the time goes in v3:
time: 367 us; the launch traced here: 366 us
  Pallas kernels  355 us (97%)
  local copies, waits for them, and re-layouts  8.08 us (2%)
    pallas_call x1, Pallas kernels, call_enter(): pl.pallas_call(functools.partial(enter_kernel, (batch, spans)), grid=(2 *...  71.9 us
    pallas_call x1, Pallas kernels, call_leave(): pl.pallas_call(functools.partial(leave_kernel, (batch, spans)), grid=(2 *...  71.1 us
    pallas_call x1, Pallas kernels, call_base(): pl.pallas_call(functools.partial(base_kernel, (batch, spans)), grid=(batc...  64.6 us
    pallas_call x1, Pallas kernels, call_turn(): pl.pallas_call(functools.partial(turn_kernel, (batch, tokens // SPAN)), g...  64.6 us
    pallas_call x1, Pallas kernels, call_mid(): pl.pallas_call(functools.partial(mid_kernel, (batch, spans)), grid=(batch...  44.9 us
    pallas_call x1, Pallas kernels, call_top(): pl.pallas_call(functools.partial(top_kernel, (batch, spans, nseq)), grid=...  35.8 us

profile of v3, /device:TPU:0, one launch (start us, length us, event | category | flops | bytes accessed | tf_op | source)
XLA Modules:
  0.0 366.2 jit_solution(925579921471029381)
XLA Ops:
  0.7 0.1 iota_compare_fusion.2
  0.7 0.7 fusion.3
  1.4 0.7 constant_dynamic-slice_fusion.1
  2.1 0.2 dynamic_update_slice.3.refs_2_
  2.4 0.0 copy-start
  2.4 0.9 copy.19
  3.3 0.3 slice_reduce_fusion
  3.6 0.1 compare_and_fusion.1
  3.7 0.3 compare_and_fusion
  4.0 1.2 add_select_fusion.refs_1_.bias_ref
  5.2 0.0 copy-done
  5.2 71.9 %enter.1 = (bf16[8,256,1536]{2,1,0:T(8,128)(2,1)}, bf16[8,16,1024]{2,1,0:T(8,128)(2,1)}, bf16[8,2,4,144,256]{4,3,2,1,0:T(8,128)(2,1)}, bf16[8,256,512]{2,1,0:T(8...) custom-call(bf16[8,256,512]{2,1,0:T(8,128)(2,1)} %refs_4_.3, ...), custom_call_target="tpu_custom_call" | custom-call | tf_op jit(solution)/shard_map/enter/pallas_call | solution.py:1222
  77.1 44.9 %mid.1 = (f32[8,256,512]{2,1,0:T(8,128)}, bf16[8,256,2048]{2,1,0:T(8,128)(2,1)}, f32[8,256,512]{2,1,0:T(8,128)}, bf16[8,256,1536]{2,1,0:T(8,128)(2,1)}, bf16[8,1...) custom-call(bf16[8,256,512]{2,1,0:T(8,128)(2,1)} %refs_4_.3, ...), custom_call_target="tpu_custom_call" | custom-call | tf_op jit(solution)/shard_map/mid/pallas_call | solution.py:1305
  122.0 35.8 %top.1 = (bf16[8,16,1024]{2,1,0:T(8,128)(2,1)}, bf16[8,2,4,144,256]{4,3,2,1,0:T(8,128)(2,1)}, bf16[8,256,512]{2,1,0:T(8,128)(2,1)}, f32[8,256,512]{2,1,0:T(8,128...) custom-call(f32[8,256,512]{2,1,0:T(8,128)} %get-tuple-element.66.x_ref.refs_0_, ...), custom_call_target="tpu_custom_call" | custom-call | tf_op jit(solution)/shard_map/top/pallas_call | solution.py:1339
  157.8 64.6 %base.1 = (f32[8,256,512]{2,1,0:T(8,128)}, bf16[8,256,1536]{2,1,0:T(8,128)(2,1)}, f32[16,1024]{1,0:T(8,128)}, bf16[2048,512]{1,0:T(8,128)(2,1)}, bf16[512,2048]{...) custom-call(bf16[8,256,512]{2,1,0:T(8,128)(2,1)} %refs_0_.5, ...), custom_call_target="tpu_custom_call" | custom-call | tf_op jit(solution)/shard_map/base/pallas_call | solution.py:1431
  222.4 64.6 %turn.1 = (f32[8,256,512]{2,1,0:T(8,128)}, bf16[8,256,512]{2,1,0:T(8,128)(2,1)}, bf16[2048,512]{1,0:T(8,128)(2,1)}, bf16[512,2048]{1,0:T(8,128)(2,1)}, bf16[512,...) custom-call(f32[8,256,512]{2,1,0:T(8,128)} %get-tuple-element.66.x_r, ...), custom_call_target="tpu_custom_call" | custom-call | tf_op jit(solution)/shard_map/turn/pallas_call | solution.py:1539
  287.0 71.1 %leave.1 = (f32[8,256,512]{2,1,0:T(8,128)}, f32[8,512]{1,0:T(8,128)}, f32[64,512]{1,0:T(8,128)}, f32[16,2048]{1,0:T(8,128)}, f32[16,512]{1,0:T(8,128)}, /*index=5*/f32[16,1536]{1,0:T(8,128)}) custom-call(bf16[8,2,4,144,256]{4,3,2,1,0:T(8,128)(2,1)} %get-tuple-element.73.refs_0_, bf16[8,256,1536]{2,1,0:T(8,128)(2,1)} %get-tuple-element.74.refs_1_, ...), custom_call_target="tpu_custom_call" | custom-call | tf_op jit(solution)/shard_map/leave/pallas_call | solution.py:1649
  358.1 0.8 constant_dynamic-slice_fusion
  358.9 0.6 fusion.4
  359.5 2.1 pack.1
  361.6 4.6 %copy.22 = f32[8,256,512]{2,1,0:T(8,128)} copy(f32[8,256,512]{2,1,0:T(8,128)} %get-tuple-element.123) | data formatting | bytes 8388608
  (4 shorter events, 0.0 us)
Async XLA Ops:
  2.4 2.9 copy-start

commit v4 on v3

--- a/solution.py
+++ b/solution.py
@@ -90,55 +90,63 @@
 
 def attention_forward(qkv_ref, sums_ref, bias_ref, prob_ref, o_ref):
     low = lane_halves()
-    spans = qkv_ref.shape[1] // SPAN
-    for span in range(spans):
-        bias = bias_ref[0, span]
-        bias = jnp.concatenate([bias, bias], 1)
-        for pair in range(PAIRS):
-            query, keys, values = pair_operands(qkv_ref, sums_ref, span, pair)
-            scores = dot(keys, head_stack(query, low, SCALE), NT) + bias
-            top = jnp.max(scores, 0, keepdims=True)
-            exps = jnp.exp(scores - top)
-            total = jnp.sum(exps, 0, keepdims=True)
-            prob = (exps * (1.0 / total)).astype(BF16)
+    units = [(span, pair) for span in range(qkv_ref.shape[1] // SPAN) for pair in range(PAIRS)]
+    for start in range(0, len(units), GROUP):
+        group = units[start : start + GROUP]
+        operands = [pair_operands(qkv_ref, sums_ref, span, pair) for span, pair in group]
+        scores = []
+        for (span, _), (query, keys, _) in zip(group, operands):
+            bias = bias_ref[0, span]
+            bias = jnp.concatenate([bias, bias], 1)
+            scores.append(dot(keys, head_stack(query, low, SCALE), NT) + bias)
+        exps = [jnp.exp(score - jnp.max(score, 0, keepdims=True)) for score in scores]
+        probs = [(e * (1.0 / jnp.sum(e, 0, keepdims=True))).astype(BF16) for e in exps]
+        both = [dot(prob, values, TN) for prob, (_, _, values) in zip(probs, operands)]
+        for (span, pair), prob, out in zip(group, probs, both):
             prob_ref[0, span, pair] = prob
-            both = dot(prob, values, TN)
             o_ref[0, span * SPAN : (span + 1) * SPAN, pair * 128 : (pair + 1) * 128] = jnp.where(
-                low, both[:SPAN], both[SPAN:]
+                low, out[:SPAN], out[SPAN:]
             ).astype(BF16)
 
 
 def attention_backward(qkv_ref, sums_ref, prob_ref, dout, dqkv_ref, dsums_ref):
     low = lane_halves()
     spans = qkv_ref.shape[1] // SPAN
-    for pair in range(PAIRS):
-        lanes = slice(pair * 128, (pair + 1) * 128)
-        klanes = slice(D + pair * 128, D + (pair + 1) * 128)
-        vlanes = slice(2 * D + pair * 128, 2 * D + (pair + 1) * 128)
-        dksum = dvsum = 0.0
-        for span in range(spans):
+    for start in range(0, PAIRS, BACK_GROUP):
+        pairs = range(start, start + BACK_GROUP)
+        units = [(span, pair) for pair in pairs for span in range(spans)]
+        operands = [pair_operands(qkv_ref, sums_ref, span, pair) for span, pair in units]
+        q_stacks = [head_stack(query, low, SCALE) for query, _, _ in operands]
+        do_stacks = [
+            head_stack(dout[span * SPAN : (span + 1) * SPAN, pair * 128 : (pair + 1) * 128], low, 1.0)
+            for span, pair in units
+        ]
+        probs = [prob_ref[0, span, pair] for span, pair in units]
+        dprobs = [dot(values, do_stack, NT) for (_, _, values), do_stack in zip(operands, do_stacks)]
+        dvalues = [dot(prob, do_stack) for prob, do_stack in zip(probs, do_stacks)]
+        dscores = []
+        for prob, dprob in zip(probs, dprobs):
+            wide = prob.astype(F32)
+            product = wide * dprob
+            dscores.append((product - wide * jnp.sum(product, 0, keepdims=True)).astype(BF16))
+        dkeys = [dot(dscore, q_stack) for dscore, q_stack in zip(dscores, q_stacks)]
+        dboths = [dot(dscore, keys, TN) for dscore, (_, keys, _) in zip(dscores, operands)]
+        for (span, pair), dboth, dkey, dvalue in zip(units, dboths, dkeys, dvalues):
             rows = slice(span * SPAN, (span + 1) * SPAN)
-            query, keys, values = pair_operands(qkv_ref, sums_ref, span, pair)
-            q_stack = head_stack(query, low, SCALE)
-            do_stack = head_stack(dout[rows, lanes], low, 1.0)
-            prob = prob_ref[0, span, pair]
-            wide = prob.astype(F32)
-            dprob = dot(values, do_stack, NT)
-            rowdot = jnp.sum(wide * dprob, 0, keepdims=True)
-            dscore = (wide * (dprob - rowdot)).astype(BF16)
-            dboth = dot(dscore, keys, TN)
             dquery = jnp.where(low, dboth[:SPAN], dboth[SPAN:]) * SCALE
-            dkeys = dot(dscore, q_stack)
-            dvalues = dot(prob, do_stack)
-            dqkv_ref[0, rows, lanes] = dquery.astype(BF16)
-            dqkv_ref[0, rows, klanes] = dkeys[:SPAN].astype(BF16)
-            dqkv_ref[0, rows, vlanes] = dvalues[:SPAN].astype(BF16)
-            dksum = dksum + dkeys[SPAN:]
-            dvsum = dvsum + dvalues[SPAN:]
-        dsums_ref[0, :, pair * 128 : (pair + 1) * 128] = dksum.astype(BF16)
-        dsums_ref[0, :, D + pair * 128 : D + (pair + 1) * 128] = dvsum.astype(BF16)
-
-
+            for part, block in enumerate((dquery, dkey[:SPAN], dvalue[:SPAN])):
+                lanes = slice(part * D + pair * 128, part * D + (pair + 1) * 128)
+                dqkv_ref[0, rows, lanes] = block.astype(BF16)
+        for at, pair in enumerate(pairs):
+            mine = range(at * spans, (at + 1) * spans)
+            dksum = sum(dkeys[i][SPAN:] for i in mine)
+            dvsum = sum(dvalues[i][SPAN:] for i in mine)
+            dsums_ref[0, :, pair * 128 : (pair + 1) * 128] = dksum.astype(BF16)
+            dsums_ref[0, :, D + pair * 128 : D + (pair + 1) * 128] = dvsum.astype(BF16)
+
+
+GROUP = 8
+BACK_GROUP = 4
 G0 = 0.7978845608
 G1 = 0.7978845608 * 0.044715
 
@@ -933,7 +941,7 @@
             self.cross(t, k).wait_recv()
 
             def add(i, carry):
-                mine[k, i] = (mine[k, i].astype(F32) + twin_in[k, i].astype(F32)).astype(BF16)
+                mine[k, i] = mine[k, i] + twin_in[k, i]
                 return carry
 
             lax.fori_loop(0, self.spot.nz, add, 0)
@@ -947,7 +955,7 @@
         self.hop(t, 1).wait_recv()
 
         def add(i, carry):
-            mine[2, i] = (mine[2, i].astype(F32) + first_in[1, i].astype(F32)).astype(BF16)
+            mine[2, i] = mine[2, i] + first_in[1, i]
             return carry
 
         lax.fori_loop(0, self.spot.nz, add, 0)
@@ -1038,23 +1046,30 @@
             self.line(d).wait_send()
 
 
+HALVES = 2
+
+
 class Exchange:
-    def __init__(self, spot, ss, rs):
-        self.spot, self.ss, self.rs = spot, ss, rs
-
-    def copies(self, source, target):
+    def __init__(self, spot, sources, lands, ss, rs):
+        self.spot, self.sources, self.lands, self.ss, self.rs = spot, sources, lands, ss, rs
+
+    @staticmethod
+    def sems(nseq):
+        return [dma(HALVES, nseq - 1), dma(HALVES, nseq - 1)]
+
+    def copies(self, h, source, target):
         spot = self.spot
         out = []
         for d in range(1, spot.nseq):
             s = modulo(spot.seq + d, spot.nseq)
-            out.append(remote(source(s), target(d), self.ss.at[d - 1], self.rs.at[d - 1], (spot.z, s)))
+            out.append(remote(source(s), target(d), self.ss.at[h, d - 1], self.rs.at[h, d - 1], (spot.z, s)))
         return out
 
-    def spread(self, own, land):
-        return self.copies(lambda s: own, lambda d: land.at[self.spot.seq])
-
-    def collect(self, parts, land):
-        return self.copies(lambda s: parts.at[s], lambda d: land.at[d - 1])
+    def spread(self, h):
+        return self.copies(h, lambda s: self.sources[h], lambda d: self.lands[h].at[self.spot.seq])
+
+    def collect(self, h):
+        return self.copies(h, lambda s: self.sources[h].at[s], lambda d: self.lands[h].at[d - 1])
 
 
 def begin(copies):
@@ -1104,20 +1119,33 @@
     return block.reshape((-1, block.shape[-1]))
 
 
+def send_means(exchange, h, own_acc):
+    rows = own_acc.shape[0] // HALVES
+    exchange.sources[h][...] = (own_acc[h * rows : (h + 1) * rows] * (1.0 / SPAN)).astype(BF16)
+    begin(exchange.spread(h))
+    exchange.lands[h][exchange.spot.seq] = exchange.sources[h][...]
+
+
+def pick_sums(b, counts, nseq, land):
+    batch, spans = counts
+    every = land.reshape((-1, land.shape[-1]))
+    return dot(row_picker(b, batch // HALVES, spans, nseq), every).astype(BF16)
+
+
 def enter_kernel(counts, *refs):
     batch, spans = counts
     (x_ref, bias_ref, gain_own, wq_sh, wo_sh, wu_sh, wd_sh,
-     qkv_ref, sums_ref, prob_ref, o_ref, gains_ref, fq, fo, fu, fd, fq_next,
-     qkv_all, own_acc, own_low, land, wq_in, wq_sem, ex_s, ex_r) = refs[:25]
-    rest = refs[25:]
+     qkv_ref, sums_ref, prob_ref, o_ref, gains_ref, fq, fo, fu, fd,
+     qkv_all, own_acc, own_a, own_b, land_a, land_b, wq_in, wq_sem, ex_s, ex_r) = refs[:26]
+    rest = refs[26:]
     spot = Spot()
-    fetch = Fetch(spot, [wq_sh.at[0], wo_sh.at[0], wu_sh.at[0], wd_sh.at[0], wq_sh.at[1]],
-                  [fq, fo, fu, fd, fq_next], rest[:7])
+    fetch = Fetch(spot, [wq_sh.at[0], wo_sh.at[0], wu_sh.at[0], wd_sh.at[0]], [fq, fo, fu, fd], rest[:7])
     adder = AllSum(spot, gain_own, rest[7:])
-    exchange = Exchange(spot, ex_s, ex_r).spread(own_low, land)
-    q0, o0, u0, d0, q1 = range(5)
+    exchange = Exchange(spot, [own_a, own_b], [land_a, land_b], ex_s, ex_r)
+    q0, o0, u0, d0 = range(4)
     step = pl.program_id(0)
     tokens = x_ref.shape[1]
+    half = batch // HALVES
 
     @pl.when(step == 0)
     def _():
@@ -1125,7 +1153,7 @@
         own_acc[...] = jnp.zeros_like(own_acc)
         spot.meet()
         adder.start()
-        for t in range(5):
+        for t in range(4):
             fetch.start(t)
         fetch.spread(q0)
         adder.plane()
@@ -1142,11 +1170,9 @@
         copy.start()
         copy.wait()
 
-    when(step == 1, does(fetch.share, o0), does(fetch.spread, d0))
+    when(step == 1, does(fetch.share, o0))
+    when(step == 2, does(fetch.relay, u0), does(fetch.share, u0))
     when(step == 3, does(fetch.close, o0))
-    when(step == 4, does(fetch.relay, u0), does(fetch.finish, o0))
-    when(step == 5, does(fetch.share, u0))
-    when(step == 6, does(fetch.spread, q1))
 
     @pl.when(step < batch)
     def _():
@@ -1161,32 +1187,41 @@
             if part > 0:
                 own_acc[:, (part - 1) * D : part * D] += dot(pick, block)
 
-    @pl.when(step == batch - 1)
-    def _():
-        own_low[...] = (own_acc[...] * (1.0 / SPAN)).astype(BF16)
-        begin(exchange)
-        land[spot.seq] = own_low[...]
-
-    when(step == batch, does(complete, exchange))
-    when(step == batch + 1, does(fetch.close, u0), does(fetch.relay, d0))
-    when(step == batch + 2, does(fetch.share, d0))
-    when(step == batch + 3, does(fetch.finish, u0))
-    when(step == batch + 4, does(fetch.relay, q1))
-    when(step == batch + 5, does(fetch.close, d0), does(fetch.share, q1))
-    when(step == batch + 6, does(fetch.finish, d0))
-    when(step == batch + 7, does(fetch.close, q1))
+    when(step == half - 1, does(send_means, exchange, 0, own_acc))
+    when(step == half, does(fetch.spread, d0))
+    when(step == half + 1, does(fetch.close, u0))
+    when(step == batch - 1, does(send_means, exchange, 1, own_acc))
+
+    @pl.when(step == batch)
+    def _():
+        complete(exchange.spread(0))
+        fetch.finish(o0)
+        fetch.finish(u0)
+
+    when(step == batch + half - 1, does(fetch.relay, d0), does(fetch.share, d0))
+
+    @pl.when(step == batch + half)
+    def _():
+        complete(exchange.spread(1))
+
+    when(step == 2 * batch - 2, does(fetch.close, d0))
+
+    @pl.when(jnp.logical_and(step >= batch, step < batch + half))
+    def _():
+        sums_ref[0] = pick_sums(step - batch, counts, spot.nseq, land_a[...])
+
+    @pl.when(step >= batch + half)
+    def _():
+        sums_ref[0] = pick_sums(step - batch - half, counts, spot.nseq, land_b[...])
 
     @pl.when(step >= batch)
     def _():
-        b = step - batch
-        every = land[...].reshape((-1, land.shape[-1]))
-        sums_ref[0] = dot(row_picker(b, batch, spans, spot.nseq), every).astype(BF16)
-        attention_forward(qkv_all.at[pl.ds(b, 1)], sums_ref, bias_ref, prob_ref, o_ref)
+        attention_forward(qkv_all.at[pl.ds(step - batch, 1)], sums_ref, bias_ref, prob_ref, o_ref)
 
     @pl.when(step == 2 * batch - 1)
     def _():
-        fetch.finish(q1)
-        for t in range(5):
+        fetch.finish(d0)
+        for t in range(4):
             fetch.drain(t)
         adder.drain()
 
@@ -1208,6 +1243,12 @@
 
 def full_shape(weights):
     return sds((lax.axis_size("dp"), lax.axis_size("seq")) + weights.shape[1:], weights.dtype)
+
+
+def exchange_buffers(nseq, rows):
+    own = pltpu.VMEM((rows // HALVES, 2 * D), BF16)
+    land = pltpu.VMEM((nseq, rows // HALVES, 2 * D), BF16)
+    return [own, own, land, land]
 
 
 def call_enter(x, bias, gain_own, wq, wo, wu, wd):
@@ -1218,19 +1259,19 @@
     keys = SPAN + nseq * spans
     outs = [sds((batch, tokens, 3 * D), BF16), sds((batch, nseq * spans, 2 * D), BF16),
             sds((batch, spans, PAIRS, keys, 2 * SPAN), BF16), sds((batch, tokens, D), BF16),
-            sds(gain_own.shape, F32)] + [full_shape(w) for w in (wq, wo, wu, wd, wq)]
+            sds(gain_own.shape, F32)] + [full_shape(w) for w in (wq, wo, wu, wd)]
     return pl.pallas_call(
         functools.partial(enter_kernel, (batch, spans)),
         grid=(2 * batch,),
         in_specs=[phased(x.shape, 0, batch), phased(bias.shape, batch, batch)]
         + [whole(a.shape) for a in (gain_own, wq, wo, wu, wd)],
         out_specs=[phased(outs[0].shape, 0, batch)] + [phased(o.shape, batch, batch) for o in outs[1:4]]
-        + [whole(gain_own.shape)] + [anywhere()] * 5,
+        + [whole(gain_own.shape)] + [anywhere()] * 4,
         out_shape=outs,
-        scratch_shapes=[pltpu.VMEM((batch, tokens, 3 * D), BF16), pltpu.VMEM((rows, 2 * D), F32),
-                        pltpu.VMEM((rows, 2 * D), BF16), pltpu.VMEM((nseq, rows, 2 * D), BF16),
-                        pltpu.VMEM(outs[5].shape, BF16), pltpu.SemaphoreType.DMA, dma(nseq - 1), dma(nseq - 1)]
-        + Fetch.scratch(5, nz) + AllSum.scratch(gain_own.shape, nz),
+        scratch_shapes=[pltpu.VMEM((batch, tokens, 3 * D), BF16), pltpu.VMEM((rows, 2 * D), F32)]
+        + exchange_buffers(nseq, rows)
+        + [pltpu.VMEM(outs[5].shape, BF16), pltpu.SemaphoreType.DMA] + Exchange.sems(nseq)
+        + Fetch.scratch(4, nz) + AllSum.scratch(gain_own.shape, nz),
         compiler_params=fused_params(0),
         name="enter",
     )(x, bias, gain_own, wq, wo, wu, wd)
@@ -1238,13 +1279,13 @@
 
 def mid_kernel(counts, *refs):
     batch, spans = counts
-    (x_ref, o_ref, gains_ref, wo_ref, wu_ref, wd_ref, wq_ref, wo_sh, wu_sh, wd_sh,
-     h_ref, u_ref, next_ref, qkv_ref, raw_ref, fo, fu, fd,
-     own_acc, own_low, land, ex_s, ex_r) = refs[:23]
+    (x_ref, o_ref, gains_ref, wo_ref, wu_ref, wd_ref, wq_sh, wo_sh, wu_sh, wd_sh,
+     h_ref, u_ref, next_ref, qkv_ref, raw_ref, fq, fo, fu, fd,
+     next_all, own_acc, own_a, own_b, land_a, land_b, wq_in, wq_sem, ex_s, ex_r) = refs[:29]
     spot = Spot()
-    fetch = Fetch(spot, [wu_sh.at[1], wd_sh.at[1], wo_sh.at[1]], [fu, fd, fo], refs[23:])
-    exchange = Exchange(spot, ex_s, ex_r).spread(own_low, land)
-    u1, d1, o1 = range(3)
+    fetch = Fetch(spot, [wq_sh.at[1], wu_sh.at[1], wd_sh.at[1], wo_sh.at[1]], [fq, fu, fd, fo], refs[29:])
+    exchange = Exchange(spot, [own_a, own_b], [land_a, land_b], ex_s, ex_r)
+    q1, u1, d1, o1 = range(4)
     step = pl.program_id(0)
 
     @pl.when(step == 0)
@@ -1252,65 +1293,82 @@
         spot.signal()
         own_acc[...] = jnp.zeros_like(own_acc)
 
-    hidden = x_ref[0].astype(F32) + dot(o_ref[0], wo_ref[...])
-    h_ref[0] = hidden
-
-    @pl.when(step == 0)
-    def _():
-        spot.meet()
-        for t in range(3):
-            fetch.start(t)
-
-    when(step == 2, does(fetch.spread, u1))
-    when(step == 3, does(fetch.spread, d1), does(fetch.spread, o1))
-    when(step == 4, does(fetch.relay, u1), does(fetch.share, u1))
-    when(step == 5, does(fetch.relay, d1), does(fetch.share, d1), does(fetch.relay, o1))
-    when(step == 6, does(fetch.close, u1), does(fetch.share, o1))
-    when(step == 7, does(fetch.close, d1), does(fetch.close, o1), does(fetch.finish, u1))
-
-    result = mlp_forward(hidden, gains_ref[2:3], wu_ref, wd_ref, u_ref)
-    next_ref[0] = result
-    unit, _ = normed(result)
-    n_one = (unit * gains_ref[1:2]).astype(BF16)
-    pick = span_adder(step, batch, spans, x_ref.shape[1])
-    for part in range(3):
-        cols = slice(part * D, (part + 1) * D)
-        block = dot(n_one, wq_ref[:, cols]).astype(BF16)
-        qkv_ref[0, :, cols] = block
-        if part > 0:
-            own_acc[:, (part - 1) * D : part * D] += dot(pick, block)
-
-    @pl.when(step == batch - 1)
-    def _():
-        own_low[...] = (own_acc[...] * (1.0 / SPAN)).astype(BF16)
-        begin(exchange)
-        land[spot.seq] = own_low[...]
-        fetch.finish(d1)
+    @pl.when(step < batch)
+    def _():
+        hidden = x_ref[0].astype(F32) + dot(o_ref[0], wo_ref[...])
+        h_ref[0] = hidden
+
+        @pl.when(step == 0)
+        def _():
+            spot.meet()
+            for t in range(4):
+                fetch.start(t)
+
+        when(step == 2, does(fetch.spread, q1))
+        when(step == 4, does(fetch.relay, q1), does(fetch.share, q1), does(fetch.spread, u1))
+        when(step == 5, does(fetch.close, q1))
+        when(step == 6, does(fetch.spread, d1))
+        when(step == 7, does(fetch.relay, u1), does(fetch.share, u1), does(fetch.spread, o1), does(fetch.finish, q1))
+        result = mlp_forward(hidden, gains_ref[2:3], wu_ref, wd_ref, u_ref)
+        next_ref[0] = result
+        next_all[step] = result
+
+    @pl.when(step == batch)
+    def _():
+        copy = pltpu.make_async_copy(fq, wq_in, wq_sem)
+        copy.start()
+        copy.wait()
+
+    when(step == batch + 2, does(fetch.close, u1), does(fetch.relay, d1), does(fetch.share, d1))
+    when(step == batch + 4, does(fetch.relay, o1), does(fetch.share, o1), does(fetch.close, d1))
+    when(step == batch + 6, does(fetch.close, o1), does(fetch.finish, u1))
+    when(step == batch + 7, does(fetch.finish, d1))
+
+    @pl.when(step >= batch)
+    def _():
+        unit, _ = normed(next_all[step - batch])
+        n_one = (unit * gains_ref[1:2]).astype(BF16)
+        pick = span_adder(step - batch, batch, spans, x_ref.shape[1])
+        for part in (1, 2, 0):
+            cols = slice(part * D, (part + 1) * D)
+            block = dot(n_one, whole_weight(wq_in, cols)).astype(BF16)
+            qkv_ref[0, :, cols] = block
+            if part > 0:
+                own_acc[:, (part - 1) * D : part * D] += dot(pick, block)
+
+    when(step == batch + batch // HALVES - 1, does(send_means, exchange, 0, own_acc))
+
+    @pl.when(step == 2 * batch - 1)
+    def _():
+        send_means(exchange, 1, own_acc)
         fetch.finish(o1)
-        complete(exchange)
-        raw_ref[...] = land[...]
-        for t in range(3):
+        for t in range(4):
             fetch.drain(t)
-
-
-def call_mid(x, o, gains, wo, wu, wd, wq_next, wo_sh, wu_sh, wd_sh):
+        complete(exchange.spread(0))
+        raw_ref[0] = land_a[...]
+        complete(exchange.spread(1))
+        raw_ref[1] = land_b[...]
+
+
+def call_mid(x, o, gains, wo, wu, wd, wq_sh, wo_sh, wu_sh, wd_sh):
     batch, tokens, _ = x.shape
     spans = tokens // SPAN
     nz, nseq = lax.axis_size("dp"), lax.axis_size("seq")
     rows = batch * spans
     outs = [sds((batch, tokens, D), F32), sds((batch, tokens, wu.shape[1]), BF16), sds((batch, tokens, D), F32),
-            sds((batch, tokens, 3 * D), BF16), sds((nseq, rows, 2 * D), BF16)]
-    outs += [full_shape(w) for w in (wo_sh, wu_sh, wd_sh)]
-    args = [x, o, gains, wo, wu, wd, wq_next, wo_sh, wu_sh, wd_sh]
+            sds((batch, tokens, 3 * D), BF16), sds((HALVES, nseq, rows // HALVES, 2 * D), BF16)]
+    outs += [full_shape(w) for w in (wq_sh, wo_sh, wu_sh, wd_sh)]
+    args = [x, o, gains, wo, wu, wd, wq_sh, wo_sh, wu_sh, wd_sh]
     return pl.pallas_call(
         functools.partial(mid_kernel, (batch, spans)),
-        grid=(batch,),
-        in_specs=[per_seq(a.shape) for a in args[:2]] + [whole(a.shape) for a in args[2:]],
-        out_specs=[per_seq(a.shape) for a in outs[:4]] + [whole(outs[4].shape)] + [anywhere()] * 3,
+        grid=(2 * batch,),
+        in_specs=[phased(a.shape, 0, batch) for a in args[:2]] + [whole(a.shape) for a in args[2:]],
+        out_specs=[phased(a.shape, 0, batch) for a in outs[:3]] + [phased(outs[3].shape, batch, batch)]
+        + [whole(outs[4].shape)] + [anywhere()] * 4,
         out_shape=outs,
-        scratch_shapes=[pltpu.VMEM((rows, 2 * D), F32), pltpu.VMEM((rows, 2 * D), BF16),
-                        pltpu.VMEM((nseq, rows, 2 * D), BF16), dma(nseq - 1), dma(nseq - 1)]
-        + Fetch.scratch(3, nz),
+        scratch_shapes=[pltpu.VMEM(x.shape, F32), pltpu.VMEM((rows, 2 * D), F32)] + exchange_buffers(nseq, rows)
+        + [pltpu.VMEM(outs[5].shape, BF16), pltpu.SemaphoreType.DMA] + Exchange.sems(nseq)
+        + Fetch.scratch(4, nz),
         compiler_params=fused_params(1),
         name="mid",
     )(*args)
@@ -1319,8 +1377,8 @@
 def top_kernel(counts, x_ref, qkv_ref, bias_ref, raw_ref, gains_ref, wo_ref, wu_ref, wd_ref,
                sums_ref, prob_ref, o_ref, h_ref, u_ref, next_ref):
     batch, spans, nseq = counts
-    every = raw_ref[...].reshape((-1, raw_ref.shape[-1]))
-    sums_ref[0] = dot(row_picker(pl.program_id(0), batch, spans, nseq), every).astype(BF16)
+    b, half = pl.program_id(0), batch // HALVES
+    sums_ref[0] = pick_sums(lax.rem(b, half), (batch, spans), nseq, raw_ref[lax.div(b, half)])
     attention_forward(qkv_ref, sums_ref, bias_ref, prob_ref, o_ref)
     hidden = x_ref[0] + dot(o_ref[0], wo_ref[...])
     h_ref[0] = hidden
@@ -1331,7 +1389,7 @@
 def call_top(x, qkv, bias, raw, gains, wo, wu, wd):
     batch, tokens, _ = x.shape
     spans = tokens // SPAN
-    nseq = raw.shape[0]
+    nseq = raw.shape[1]
     outs = [sds((batch, nseq * spans, 2 * D), BF16),
             sds((batch, spans, PAIRS, SPAN + nseq * spans, 2 * SPAN), BF16), sds((batch, tokens, D), BF16),
             sds((batch, tokens, D), F32), sds((batch, tokens, wu.shape[1]), BF16), sds((batch, tokens, D), BF16)]
@@ -1369,21 +1427,33 @@
     return dot(dattn, wo_ref[...], NT).astype(BF16)
 
 
-def pile(b, batch, spans, nseq, dsums_ref, part_acc):
-    part_acc[...] += dot(row_picker(b, batch, spans, nseq), dsums_ref[0], TN)
-
-
-def ship(spot, part_acc, part_low, copies):
-    part_low[...] = part_acc[...].astype(BF16).reshape(part_low.shape)
-    begin(copies)
-
-
-def gathered(spot, part_low, land, copies):
-    total = part_low[spot.seq].astype(F32)
-    complete(copies)
+def pile(b, counts, nseq, dsums_ref, part_acc):
+    batch, spans = counts
+    local = lax.rem(b, batch // HALVES)
+    part_acc[...] += dot(row_picker(local, batch // HALVES, spans, nseq), dsums_ref[0], TN)
+
+
+def ship(exchange, h, part_acc):
+    source = exchange.sources[h]
+    source[...] = part_acc[...].astype(BF16).reshape(source.shape)
+    part_acc[...] = jnp.zeros_like(part_acc)
+    begin(exchange.collect(h))
+
+
+def gathered(exchange, h, total_ref):
+    spot = exchange.spot
+    complete(exchange.collect(h))
+    total = exchange.sources[h][spot.seq].astype(F32)
     for d in range(spot.nseq - 1):
-        total = total + land[d].astype(F32)
-    return total
+        total = total + exchange.lands[h][d].astype(F32)
+    rows = total.shape[0]
+    total_ref[h * rows : (h + 1) * rows] = total
+
+
+def collect_buffers(nseq, rows):
+    part = pltpu.VMEM((nseq, rows // HALVES, 2 * D), BF16)
+    land = pltpu.VMEM((nseq - 1, rows // HALVES, 2 * D), BF16)
+    return [pltpu.VMEM((nseq * rows // HALVES, 2 * D), F32), part, part, land, land]
 
 
 def zero(*refs):
@@ -1395,9 +1465,9 @@
     batch, spans = counts
     (dy_ref, u_ref, h_ref, o_ref, prob_ref, qkv_ref, sums_ref, gains_ref, wo_ref, wu_ref, wd_ref,
      dh_ref, dqkv_ref, total_ref, gd_out, gu_out, go_out, gg_ref,
-     gd_ref, gu_ref, go_ref, dsums, part_acc, part_low, land, ex_s, ex_r) = refs
+     gd_ref, gu_ref, go_ref, dsums, part_acc, part_a, part_b, land_a, land_b, ex_s, ex_r) = refs
     spot = Spot()
-    exchange = Exchange(spot, ex_s, ex_r).collect(part_low, land)
+    exchange = Exchange(spot, [part_a, part_b], [land_a, land_b], ex_s, ex_r)
     step = pl.program_id(0)
 
     @pl.when(step == 0)
@@ -1408,16 +1478,21 @@
     dout = mlp_back(dy_ref[0].astype(F32), u_ref, h_ref, o_ref, gains_ref[3:4], wo_ref, wu_ref, wd_ref,
                     dh_ref, gd_ref, gu_ref, go_ref, gg_ref)
     attention_backward(qkv_ref, sums_ref, prob_ref, dout, dqkv_ref, dsums)
-    pile(step, batch, spans, spot.nseq, dsums, part_acc)
+    pile(step, counts, spot.nseq, dsums, part_acc)
+
+    @pl.when(step == batch // HALVES - 1)
+    def _():
+        spot.meet()
+        ship(exchange, 0, part_acc)
 
     @pl.when(step == batch - 1)
     def _():
-        spot.meet()
-        ship(spot, part_acc, part_low, exchange)
+        ship(exchange, 1, part_acc)
         gd_out[...] = gd_ref[...].astype(BF16)
         gu_out[...] = gu_ref[...].astype(BF16)
         go_out[...] = go_ref[...].astype(BF16)
-        total_ref[...] = gathered(spot, part_low, land, exchange)
+        gathered(exchange, 0, total_ref)
+        gathered(exchange, 1, total_ref)
 
 
 def call_base(dy, u, h, o, prob, qkv, sums, gains, wo, wu, wd):
@@ -1435,16 +1510,14 @@
         out_specs=[per_seq(a.shape) for a in outs[:2]] + [whole(a.shape) for a in outs[2:]],
         out_shape=outs,
         scratch_shapes=[pltpu.VMEM(wd.shape, F32), pltpu.VMEM(wu.shape, F32), pltpu.VMEM(wo.shape, F32),
-                        pltpu.VMEM((1, nseq * spans, 2 * D), BF16), pltpu.VMEM((nseq * rows, 2 * D), F32),
-                        pltpu.VMEM((nseq, rows, 2 * D), BF16), pltpu.VMEM((nseq - 1, rows, 2 * D), BF16),
-                        dma(nseq - 1), dma(nseq - 1)],
+                        pltpu.VMEM((1, nseq * spans, 2 * D), BF16)]
+        + collect_buffers(nseq, rows) + Exchange.sems(nseq),
         compiler_params=fused_params(2),
         name="base",
     )(*args)
 
 
-def qkv_back(x32, gain, near, share, dh, weight, gq_ref, gg_ref):
-    unit, rstd = normed(x32)
+def qkv_back(unit, rstd, gain, near, share, dh, weight, gq, gg_ref, skip=()):
     n_one = (unit * gain).astype(BF16)
     dn_one = 0.0
     for part in range(3):
@@ -1452,11 +1525,12 @@
         block = near(cols)
         if part > 0:
             pieces = []
-            for span in range(x32.shape[0] // SPAN):
+            for span in range(unit.shape[0] // SPAN):
                 row = share(span, slice((part - 1) * D, part * D)) * (1.0 / SPAN)
                 pieces.append(block[span * SPAN : (span + 1) * SPAN].astype(F32) + row)
             block = jnp.concatenate(pieces, 0).astype(BF16)
-        gq_ref[:, cols] += dot(n_one, block, TN)
+        if part not in skip:
+            gq[part][...] += dot(n_one, block, TN)
         dn_one = dn_one + dot(block, weight(cols), NT)
     dnorm, grad_gain = norm_backward(dn_one, unit, rstd, gain)
     gg_ref[...] += grad_gain
@@ -1479,34 +1553,36 @@
     def _():
         spot.signal()
         zero(gq_ref, gd_ref, gu_ref, go_ref, gg_ref, ggq_ref)
+
+    @pl.when(step == 1)
+    def _():
         spot.meet()
         for t in range(3):
             fold.start(t)
 
-    when(step == 2, does(fold.combine, d1))
-    when(step == 3, does(fold.combine, u1))
-    when(step == 4, does(fold.combine, o1))
-    when(step == 6, does(fold.middle, d1))
+    when(step == 3, does(fold.combine, d1))
+    when(step == 4, does(fold.combine, u1))
+    when(step == 5, does(fold.combine, o1))
+    when(step == 7, does(fold.middle, d1))
 
     @pl.when(step == batch)
     def _():
         gq_low[...] = gq_ref[...].astype(BF16).reshape(gq_low.shape)
         fold.start(q1)
-        fold.middle(u1)
-
-    when(step == batch + 1, does(fold.middle, o1), does(fold.column, d1), does(fold.combine, q1))
-    when(step == batch + 2, does(fold.column, u1), does(fold.column, o1))
-    when(step == batch + 3, does(fold.middle, q1), does(fold.finish, d1))
-    when(step == batch + 4, does(fold.finish, u1), does(fold.finish, o1))
-    when(step == batch + 5, does(fold.column, q1))
+
+    when(step == batch + 1, does(fold.middle, u1), does(fold.middle, o1), does(fold.combine, q1))
+    when(step == batch + 2, does(fold.column, d1), does(fold.column, u1), does(fold.column, o1))
+    when(step == batch + 4, does(fold.middle, q1))
+    when(step == batch + 5, does(fold.finish, d1), does(fold.finish, u1), does(fold.finish, o1), does(fold.column, q1))
     when(step == batch + 7, does(fold.finish, q1))
 
     @pl.when(step < batch)
     def _():
+        unit, rstd = normed(x_ref[0])
         dx_all[step] = qkv_back(
-            x_ref[0], gains_ref[1:2], lambda cols: near_ref[0, :, cols],
+            unit, rstd, gains_ref[1:2], lambda cols: near_ref[0, :, cols],
             lambda span, cols: total_ref[pl.ds(step * spans + span, 1), cols], dh_ref[0],
-            lambda cols: wq_ref[:, cols], gq_ref, ggq_ref)
+            lambda cols: wq_ref[:, cols], [gq_ref.at[:, part * D : (part + 1) * D] for part in range(3)], ggq_ref)
 
     @pl.when(step >= batch)
     def _():
@@ -1565,73 +1641,97 @@
     batch, spans = counts
     (prob_ref, qkv_ref, sums_ref, dout_ref, x_ref, dh_ref, gains_ref, wq_ref, g_mlp0, g_attn1, g_mlp1,
      pd, pu, po,
-     dx_ref, gsum_ref, sd, su, so, sq,
-     near_all, gq_ref, gq_low, gg_ref, gain_src, dsums, part_acc, part_low, land, total, ex_s, ex_r) = refs[:32]
-    rest = refs[32:]
+     dx_ref, gsum_ref, sd, su, so, s0, s1, s2,
+     near_all, unit_all, rstd_all, a0, a1, a2, l0, l1, l2, gg_ref, gain_src, dsums,
+     part_acc, part_a, part_b, land_a, land_b, total, ex_s, ex_r) = refs[:42]
+    rest = refs[42:]
     spot = Spot()
-    fold = Fold(spot, [pd, pu, po, gq_low], [sd, su, so, sq], rest[:24], rest[24:31])
-    adder = AllSum(spot, gain_src, rest[31:])
-    exchange = Exchange(spot, ex_s, ex_r).collect(part_low, land)
-    d0, u0, o0, q0 = range(4)
+    fold = Fold(spot, [pd, pu, po, l0, l1, l2], [sd, su, so, s0, s1, s2], rest[:36], rest[36:43])
+    adder = AllSum(spot, gain_src, rest[43:])
+    exchange = Exchange(spot, [part_a, part_b], [land_a, land_b], ex_s, ex_r)
+    d0, u0, o0, q0, k0, v0 = range(6)
     step = pl.program_id(0)
+    half = batch // HALVES
+
+    def pour(acc, low):
+        low[...] = acc[...].astype(BF16).reshape(low.shape)
 
     @pl.when(step == 0)
     def _():
         spot.signal()
-        zero(gq_ref, gg_ref, part_acc)
+        zero(a0, a1, a2, gg_ref, part_acc)
+
+    @pl.when(step == 1)
+    def _():
         spot.meet()
         for t in range(3):
             fold.start(t)
 
     when(step == 2, does(fold.combine, d0))
-    when(step == 3, does(fold.combine, u0))
-    when(step == 4, does(fold.combine, o0))
-    when(step == 6, does(fold.middle, d0))
+    when(step == half + 1, does(fold.middle, d0), does(fold.combine, u0), does(fold.combine, o0))
+    when(step == batch - 1, does(fold.column, d0))
 
     @pl.when(step == batch)
     def _():
-        total[...] = gathered(spot, part_low, land, exchange)
-        fold.middle(u0)
-        fold.middle(o0)
-
-    when(step == batch + 1, does(fold.column, d0))
-    when(step == batch + 3, does(fold.column, u0), does(fold.column, o0))
-    when(step == batch + 5, does(fold.finish, d0))
-    when(step == batch + 6, does(fold.finish, u0), does(fold.finish, o0))
+        pour(a0, l0)
+        fold.start(q0)
+        gathered(exchange, 0, total)
+
+    when(step == batch + 2, does(fold.middle, u0), does(fold.combine, q0))
+    when(step == batch + 3, does(fold.middle, o0))
+    when(step == batch + half, does(gathered, exchange, 1, total))
+    when(step == batch + 5, does(fold.column, u0))
+    when(step == batch + 6, does(fold.column, o0), does(fold.middle, q0))
+    when(step == batch + 7, does(fold.finish, d0), does(fold.column, q0))
 
     @pl.when(step < batch)
     def _():
-        attention_backward(qkv_ref, sums_ref, prob_ref, dout_ref[0], near_all.at[pl.ds(step, 1)], dsums)
-        pile(step, batch, spans, spot.nseq, dsums, part_acc)
-
-    when(step == batch - 1, does(ship, spot, part_acc, part_low, exchange))
+        near = near_all.at[pl.ds(step, 1)]
+        attention_backward(qkv_ref, sums_ref, prob_ref, dout_ref[0], near, dsums)
+        pile(step, counts, spot.nseq, dsums, part_acc)
+        unit, rstd = normed(x_ref[0].astype(F32))
+        unit_all[step] = unit
+        rstd_all[step] = rstd
+        a0[...] += dot((unit * gains_ref[0:1]).astype(BF16), near_all[step, :, :D], TN)
+
+    when(step == half - 1, does(ship, exchange, 0, part_acc))
+    when(step == batch - 1, does(ship, exchange, 1, part_acc))
 
     @pl.when(step >= batch)
     def _():
         b = step - batch
         dx_ref[0] = qkv_back(
-            x_ref[0].astype(F32), gains_ref[0:1], lambda cols: near_all[b, :, cols],
+            unit_all[b], rstd_all[b], gains_ref[0:1], lambda cols: near_all[b, :, cols],
             lambda span, cols: total[pl.ds(b * spans + span, 1), cols], dh_ref[0],
-            lambda cols: wq_ref[:, cols], gq_ref, gg_ref)
+            lambda cols: wq_ref[:, cols], [a0, a1, a2], gg_ref, (0,))
 
     @pl.when(step == 2 * batch - 1)
     def _():
-        gq_low[...] = gq_ref[...].astype(BF16).reshape(gq_low.shape)
-        fold.start(q0)
+        pour(a1, l1)
+        fold.start(k0)
+        pour(a2, l2)
+        fold.start(v0)
         gain_src[...] = jnp.zeros_like(gain_src)
         gain_src[0:1] = gg_ref[...]
         gain_src[1:2] = g_attn1[...]
         gain_src[2:3] = g_mlp0[...]
         gain_src[3:4] = g_mlp1[...]
         adder.start()
-        fold.combine(q0)
+        fold.combine(k0)
+        fold.combine(v0)
         adder.plane()
-        fold.middle(q0)
+        fold.finish(u0)
+        fold.finish(o0)
+        fold.middle(k0)
+        fold.middle(v0)
         adder.column()
-        fold.column(q0)
+        fold.column(k0)
+        fold.column(v0)
+        fold.finish(q0)
         gsum_ref[...] = adder.total()
-        fold.finish(q0)
-        for t in range(4):
+        fold.finish(k0)
+        fold.finish(v0)
+        for t in range(6):
             fold.drain(t)
         adder.drain()
 
@@ -1642,43 +1742,48 @@
     nz, nseq = lax.axis_size("dp"), lax.axis_size("seq")
     rows = batch * spans
     parts = [by_owner(a) for a in (pd, pu, po)]
-    owned = by_owner(sds_like(wq))
-    shapes = [a.shape[3:] for a in parts] + [owned.shape[3:]]
+    square = (D, D)
+    owned = (nz, nseq // CORES, CORES, D // (nz * nseq), D)
+    shapes = [a.shape[3:] for a in parts] + [owned[3:]] * 3
     args = [prob, qkv, sums, dout, x, dh, gains, wq, g_mlp0, g_attn1, g_mlp1] + parts
     outs = [sds(dh.shape, F32), sds(gains.shape, F32)] + [sds(s, F32) for s in shapes]
     return pl.pallas_call(
         functools.partial(leave_kernel, (batch, spans)),
         grid=(2 * batch,),
-        in_specs=[phased(a.shape, 0, batch) for a in args[:4]] + [phased(a.shape, batch, batch) for a in args[4:6]]
+        in_specs=[phased(a.shape, 0, batch) for a in args[:5]] + [phased(dh.shape, batch, batch)]
         + [whole(a.shape) for a in args[6:11]] + [anywhere()] * 3,
         out_specs=[phased(outs[0].shape, batch, batch)] + [whole(a.shape) for a in outs[1:]],
         out_shape=outs,
-        scratch_shapes=[pltpu.VMEM(qkv.shape, BF16), pltpu.VMEM(wq.shape, F32), pltpu.VMEM(owned.shape, BF16),
-                        pltpu.VMEM((1, D), F32), pltpu.VMEM(gains.shape, F32),
-                        pltpu.VMEM((1, nseq * spans, 2 * D), BF16), pltpu.VMEM((nseq * rows, 2 * D), F32),
-                        pltpu.VMEM((nseq, rows, 2 * D), BF16), pltpu.VMEM((nseq - 1, rows, 2 * D), BF16),
-                        pltpu.VMEM((rows, 2 * D), F32), dma(nseq - 1), dma(nseq - 1)]
-        + Fold.buffers(shapes, nz) + Fold.sems(4, nz) + AllSum.scratch(gains.shape, nz),
+        scratch_shapes=[pltpu.VMEM(qkv.shape, BF16), pltpu.VMEM(x.shape, F32), pltpu.VMEM((batch, tokens, 1), F32)]
+        + [pltpu.VMEM(square, F32)] * 3 + [pltpu.VMEM(owned, BF16)] * 3
+        + [pltpu.VMEM((1, D), F32), pltpu.VMEM(gains.shape, F32), pltpu.VMEM((1, nseq * spans, 2 * D), BF16)]
+        + collect_buffers(nseq, rows) + [pltpu.VMEM((rows, 2 * D), F32)] + Exchange.sems(nseq)
+        + Fold.buffers(shapes, nz) + Fold.sems(6, nz) + AllSum.scratch(gains.shape, nz),
         compiler_params=fused_params(4),
         name="leave",
     )(*args)
 
 
-def pack_kernel(count, *refs):
-    ins, outs = refs[: 2 * count], refs[2 * count :]
-    for m in range(count):
-        for l in range(2):
-            outs[m][l] = ins[2 * m + l][...]
-
-
-def call_pack(pairs):
-    flat = [a for pair in pairs for a in pair]
-    outs = [sds((2,) + pair[0].shape, F32) for pair in pairs]
+def pack_kernel(plan, *refs):
+    ins, outs = refs[: -len(plan)], refs[-len(plan) :]
+    at = 0
+    for out, layers in zip(outs, plan):
+        for l, pieces in enumerate(layers):
+            start = 0
+            for width in pieces:
+                out[l, :, start : start + width] = ins[at][...]
+                at, start = at + 1, start + width
+
+
+def call_pack(tensors):
+    flat = [a for layers in tensors for pieces in layers for a in pieces]
+    plan = [[[a.shape[1] for a in pieces] for pieces in layers] for layers in tensors]
+    outs = [sds((len(layers), layers[0][0].shape[0], sum(a.shape[1] for a in layers[0])), F32) for layers in tensors]
     vmem = pl.BlockSpec(memory_space=pltpu.VMEM)
     return pl.pallas_call(
-        functools.partial(pack_kernel, len(pairs)),
+        functools.partial(pack_kernel, plan),
         in_specs=[vmem] * len(flat),
-        out_specs=[vmem] * len(pairs),
+        out_specs=[vmem] * len(tensors),
         out_shape=outs,
         name="pack",
     )(*flat)
@@ -1696,20 +1801,20 @@
     def flat(a):
         return a.reshape((-1, a.shape[-1]))
 
-    qkv0, sums0, prob0, o0, gains, wq0, wo0, wu0, wd0, wq1 = call_enter(
+    qkv0, sums0, prob0, o0, gains, wq0, wo0, wu0, wd0 = call_enter(
         inputs, bias, gain_own, w_qkv, w_out, w_up, w_down)
-    wq0, wo0, wu0, wd0, wq1 = (flat(a) for a in (wq0, wo0, wu0, wd0, wq1))
-    h0, u0, x1, qkv1, raw1, wo1, wu1, wd1 = call_mid(
-        inputs, o0, gains, wo0, wu0, wd0, wq1, w_out, w_up, w_down)
-    wo1, wu1, wd1 = flat(wo1), flat(wu1), flat(wd1)
+    wq0, wo0, wu0, wd0 = (flat(a) for a in (wq0, wo0, wu0, wd0))
+    h0, u0, x1, qkv1, raw1, wq1, wo1, wu1, wd1 = call_mid(
+        inputs, o0, gains, wo0, wu0, wd0, w_qkv, w_out, w_up, w_down)
+    wq1, wo1, wu1, wd1 = (flat(a) for a in (wq1, wo1, wu1, wd1))
     sums1, prob1, o1, h1, u1, outputs = call_top(x1, qkv1, bias, raw1, gains, wo1, wu1, wd1)
     dh1, near1, total1, gd1, gu1, go1, g_mlp1 = call_base(
         cotangent, u1, h1, o1, prob1, qkv1, sums1, gains, wo1, wu1, wd1)
     dh0, dout0, gd0, gu0, go0, g_attn1, g_mlp0, sd1, su1, so1, sq1 = call_turn(
         x1, near1, dh1, u0, h0, o0, total1, gains, wq1, wo0, wu0, wd0, gd1, gu1, go1)
-    dx, gsum, sd0, su0, so0, sq0 = call_leave(
+    dx, gsum, sd0, su0, so0, *sq0 = call_leave(
         prob0, qkv0, sums0, dout0, inputs, dh0, gains, wq0, g_mlp0, g_attn1, g_mlp1, gd0, gu0, go0)
-    gq, go, gu, gd = call_pack([(sq0, sq1), (so0, so1), (su0, su1), (sd0, sd1)])
+    gq, go, gu, gd = call_pack([[sq0, [sq1]], [[so0], [so1]], [[su0], [su1]], [[sd0], [sd1]]])
     gain_share = lax.dynamic_slice(gsum, (0, rank * slots), (4, slots))
     return outputs, dx, gq, go, gu, gd, gain_share[:2], gain_share[2:]
 

time: 367 us -> 323 us (0.88)
  Pallas kernels: 355 us -> 311 us
    pallas_call x1, Pallas kernels: 71.1 us -> 53.4 us  [call_leave(): pl.pallas_call(functools.partial(leave_kernel, (batch, spans)), grid=(2 *...]
    pallas_call x1, Pallas kernels: 64.6 us -> 50.5 us  [call_base(): pl.pallas_call(functools.partial(base_kernel, (batch, spans)), grid=(batc...]
    pallas_call x1, Pallas kernels: 71.9 us -> 58.1 us  [call_enter(): pl.pallas_call(functools.partial(enter_kernel, (batch, spans)), grid=(2 *...]
    pallas_call x2, Pallas kernels: 47 us -> 54.5 us  [the longest x1 52.4 us: call_mid(): pl.pallas_call(functools.partial(mid_kernel, (batch, spans)), grid=(2 * b...]
    pallas_call x1, Pallas kernels: 35.8 us -> 29.4 us  [call_top(): pl.pallas_call(functools.partial(top_kernel, (batch, spans, nseq)), grid=...]
where the time goes in v4:
time: 323 us; the launch traced here: 322 us
  Pallas kernels  311 us (96%)
  local copies, waits for them, and re-layouts  8.08 us (3%)
    pallas_call x1, Pallas kernels, call_turn(): pl.pallas_call(functools.partial(turn_kernel, (batch, tokens // SPAN)), g...  65.3 us
    pallas_call x1, Pallas kernels, call_enter(): pl.pallas_call(functools.partial(enter_kernel, (batch, spans)), grid=(2 *...  58.1 us
    pallas_call x1, Pallas kernels, call_leave(): pl.pallas_call(functools.partial(leave_kernel, (batch, spans)), grid=(2 *...  53.4 us
    pallas_call x1, Pallas kernels, call_mid(): pl.pallas_call(functools.partial(mid_kernel, (batch, spans)), grid=(2 * b...  52.4 us
    pallas_call x1, Pallas kernels, call_base(): pl.pallas_call(functools.partial(base_kernel, (batch, spans)), grid=(batc...  50.5 us
    pallas_call x1, Pallas kernels, call_top(): pl.pallas_call(functools.partial(top_kernel, (batch, spans, nseq)), grid=...  29.4 us

profile of v4, /device:TPU:0, one launch (start us, length us, event | category | flops | bytes accessed | tf_op | source)
XLA Modules:
  0.0 322.4 jit_solution(13208405101801187897)
XLA Ops:
  0.7 0.1 iota_compare_fusion.2
  0.7 0.7 fusion.3
  1.4 0.7 constant_dynamic-slice_fusion.1
  2.1 0.2 dynamic_update_slice.3.refs_2_
  2.4 0.0 copy-start
  2.4 0.9 copy.19
  3.3 0.3 slice_reduce_fusion
  3.6 0.1 compare_and_fusion.1
  3.7 0.3 compare_and_fusion
  4.0 1.2 add_select_fusion.refs_1_.bias_ref
  5.2 0.0 copy-done
  5.2 58.1 %enter.1 = (bf16[8,256,1536]{2,1,0:T(8,128)(2,1)}, bf16[8,16,1024]{2,1,0:T(8,128)(2,1)}, bf16[8,2,4,144,256]{4,3,2,1,0:T(8,128)(2,1)}, bf16[8,256,512]{2,1,0:T(8...) custom-call(bf16[8,256,512]{2,1,0:T(8,128)(2,1)} %refs_4_.3, ...), custom_call_target="tpu_custom_call" | custom-call | tf_op jit(solution)/shard_map/enter/pallas_call | solution.py:1263
  63.3 52.4 %mid.1 = (f32[8,256,512]{2,1,0:T(8,128)}, bf16[8,256,2048]{2,1,0:T(8,128)(2,1)}, f32[8,256,512]{2,1,0:T(8,128)}, bf16[8,256,1536]{2,1,0:T(8,128)(2,1)}, bf16[2,8...) custom-call(bf16[8,256,512]{2,1,0:T(8,128)(2,1)} %refs_4_.3, ...), custom_call_target="tpu_custom_call" | custom-call | tf_op jit(solution)/shard_map/mid/pallas_call | solution.py:1362
  115.8 29.4 %top.1 = (bf16[8,16,1024]{2,1,0:T(8,128)(2,1)}, bf16[8,2,4,144,256]{4,3,2,1,0:T(8,128)(2,1)}, bf16[8,256,512]{2,1,0:T(8,128)(2,1)}, f32[8,256,512]{2,1,0:T(8,128...) custom-call(f32[8,256,512]{2,1,0:T(8,128)} %get-tuple-element.67.x_ref.refs_0_, ...), custom_call_target="tpu_custom_call" | custom-call | tf_op jit(solution)/shard_map/top/pallas_call | solution.py:1397
  145.2 50.5 %base.1 = (f32[8,256,512]{2,1,0:T(8,128)}, bf16[8,256,1536]{2,1,0:T(8,128)(2,1)}, f32[16,1024]{1,0:T(8,128)}, bf16[2048,512]{1,0:T(8,128)(2,1)}, bf16[512,2048]{...) custom-call(bf16[8,256,512]{2,1,0:T(8,128)(2,1)} %refs_0_.5, ...), custom_call_target="tpu_custom_call" | custom-call | tf_op jit(solution)/shard_map/base/pallas_call | solution.py:1506
  195.7 65.3 %turn.1 = (f32[8,256,512]{2,1,0:T(8,128)}, bf16[8,256,512]{2,1,0:T(8,128)(2,1)}, bf16[2048,512]{1,0:T(8,128)(2,1)}, bf16[512,2048]{1,0:T(8,128)(2,1)}, bf16[512,...) custom-call(f32[8,256,512]{2,1,0:T(8,128)} %get-tuple-element.67.x_r, ...), custom_call_target="tpu_custom_call" | custom-call | tf_op jit(solution)/shard_map/turn/pallas_call | solution.py:1615
  261.0 53.4 %leave.1 = (f32[8,256,512]{2,1,0:T(8,128)}, f32[8,512]{1,0:T(8,128)}, f32[64,512]{1,0:T(8,128)}, f32[16,2048]{1,0:T(8,128)}, f32[16,512]{1,0:T(8,128)}, /*index=...) custom-call(bf16[8,2,4,144,256]{4,3,2,1,0:T(8,128)(2,1)} %get-tuple-element.74.refs_0_, ...), custom_call_target="tpu_custom_call" | custom-call | tf_op jit(solution)/shard_map/leave/pallas_call | solution.py:1750
  314.3 0.8 constant_dynamic-slice_fusion
  315.1 0.6 fusion.4
  315.7 2.1 pack.1
  317.8 4.6 %copy.22 = f32[8,256,512]{2,1,0:T(8,128)} copy(f32[8,256,512]{2,1,0:T(8,128)} %get-tuple-element.127) | data formatting | bytes 8388608
  (4 shorter events, 0.0 us)
Async XLA Ops:
  2.4 2.9 copy-start

commit v5 on v4

--- a/solution.py
+++ b/solution.py
@@ -173,7 +173,7 @@
     total = h32
     for start in range(0, wu_ref.shape[1], CHUNK):
         upper = dot(n_two, wu_ref[:, start : start + CHUNK])
-        u_ref[0, :, start : start + CHUNK] = upper.astype(BF16)
+        u_ref[:, :, start : start + CHUNK] = upper.astype(BF16).reshape((u_ref.shape[0], -1, CHUNK))
         total = total + dot(gelu(upper).astype(BF16), wd_ref[start : start + CHUNK, :])
     return total
 
@@ -815,56 +815,74 @@
     return pltpu.SemaphoreType.DMA(shape)
 
 
-class Fetch:
-    def __init__(self, spot, shards, fulls, sems):
-        self.spot, self.shards, self.fulls = spot, shards, fulls
-        self.own, self.zs, self.zr, self.hs, self.hr, self.cs, self.cr = sems
+class Lines:
+    def __init__(self, spot, shards, cols, sems):
+        self.spot, self.shards, self.cols = spot, shards, cols
+        self.own, self.ss, self.rs = sems
 
     @staticmethod
-    def scratch(count, nz):
-        return [dma(count), dma(count, nz - 1), dma(count, nz - 1), dma(count, 3), dma(count, 3),
-                dma(count, 4), dma(count, 4)]
+    def sems(count, nz):
+        return [dma(count), dma(count, nz - 1), dma(count, nz - 1)]
 
     def local(self, t):
-        return pltpu.make_async_copy(
-            self.shards[t], self.fulls[t].at[self.spot.z, self.spot.seq], self.own.at[t])
+        return pltpu.make_async_copy(self.shards[t], self.cols[t].at[self.spot.z], self.own.at[t])
 
     def line(self, t, d):
-        return remote(self.shards[t], self.fulls[t].at[self.spot.z, self.spot.seq], self.zs.at[t, d - 1],
-                      self.zr.at[t, d - 1], self.spot.on_line(d))
-
-    def hop(self, t, k):
-        spot = self.spot
-        chip = (spot.chip, spot.chip, spot.first)[k]
-        target = (spot.first, spot.second, spot.second)[k]
-        block = self.fulls[t].at[:, chip * CORES + spot.core]
-        return remote(block, block, self.hs.at[t, k], self.hr.at[t, k], spot.at_chip(target))
-
-    def cross(self, t, k):
-        spot = self.spot
-        chip = (spot.chip, spot.first, spot.second, spot.diagonal)[k]
-        block = self.fulls[t].at[:, chip * CORES + spot.core]
-        return remote(block, block, self.cs.at[t, k], self.cr.at[t, k], spot.twin())
+        return remote(self.shards[t], self.cols[t].at[self.spot.z], self.ss.at[t, d - 1], self.rs.at[t, d - 1],
+                      self.spot.on_line(d))
 
     def start(self, t):
         self.local(t).start()
         for d in range(1, self.spot.nz):
             self.line(t, d).start()
 
-    def spread(self, t):
+    def arrive(self, t):
         self.local(t).wait()
         for d in range(1, self.spot.nz):
             self.line(t, d).wait_recv()
+
+    def drain(self, t):
+        for d in range(1, self.spot.nz):
+            self.line(t, d).wait_send()
+
+
+class Plane:
+    def __init__(self, spot, cols, fulls, sems):
+        self.spot, self.cols, self.fulls = spot, cols, fulls
+        self.own, self.hs, self.hr, self.cs, self.cr = sems
+
+    @staticmethod
+    def sems(count):
+        return [dma(count), dma(count, 3), dma(count, 3), dma(count, 4), dma(count, 4)]
+
+    def block(self, t, chip):
+        return self.fulls[t].at[:, chip * CORES + self.spot.core]
+
+    def local(self, t):
+        return pltpu.make_async_copy(self.cols[t], self.block(t, self.spot.chip), self.own.at[t])
+
+    def hop(self, t, k):
+        spot = self.spot
+        target = (spot.first, spot.second, spot.second)[k]
+        source = self.cols[t] if k < 2 else self.block(t, spot.first)
+        land = self.block(t, (spot.chip, spot.chip, spot.first)[k])
+        return remote(source, land, self.hs.at[t, k], self.hr.at[t, k], spot.at_chip(target))
+
+    def cross(self, t, k):
+        spot = self.spot
+        land = self.block(t, (spot.chip, spot.first, spot.second, spot.diagonal)[k])
+        return remote(land if k else self.cols[t], land, self.cs.at[t, k], self.cr.at[t, k], spot.twin())
+
+    def spread(self, t):
         self.hop(t, 0).start()
         self.hop(t, 1).start()
         self.cross(t, 0).start()
+        self.local(t).start()
 
     def relay(self, t):
         self.hop(t, 0).wait_recv()
         self.hop(t, 2).start()
         self.cross(t, 1).start()
-
-    def share(self, t):
         self.hop(t, 1).wait_recv()
         self.cross(t, 2).start()
 
@@ -873,12 +891,11 @@
         self.cross(t, 3).start()
 
     def finish(self, t):
+        self.local(t).wait()
         for k in range(4):
             self.cross(t, k).wait_recv()
 
     def drain(self, t):
-        for d in range(1, self.spot.nz):
-            self.line(t, d).wait_send()
         for k in range(3):
             self.hop(t, k).wait_send()
         for k in range(4):
@@ -995,48 +1012,48 @@
 class AllSum:
     def __init__(self, spot, source, bufs):
         self.spot, self.source = spot, source
-        self.twin_in, self.pair, self.plane_in, self.col, self.line_in, self.ss, self.rs = bufs
+        self.line_in, self.col, self.plane_in, self.pair, self.twin_in, self.ss, self.rs = bufs
 
     @staticmethod
     def scratch(shape, nz):
-        return [pltpu.VMEM(shape, F32), pltpu.VMEM(shape, F32), pltpu.VMEM((3,) + shape, F32),
-                pltpu.VMEM(shape, F32), pltpu.VMEM((nz - 1,) + shape, F32), dma(3 + nz), dma(3 + nz)]
+        return [pltpu.VMEM((nz - 1,) + shape, F32), pltpu.VMEM(shape, F32), pltpu.VMEM((3,) + shape, F32),
+                pltpu.VMEM(shape, F32), pltpu.VMEM(shape, F32), dma(3 + nz), dma(3 + nz)]
 
     def cross(self):
-        return remote(self.source, self.twin_in, self.ss.at[0], self.rs.at[0], self.spot.twin())
+        return remote(self.pair, self.twin_in, self.ss.at[0], self.rs.at[0], self.spot.twin())
 
     def hop(self, k):
         chip = (self.spot.first, self.spot.second, self.spot.diagonal)[k]
-        return remote(self.pair, self.plane_in.at[k], self.ss.at[1 + k], self.rs.at[1 + k],
+        return remote(self.col, self.plane_in.at[k], self.ss.at[1 + k], self.rs.at[1 + k],
                       self.spot.at_chip(chip))
 
     def line(self, d):
-        return remote(self.col, self.line_in.at[d - 1], self.ss.at[3 + d], self.rs.at[3 + d],
+        return remote(self.source, self.line_in.at[d - 1], self.ss.at[3 + d], self.rs.at[3 + d],
                       self.spot.on_line(d))
 
     def start(self):
-        self.cross().start()
-
-    def plane(self):
-        self.cross().wait_recv()
-        self.pair[...] = self.source[...] + self.twin_in[...]
-        for k in range(3):
-            self.hop(k).start()
-
-    def column(self):
-        for k in range(3):
-            self.hop(k).wait_recv()
-        self.col[...] = self.pair[...] + self.plane_in[0] + self.plane_in[1] + self.plane_in[2]
         for d in range(1, self.spot.nz):
             self.line(d).start()
 
-    def total(self):
-        out = self.col[...]
+    def plane(self):
+        out = self.source[...]
         for d in range(1, self.spot.nz):
             self.line(d).wait_recv()
         for d in range(self.spot.nz - 1):
             out = out + self.line_in[d]
-        return out
+        self.col[...] = out
+        for k in range(3):
+            self.hop(k).start()
+
+    def column(self):
+        for k in range(3):
+            self.hop(k).wait_recv()
+        self.pair[...] = self.col[...] + self.plane_in[0] + self.plane_in[1] + self.plane_in[2]
+        self.cross().start()
+
+    def total(self):
+        self.cross().wait_recv()
+        return self.pair[...] + self.twin_in[...]
 
     def drain(self):
         self.cross().wait_send()
@@ -1132,20 +1149,49 @@
     return dot(row_picker(b, batch // HALVES, spans, nseq), every).astype(BF16)
 
 
+QKV_ORDER = (1, 2, 0)
+PARTS = len(QKV_ORDER)
+U_CUTS = 2
+
+
 def enter_kernel(counts, *refs):
     batch, spans = counts
     (x_ref, bias_ref, gain_own, wq_sh, wo_sh, wu_sh, wd_sh,
-     qkv_ref, sums_ref, prob_ref, o_ref, gains_ref, fq, fo, fu, fd,
-     qkv_all, own_acc, own_a, own_b, land_a, land_b, wq_in, wq_sem, ex_s, ex_r) = refs[:26]
-    rest = refs[26:]
+     qkv_ref, sums_ref, prob_ref, o_ref, gains_ref, fk, fv, fq, fo, fu, fd, cq, cu, cd, co,
+     n_all, qkv_all, own_acc, own_a, own_b, land_a, land_b, ik, iv, iq, out_sem, qkv_sem, ex_s, ex_r) = refs[:36]
+    rest = refs[36:]
     spot = Spot()
-    fetch = Fetch(spot, [wq_sh.at[0], wo_sh.at[0], wu_sh.at[0], wd_sh.at[0]], [fq, fo, fu, fd], rest[:7])
-    adder = AllSum(spot, gain_own, rest[7:])
+    wide = wu_sh.shape[-1] // U_CUTS
+    cuts = [slice(i * wide, (i + 1) * wide) for i in range(U_CUTS)]
+    shards = [wq_sh.at[0, :, part * D : (part + 1) * D] for part in QKV_ORDER]
+    shards += [wo_sh.at[0]] + [wu_sh.at[0, :, cols] for cols in cuts] + [wd_sh.at[0]]
+    cols = list(rest[:7])
+    lines = Lines(spot, shards + [wq_sh.at[1], wu_sh.at[1], wd_sh.at[1], wo_sh.at[1]], cols + [cq, cu, cd, co],
+                  rest[7:10])
+    plane = Plane(spot, cols, [ik, iv, iq, fo] + [fu.at[:, :, :, c] for c in cuts] + [fd], rest[10:15])
+    adder = AllSum(spot, gain_own, rest[15:])
     exchange = Exchange(spot, [own_a, own_b], [land_a, land_b], ex_s, ex_r)
-    q0, o0, u0, d0 = range(4)
+    k0, v0, q0, o0, ua, ub, d0 = range(7)
+    inner, outer = (ik, iv, iq), (fk, fv, fq)
     step = pl.program_id(0)
     tokens = x_ref.shape[1]
     half = batch // HALVES
+    first = PARTS + 1
+
+    def keep(t):
+        return pltpu.make_async_copy(inner[t], outer[t], out_sem.at[t])
+
+    def record(b):
+        return pltpu.make_async_copy(qkv_all.at[b], qkv_ref.at[b], qkv_sem.at[b])
+
+    def spread(t):
+        lines.arrive(t)
+        plane.spread(t)
+
+    def settle(t):
+        plane.close(t)
+        plane.finish(t)
+        keep(t).start()
 
     @pl.when(step == 0)
     def _():
@@ -1153,76 +1199,102 @@
         own_acc[...] = jnp.zeros_like(own_acc)
         spot.meet()
         adder.start()
-        for t in range(4):
-            fetch.start(t)
-        fetch.spread(q0)
+        for t in range(11):
+            lines.start(t)
         adder.plane()
-        fetch.spread(o0)
+        spread(k0)
+        spread(v0)
         adder.column()
-        fetch.relay(q0)
+        spread(q0)
+        plane.relay(k0)
+        spread(o0)
+        plane.relay(v0)
         gains_ref[...] = adder.total()
-        fetch.share(q0)
-        fetch.spread(u0)
-        fetch.close(q0)
-        fetch.relay(o0)
-        fetch.finish(q0)
-        copy = pltpu.make_async_copy(fq, wq_in, wq_sem)
-        copy.start()
-        copy.wait()
-
-    when(step == 1, does(fetch.share, o0))
-    when(step == 2, does(fetch.relay, u0), does(fetch.share, u0))
-    when(step == 3, does(fetch.close, o0))
-
-    @pl.when(step < batch)
-    def _():
-        unit, _ = normed(x_ref[0].astype(F32))
-        n_one = (unit * gains_ref[0:1]).astype(BF16)
-        pick = span_adder(step, batch, spans, tokens)
-        for part in range(3):
-            cols = slice(part * D, (part + 1) * D)
-            block = dot(n_one, whole_weight(wq_in, cols)).astype(BF16)
-            qkv_ref[0, :, cols] = block
-            qkv_all[step, :, cols] = block
-            if part > 0:
-                own_acc[:, (part - 1) * D : part * D] += dot(pick, block)
-
-    when(step == half - 1, does(send_means, exchange, 0, own_acc))
-    when(step == half, does(fetch.spread, d0))
-    when(step == half + 1, does(fetch.close, u0))
-    when(step == batch - 1, does(send_means, exchange, 1, own_acc))
-
-    @pl.when(step == batch)
+
+        def norm(b, carry):
+            unit, _ = normed(x_ref[b].astype(F32))
+            n_all[b] = (unit * gains_ref[0:1]).astype(BF16)
+            return carry
+
+        lax.fori_loop(0, batch // 2, norm, 0)
+        plane.relay(q0)
+        lax.fori_loop(batch // 2, batch, norm, 0)
+        settle(k0)
+
+    @pl.when(step == 2)
+    def _():
+        plane.relay(o0)
+        spread(ua)
+        settle(v0)
+
+    @pl.when(step == 3)
+    def _():
+        spread(ub)
+        plane.relay(ua)
+        settle(q0)
+
+    for at, part in enumerate(QKV_ORDER):
+
+        @pl.when(step == 1 + at)
+        def _(at=at, part=part):
+            weight = inner[at]
+
+            def project(b, carry):
+                block = dot(n_all[b], weight[...].reshape((D, D))).astype(BF16)
+                qkv_all[b, :, part * D : (part + 1) * D] = block
+                if part > 0:
+                    pick = span_adder(b, batch, spans, tokens)
+                    own_acc[:, (part - 1) * D : part * D] += dot(pick, block)
+                return carry
+
+            lax.fori_loop(0, batch, project, 0)
+
+    @pl.when(step == 2)
+    def _():
+        send_means(exchange, 0, own_acc)
+        send_means(exchange, 1, own_acc)
+
+    @pl.when(step == first)
     def _():
         complete(exchange.spread(0))
-        fetch.finish(o0)
-        fetch.finish(u0)
-
-    when(step == batch + half - 1, does(fetch.relay, d0), does(fetch.share, d0))
-
-    @pl.when(step == batch + half)
-    def _():
         complete(exchange.spread(1))
-
-    when(step == 2 * batch - 2, does(fetch.close, d0))
-
-    @pl.when(jnp.logical_and(step >= batch, step < batch + half))
-    def _():
-        sums_ref[0] = pick_sums(step - batch, counts, spot.nseq, land_a[...])
-
-    @pl.when(step >= batch + half)
-    def _():
-        sums_ref[0] = pick_sums(step - batch - half, counts, spot.nseq, land_b[...])
-
-    @pl.when(step >= batch)
-    def _():
-        attention_forward(qkv_all.at[pl.ds(step - batch, 1)], sums_ref, bias_ref, prob_ref, o_ref)
-
-    @pl.when(step == 2 * batch - 1)
-    def _():
-        fetch.finish(d0)
-        for t in range(4):
-            fetch.drain(t)
+        for b in range(batch):
+            record(b).start()
+        spread(d0)
+        plane.close(o0)
+
+    when(step == first + 2, does(plane.relay, ub), does(plane.finish, o0))
+    when(step == first + 3, does(plane.close, ua))
+    when(step == first + 6, does(plane.relay, d0), does(plane.finish, ua))
+    when(step == first + 7, does(plane.close, ub))
+
+    @pl.when(jnp.logical_and(step >= first, step < first + half))
+    def _():
+        sums_ref[0] = pick_sums(step - first, counts, spot.nseq, land_a[...])
+
+    @pl.when(step >= first + half)
+    def _():
+        sums_ref[0] = pick_sums(step - first - half, counts, spot.nseq, land_b[...])
+
+    @pl.when(step >= first)
+    def _():
+        attention_forward(qkv_all.at[pl.ds(step - first, 1)], sums_ref, bias_ref, prob_ref, o_ref)
+
+    @pl.when(step == first + batch - 1)
+    def _():
+        plane.close(d0)
+        plane.finish(ub)
+        for t in range(7, 11):
+            lines.arrive(t)
+        plane.finish(d0)
+        for t in range(PARTS):
+            keep(t).wait()
+        for b in range(batch):
+            record(b).wait()
+        for t in range(11):
+            lines.drain(t)
+        for t in range(7):
+            plane.drain(t)
         adder.drain()
 
 
@@ -1241,8 +1313,12 @@
                                 collective_id=collective_id, has_side_effects=True)
 
 
-def full_shape(weights):
-    return sds((lax.axis_size("dp"), lax.axis_size("seq")) + weights.shape[1:], weights.dtype)
+def full_shape(shape):
+    return sds((lax.axis_size("dp"), lax.axis_size("seq")) + tuple(shape), BF16)
+
+
+def col_shape(weights):
+    return sds((lax.axis_size("dp"),) + weights.shape[1:], BF16)
 
 
 def exchange_buffers(nseq, rows):
@@ -1257,21 +1333,28 @@
     nz, nseq = lax.axis_size("dp"), lax.axis_size("seq")
     rows = batch * spans
     keys = SPAN + nseq * spans
+    own_rows = wq.shape[1]
+    square = full_shape((own_rows, D))
     outs = [sds((batch, tokens, 3 * D), BF16), sds((batch, nseq * spans, 2 * D), BF16),
             sds((batch, spans, PAIRS, keys, 2 * SPAN), BF16), sds((batch, tokens, D), BF16),
-            sds(gain_own.shape, F32)] + [full_shape(w) for w in (wq, wo, wu, wd)]
+            sds(gain_own.shape, F32)] + [square] * PARTS + [full_shape(w.shape[1:]) for w in (wo, wu, wd)]
+    outs += [col_shape(w) for w in (wq, wu, wd, wo)]
+    cols = [(own_rows, D)] * (PARTS + 1) + [(own_rows, wu.shape[2] // U_CUTS)] * U_CUTS + [wd.shape[1:]]
+    first = PARTS + 1
     return pl.pallas_call(
         functools.partial(enter_kernel, (batch, spans)),
-        grid=(2 * batch,),
-        in_specs=[phased(x.shape, 0, batch), phased(bias.shape, batch, batch)]
+        grid=(first + batch,),
+        in_specs=[whole(x.shape), phased(bias.shape, first, batch)]
         + [whole(a.shape) for a in (gain_own, wq, wo, wu, wd)],
-        out_specs=[phased(outs[0].shape, 0, batch)] + [phased(o.shape, batch, batch) for o in outs[1:4]]
-        + [whole(gain_own.shape)] + [anywhere()] * 4,
+        out_specs=[anywhere()] + [phased(o.shape, first, batch) for o in outs[1:4]]
+        + [whole(gain_own.shape)] + [anywhere()] * (PARTS + 7),
         out_shape=outs,
-        scratch_shapes=[pltpu.VMEM((batch, tokens, 3 * D), BF16), pltpu.VMEM((rows, 2 * D), F32)]
-        + exchange_buffers(nseq, rows)
-        + [pltpu.VMEM(outs[5].shape, BF16), pltpu.SemaphoreType.DMA] + Exchange.sems(nseq)
-        + Fetch.scratch(4, nz) + AllSum.scratch(gain_own.shape, nz),
+        scratch_shapes=[pltpu.VMEM(x.shape, BF16), pltpu.VMEM((batch, tokens, 3 * D), BF16),
+                        pltpu.VMEM((rows, 2 * D), F32)]
+        + exchange_buffers(nseq, rows) + [pltpu.VMEM(square.shape, BF16)] * PARTS
+        + [dma(PARTS), dma(batch)] + Exchange.sems(nseq)
+        + [pltpu.VMEM((nz,) + tuple(c), BF16) for c in cols]
+        + Lines.sems(11, nz) + Plane.sems(7) + AllSum.scratch(gain_own.shape, nz),
         compiler_params=fused_params(0),
         name="enter",
     )(x, bias, gain_own, wq, wo, wu, wd)
@@ -1279,14 +1362,15 @@
 
 def mid_kernel(counts, *refs):
     batch, spans = counts
-    (x_ref, o_ref, gains_ref, wo_ref, wu_ref, wd_ref, wq_sh, wo_sh, wu_sh, wd_sh,
+    (x_ref, o_ref, gains_ref, wo_ref, wu_ref, wd_ref, cq, cu, cd, co,
      h_ref, u_ref, next_ref, qkv_ref, raw_ref, fq, fo, fu, fd,
      next_all, own_acc, own_a, own_b, land_a, land_b, wq_in, wq_sem, ex_s, ex_r) = refs[:29]
     spot = Spot()
-    fetch = Fetch(spot, [wq_sh.at[1], wu_sh.at[1], wd_sh.at[1], wo_sh.at[1]], [fq, fu, fd, fo], refs[29:])
+    plane = Plane(spot, [cq, cu, cd, co], [wq_in, fu, fd, fo], refs[29:])
     exchange = Exchange(spot, [own_a, own_b], [land_a, land_b], ex_s, ex_r)
     q1, u1, d1, o1 = range(4)
     step = pl.program_id(0)
+    keep = pltpu.make_async_copy(wq_in, fq, wq_sem)
 
     @pl.when(step == 0)
     def _():
@@ -1297,32 +1381,19 @@
     def _():
         hidden = x_ref[0].astype(F32) + dot(o_ref[0], wo_ref[...])
         h_ref[0] = hidden
-
-        @pl.when(step == 0)
-        def _():
-            spot.meet()
-            for t in range(4):
-                fetch.start(t)
-
-        when(step == 2, does(fetch.spread, q1))
-        when(step == 4, does(fetch.relay, q1), does(fetch.share, q1), does(fetch.spread, u1))
-        when(step == 5, does(fetch.close, q1))
-        when(step == 6, does(fetch.spread, d1))
-        when(step == 7, does(fetch.relay, u1), does(fetch.share, u1), does(fetch.spread, o1), does(fetch.finish, q1))
+        when(step == 0, does(spot.meet), does(plane.spread, q1), does(plane.spread, u1))
         result = mlp_forward(hidden, gains_ref[2:3], wu_ref, wd_ref, u_ref)
         next_ref[0] = result
         next_all[step] = result
 
-    @pl.when(step == batch)
-    def _():
-        copy = pltpu.make_async_copy(fq, wq_in, wq_sem)
-        copy.start()
-        copy.wait()
-
-    when(step == batch + 2, does(fetch.close, u1), does(fetch.relay, d1), does(fetch.share, d1))
-    when(step == batch + 4, does(fetch.relay, o1), does(fetch.share, o1), does(fetch.close, d1))
-    when(step == batch + 6, does(fetch.close, o1), does(fetch.finish, u1))
-    when(step == batch + 7, does(fetch.finish, d1))
+    when(step == 3, does(plane.relay, q1), does(plane.spread, d1))
+    when(step == 5, does(plane.relay, u1), does(plane.spread, o1))
+    when(step == 6, does(plane.close, q1))
+    when(step == batch, does(plane.finish, q1), does(keep.start), does(plane.relay, d1))
+    when(step == batch + 1, does(plane.close, u1))
+    when(step == batch + 2, does(plane.relay, o1))
+    when(step == batch + 5, does(plane.close, d1), does(plane.finish, u1))
+    when(step == batch + 6, does(plane.close, o1))
 
     @pl.when(step >= batch)
     def _():
@@ -1341,24 +1412,26 @@
     @pl.when(step == 2 * batch - 1)
     def _():
         send_means(exchange, 1, own_acc)
-        fetch.finish(o1)
+        plane.finish(d1)
+        plane.finish(o1)
+        keep.wait()
         for t in range(4):
-            fetch.drain(t)
+            plane.drain(t)
         complete(exchange.spread(0))
         raw_ref[0] = land_a[...]
         complete(exchange.spread(1))
         raw_ref[1] = land_b[...]
 
 
-def call_mid(x, o, gains, wo, wu, wd, wq_sh, wo_sh, wu_sh, wd_sh):
+def call_mid(x, o, gains, wo, wu, wd, cq, cu, cd, co):
     batch, tokens, _ = x.shape
     spans = tokens // SPAN
-    nz, nseq = lax.axis_size("dp"), lax.axis_size("seq")
+    nseq = lax.axis_size("seq")
     rows = batch * spans
     outs = [sds((batch, tokens, D), F32), sds((batch, tokens, wu.shape[1]), BF16), sds((batch, tokens, D), F32),
             sds((batch, tokens, 3 * D), BF16), sds((HALVES, nseq, rows // HALVES, 2 * D), BF16)]
-    outs += [full_shape(w) for w in (wq_sh, wo_sh, wu_sh, wd_sh)]
-    args = [x, o, gains, wo, wu, wd, wq_sh, wo_sh, wu_sh, wd_sh]
+    outs += [full_shape(c.shape[1:]) for c in (cq, co, cu, cd)]
+    args = [x, o, gains, wo, wu, wd, cq, cu, cd, co]
     return pl.pallas_call(
         functools.partial(mid_kernel, (batch, spans)),
         grid=(2 * batch,),
@@ -1367,23 +1440,36 @@
         + [whole(outs[4].shape)] + [anywhere()] * 4,
         out_shape=outs,
         scratch_shapes=[pltpu.VMEM(x.shape, F32), pltpu.VMEM((rows, 2 * D), F32)] + exchange_buffers(nseq, rows)
-        + [pltpu.VMEM(outs[5].shape, BF16), pltpu.SemaphoreType.DMA] + Exchange.sems(nseq)
-        + Fetch.scratch(4, nz),
+        + [pltpu.VMEM(outs[5].shape, BF16), pltpu.SemaphoreType.DMA] + Exchange.sems(nseq) + Plane.sems(4),
         compiler_params=fused_params(1),
         name="mid",
     )(*args)
 
 
+TEAM = 2
+
+
+def flat_rows(ref):
+    return ref[...].reshape((-1, ref.shape[-1]))
+
+
+def per_team(shape):
+    rest = len(shape) - 1
+    return pl.BlockSpec((TEAM,) + tuple(shape[1:]), lambda b: (b,) + (0,) * rest)
+
+
 def top_kernel(counts, x_ref, qkv_ref, bias_ref, raw_ref, gains_ref, wo_ref, wu_ref, wd_ref,
                sums_ref, prob_ref, o_ref, h_ref, u_ref, next_ref):
     batch, spans, nseq = counts
-    b, half = pl.program_id(0), batch // HALVES
-    sums_ref[0] = pick_sums(lax.rem(b, half), (batch, spans), nseq, raw_ref[lax.div(b, half)])
-    attention_forward(qkv_ref, sums_ref, bias_ref, prob_ref, o_ref)
-    hidden = x_ref[0] + dot(o_ref[0], wo_ref[...])
-    h_ref[0] = hidden
+    half = batch // HALVES
+    for i in range(TEAM):
+        b, one = pl.program_id(0) * TEAM + i, pl.ds(i, 1)
+        sums_ref[i] = pick_sums(lax.rem(b, half), (batch, spans), nseq, raw_ref[lax.div(b, half)])
+        attention_forward(qkv_ref.at[one], sums_ref.at[one], bias_ref.at[one], prob_ref.at[one], o_ref.at[one])
+    hidden = flat_rows(x_ref) + dot(flat_rows(o_ref), wo_ref[...])
+    h_ref[...] = hidden.reshape(h_ref.shape)
     result = mlp_forward(hidden, gains_ref[3:4], wu_ref, wd_ref, u_ref)
-    next_ref[0] = result.astype(next_ref.dtype)
+    next_ref[...] = result.reshape(next_ref.shape).astype(next_ref.dtype)
 
 
 def call_top(x, qkv, bias, raw, gains, wo, wu, wd):
@@ -1396,9 +1482,9 @@
     args = [x, qkv, bias, raw, gains, wo, wu, wd]
     return pl.pallas_call(
         functools.partial(top_kernel, (batch, spans, nseq)),
-        grid=(batch,),
-        in_specs=[per_seq(a.shape) for a in args[:3]] + [whole(a.shape) for a in args[3:]],
-        out_specs=[per_seq(a.shape) for a in outs],
+        grid=(batch // TEAM,),
+        in_specs=[per_team(a.shape) for a in args[:3]] + [whole(a.shape) for a in args[3:]],
+        out_specs=[per_team(a.shape) for a in outs],
         out_shape=outs,
         compiler_params=params(),
         name="top",
@@ -1407,13 +1493,13 @@
 
 def mlp_back(dy32, u_ref, h_ref, o_ref, gain, wo_ref, wu_ref, wd_ref, dh_ref, gd_ref, gu_ref, go_ref, gg_ref):
     ddown = dy32.astype(BF16)
-    unit, rstd = normed(h_ref[0])
+    unit, rstd = normed(flat_rows(h_ref))
     n_two = (unit * gain).astype(BF16)
     dn_two = 0.0
     for start in range(0, wu_ref.shape[1], CHUNK):
         cols = slice(start, start + CHUNK)
         dactive = dot(ddown, wd_ref[cols, :], NT)
-        active, slope = gelu_both(u_ref[0, :, cols].astype(F32))
+        active, slope = gelu_both(u_ref[:, :, cols].reshape((-1, CHUNK)).astype(F32))
         gd_ref[cols, :] += dot(active.astype(BF16), ddown, TN)
         dupper = (dactive * slope).astype(BF16)
         gu_ref[:, cols] += dot(n_two, dupper, TN)
@@ -1421,9 +1507,9 @@
     dnorm, grad_gain = norm_backward(dn_two, unit, rstd, gain)
     gg_ref[...] += grad_gain
     dhidden = dy32 + dnorm
-    dh_ref[0] = dhidden
+    dh_ref[...] = dhidden.reshape(dh_ref.shape)
     dattn = dhidden.astype(BF16)
-    go_ref[...] += dot(o_ref[0], dattn, TN)
+    go_ref[...] += dot(flat_rows(o_ref), dattn, TN)
     return dot(dattn, wo_ref[...], NT).astype(BF16)
 
 
@@ -1475,17 +1561,21 @@
         spot.signal()
         zero(gd_ref, gu_ref, go_ref, gg_ref, part_acc)
 
-    dout = mlp_back(dy_ref[0].astype(F32), u_ref, h_ref, o_ref, gains_ref[3:4], wo_ref, wu_ref, wd_ref,
+    dout = mlp_back(flat_rows(dy_ref).astype(F32), u_ref, h_ref, o_ref, gains_ref[3:4], wo_ref, wu_ref, wd_ref,
                     dh_ref, gd_ref, gu_ref, go_ref, gg_ref)
-    attention_backward(qkv_ref, sums_ref, prob_ref, dout, dqkv_ref, dsums)
-    pile(step, counts, spot.nseq, dsums, part_acc)
-
-    @pl.when(step == batch // HALVES - 1)
+    tokens = dy_ref.shape[1]
+    for i in range(TEAM):
+        one = pl.ds(i, 1)
+        attention_backward(qkv_ref.at[one], sums_ref.at[one], prob_ref.at[one], dout[i * tokens : (i + 1) * tokens],
+                           dqkv_ref.at[one], dsums)
+        pile(step * TEAM + i, counts, spot.nseq, dsums, part_acc)
+
+    @pl.when(step == batch // HALVES // TEAM - 1)
     def _():
         spot.meet()
         ship(exchange, 0, part_acc)
 
-    @pl.when(step == batch - 1)
+    @pl.when(step == batch // TEAM - 1)
     def _():
         ship(exchange, 1, part_acc)
         gd_out[...] = gd_ref[...].astype(BF16)
@@ -1505,9 +1595,9 @@
             sds(wu.shape, BF16), sds(wo.shape, BF16), sds((1, D), F32)]
     return pl.pallas_call(
         functools.partial(base_kernel, (batch, spans)),
-        grid=(batch,),
-        in_specs=[per_seq(a.shape) for a in args[:7]] + [whole(a.shape) for a in args[7:]],
-        out_specs=[per_seq(a.shape) for a in outs[:2]] + [whole(a.shape) for a in outs[2:]],
+        grid=(batch // TEAM,),
+        in_specs=[per_team(a.shape) for a in args[:7]] + [whole(a.shape) for a in args[7:]],
+        out_specs=[per_team(a.shape) for a in outs[:2]] + [whole(a.shape) for a in outs[2:]],
         out_shape=outs,
         scratch_shapes=[pltpu.VMEM(wd.shape, F32), pltpu.VMEM(wu.shape, F32), pltpu.VMEM(wo.shape, F32),
                         pltpu.VMEM((1, nseq * spans, 2 * D), BF16)]
@@ -1560,20 +1650,22 @@
         for t in range(3):
             fold.start(t)
 
-    when(step == 3, does(fold.combine, d1))
-    when(step == 4, does(fold.combine, u1))
-    when(step == 5, does(fold.combine, o1))
-    when(step == 7, does(fold.middle, d1))
+    when(step == 4, does(fold.combine, d1))
+    when(step == 5, does(fold.combine, u1))
+    when(step == 6, does(fold.combine, o1))
 
     @pl.when(step == batch)
     def _():
         gq_low[...] = gq_ref[...].astype(BF16).reshape(gq_low.shape)
         fold.start(q1)
+        fold.middle(d1)
 
     when(step == batch + 1, does(fold.middle, u1), does(fold.middle, o1), does(fold.combine, q1))
-    when(step == batch + 2, does(fold.column, d1), does(fold.column, u1), does(fold.column, o1))
-    when(step == batch + 4, does(fold.middle, q1))
-    when(step == batch + 5, does(fold.finish, d1), does(fold.finish, u1), does(fold.finish, o1), does(fold.column, q1))
+    when(step == batch + 2, does(fold.column, d1))
+    when(step == batch + 3, does(fold.column, u1), does(fold.column, o1), does(fold.middle, q1))
+    when(step == batch + 4, does(fold.column, q1))
+    when(step == batch + 5, does(fold.finish, d1))
+    when(step == batch + 6, does(fold.finish, u1), does(fold.finish, o1))
     when(step == batch + 7, does(fold.finish, q1))
 
     @pl.when(step < batch)
@@ -1639,12 +1731,12 @@
 
 def leave_kernel(counts, *refs):
     batch, spans = counts
-    (prob_ref, qkv_ref, sums_ref, dout_ref, x_ref, dh_ref, gains_ref, wq_ref, g_mlp0, g_attn1, g_mlp1,
+    (prob_ref, qkv_ref, sums_ref, dout_ref, x_ref, dh_ref, gains_ref, w0, w1, w2, g_mlp0, g_attn1, g_mlp1,
      pd, pu, po,
      dx_ref, gsum_ref, sd, su, so, s0, s1, s2,
      near_all, unit_all, rstd_all, a0, a1, a2, l0, l1, l2, gg_ref, gain_src, dsums,
-     part_acc, part_a, part_b, land_a, land_b, total, ex_s, ex_r) = refs[:42]
-    rest = refs[42:]
+     part_acc, part_a, part_b, land_a, land_b, total, ex_s, ex_r) = refs[:44]
+    rest = refs[44:]
     spot = Spot()
     fold = Fold(spot, [pd, pu, po, l0, l1, l2], [sd, su, so, s0, s1, s2], rest[:36], rest[36:43])
     adder = AllSum(spot, gain_src, rest[43:])
@@ -1703,7 +1795,7 @@
         dx_ref[0] = qkv_back(
             unit_all[b], rstd_all[b], gains_ref[0:1], lambda cols: near_all[b, :, cols],
             lambda span, cols: total[pl.ds(b * spans + span, 1), cols], dh_ref[0],
-            lambda cols: wq_ref[:, cols], [a0, a1, a2], gg_ref, (0,))
+            lambda cols: (w0, w1, w2)[cols.start // D][...], [a0, a1, a2], gg_ref, (0,))
 
     @pl.when(step == 2 * batch - 1)
     def _():
@@ -1736,7 +1828,7 @@
         adder.drain()
 
 
-def call_leave(prob, qkv, sums, dout, x, dh, gains, wq, g_mlp0, g_attn1, g_mlp1, pd, pu, po):
+def call_leave(prob, qkv, sums, dout, x, dh, gains, w0, w1, w2, g_mlp0, g_attn1, g_mlp1, pd, pu, po):
     batch, tokens, _ = x.shape
     spans = tokens // SPAN
     nz, nseq = lax.axis_size("dp"), lax.axis_size("seq")
@@ -1745,13 +1837,13 @@
     square = (D, D)
     owned = (nz, nseq // CORES, CORES, D // (nz * nseq), D)
     shapes = [a.shape[3:] for a in parts] + [owned[3:]] * 3
-    args = [prob, qkv, sums, dout, x, dh, gains, wq, g_mlp0, g_attn1, g_mlp1] + parts
+    args = [prob, qkv, sums, dout, x, dh, gains, w0, w1, w2, g_mlp0, g_attn1, g_mlp1] + parts
     outs = [sds(dh.shape, F32), sds(gains.shape, F32)] + [sds(s, F32) for s in shapes]
     return pl.pallas_call(
         functools.partial(leave_kernel, (batch, spans)),
         grid=(2 * batch,),
         in_specs=[phased(a.shape, 0, batch) for a in args[:5]] + [phased(dh.shape, batch, batch)]
-        + [whole(a.shape) for a in args[6:11]] + [anywhere()] * 3,
+        + [whole(a.shape) for a in args[6:13]] + [anywhere()] * 3,
         out_specs=[phased(outs[0].shape, batch, batch)] + [whole(a.shape) for a in outs[1:]],
         out_shape=outs,
         scratch_shapes=[pltpu.VMEM(qkv.shape, BF16), pltpu.VMEM(x.shape, F32), pltpu.VMEM((batch, tokens, 1), F32)]
@@ -1801,11 +1893,11 @@
     def flat(a):
         return a.reshape((-1, a.shape[-1]))
 
-    qkv0, sums0, prob0, o0, gains, wq0, wo0, wu0, wd0 = call_enter(
+    qkv0, sums0, prob0, o0, gains, wk0, wv0, wq0, wo0, wu0, wd0, cq1, cu1, cd1, co1 = call_enter(
         inputs, bias, gain_own, w_qkv, w_out, w_up, w_down)
-    wq0, wo0, wu0, wd0 = (flat(a) for a in (wq0, wo0, wu0, wd0))
+    wk0, wv0, wq0, wo0, wu0, wd0 = (flat(a) for a in (wk0, wv0, wq0, wo0, wu0, wd0))
     h0, u0, x1, qkv1, raw1, wq1, wo1, wu1, wd1 = call_mid(
-        inputs, o0, gains, wo0, wu0, wd0, w_qkv, w_out, w_up, w_down)
+        inputs, o0, gains, wo0, wu0, wd0, cq1, cu1, cd1, co1)
     wq1, wo1, wu1, wd1 = (flat(a) for a in (wq1, wo1, wu1, wd1))
     sums1, prob1, o1, h1, u1, outputs = call_top(x1, qkv1, bias, raw1, gains, wo1, wu1, wd1)
     dh1, near1, total1, gd1, gu1, go1, g_mlp1 = call_base(
@@ -1813,7 +1905,7 @@
     dh0, dout0, gd0, gu0, go0, g_attn1, g_mlp0, sd1, su1, so1, sq1 = call_turn(
         x1, near1, dh1, u0, h0, o0, total1, gains, wq1, wo0, wu0, wd0, gd1, gu1, go1)
     dx, gsum, sd0, su0, so0, *sq0 = call_leave(
-        prob0, qkv0, sums0, dout0, inputs, dh0, gains, wq0, g_mlp0, g_attn1, g_mlp1, gd0, gu0, go0)
+        prob0, qkv0, sums0, dout0, inputs, dh0, gains, wq0, wk0, wv0, g_mlp0, g_attn1, g_mlp1, gd0, gu0, go0)
     gq, go, gu, gd = call_pack([[sq0, [sq1]], [[so0], [so1]], [[su0], [su1]], [[sd0], [sd1]]])
     gain_share = lax.dynamic_slice(gsum, (0, rank * slots), (4, slots))
     return outputs, dx, gq, go, gu, gd, gain_share[:2], gain_share[2:]

time: 323 us -> 308 us (0.954)
  Pallas kernels: 311 us -> 297 us
    pallas_call x1, Pallas kernels: 52.4 us -> 42.8 us  [call_mid(): pl.pallas_call(functools.partial(mid_kernel, (batch, spans)), grid=(2 * b...]
    pallas_call x1, Pallas kernels: 29.4 us -> 25.8 us  [call_top(): pl.pallas_call(functools.partial(top_kernel, (batch, spans, nseq)), grid=...]
where the time goes in v5:
time: 308 us
  Pallas kernels  297 us (96%)
  local copies, waits for them, and re-layouts  8.08 us (3%)
    pallas_call x1, Pallas kernels, call_turn(): pl.pallas_call(functools.partial(turn_kernel, (batch, tokens // SPAN)), g...  64.5 us
    pallas_call x1, Pallas kernels, call_enter(): pl.pallas_call(functools.partial(enter_kernel, (batch, spans)), grid=(fir...  56.9 us
    pallas_call x1, Pallas kernels, call_leave(): pl.pallas_call(functools.partial(leave_kernel, (batch, spans)), grid=(2 *...  54.2 us
    pallas_call x1, Pallas kernels, call_base(): pl.pallas_call(functools.partial(base_kernel, (batch, spans)), grid=(batc...  50.5 us
    pallas_call x1, Pallas kernels, call_mid(): pl.pallas_call(functools.partial(mid_kernel, (batch, spans)), grid=(2 * b...  42.8 us
    pallas_call x1, Pallas kernels, call_top(): pl.pallas_call(functools.partial(top_kernel, (batch, spans, nseq)), grid=...  25.8 us

profile of v5, /device:TPU:0, one launch (start us, length us, event | category | flops | bytes accessed | tf_op | source)
XLA Modules:
  0.0 308.1 jit_solution(1204601506496515942)
XLA Ops:
  0.7 0.1 iota_compare_fusion.2
  0.7 0.7 fusion.3
  1.4 0.7 constant_dynamic-slice_fusion.1
  2.1 0.2 dynamic_update_slice.3.refs_2_
  2.4 0.0 copy-start
  2.4 0.9 copy.19
  3.3 0.3 slice_reduce_fusion
  3.6 0.1 compare_and_fusion.1
  3.7 0.3 compare_and_fusion
  4.0 1.2 add_select_fusion.refs_1_.bias_ref
  5.2 0.0 copy-done
  5.2 56.9 %enter.1 = (bf16[8,256,1536]{2,1,0:T(8,128)(2,1)}, bf16[8,16,1024]{2,1,0:T(8,128)(2,1)}, bf16[8,2,4,144,256]{4,3,2,1,0:T(8,128)(2,1)}, bf16[8,256,512]{2,1,0:T(8...) custom-call(bf16[8,256,512]{2,1,0:T(8,128)(2,1)} %refs_4_.3, ...), custom_call_target="tpu_custom_call" | custom-call | tf_op jit(solution)/shard_map/enter/pallas_call | solution.py:1344
  62.2 42.8 %mid.1 = (f32[8,256,512]{2,1,0:T(8,128)}, bf16[8,256,2048]{2,1,0:T(8,128)(2,1)}, f32[8,256,512]{2,1,0:T(8,128)}, bf16[8,256,1536]{2,1,0:T(8,128)(2,1)}, bf16[2,8...) custom-call(bf16[8,256,512]{2,1,0:T(8,128)(2,1)} %refs_4_.3, ...), custom_call_target="tpu_custom_call" | custom-call | tf_op jit(solution)/shard_map/mid/pallas_call | solution.py:1435
  105.0 25.8 %top.1 = (bf16[8,16,1024]{2,1,0:T(8,128)(2,1)}, bf16[8,2,4,144,256]{4,3,2,1,0:T(8,128)(2,1)}, bf16[8,256,512]{2,1,0:T(8,128)(2,1)}, f32[8,256,512]{2,1,0:T(8,128...) custom-call(f32[8,256,512]{2,1,0:T(8,128)} %get-tuple-element.77.x_ref.refs_0_, ...), custom_call_target="tpu_custom_call" | custom-call | tf_op jit(solution)/shard_map/top/pallas_call | solution.py:1483
  130.8 50.5 %base.1 = (f32[8,256,512]{2,1,0:T(8,128)}, bf16[8,256,1536]{2,1,0:T(8,128)(2,1)}, f32[16,1024]{1,0:T(8,128)}, bf16[2048,512]{1,0:T(8,128)(2,1)}, bf16[512,2048]{...) custom-call(bf16[8,256,512]{2,1,0:T(8,128)(2,1)} %refs_0_.5, ...), custom_call_target="tpu_custom_call" | custom-call | tf_op jit(solution)/shard_map/base/pallas_call | solution.py:1596
  181.3 64.5 %turn.1 = (f32[8,256,512]{2,1,0:T(8,128)}, bf16[8,256,512]{2,1,0:T(8,128)(2,1)}, bf16[2048,512]{1,0:T(8,128)(2,1)}, bf16[512,2048]{1,0:T(8,128)(2,1)}, bf16[512,...) custom-call(f32[8,256,512]{2,1,0:T(8,128)} %get-tuple-element.77.x_r, ...), custom_call_target="tpu_custom_call" | custom-call | tf_op jit(solution)/shard_map/turn/pallas_call | solution.py:1707
  245.8 54.2 %leave.1 = (f32[8,256,512]{2,1,0:T(8,128)}, f32[8,512]{1,0:T(8,128)}, f32[64,512]{1,0:T(8,128)}, f32[16,2048]{1,0:T(8,128)}, f32[16,512]{1,0:T(8,128)}, /*index=...) custom-call(bf16[8,2,4,144,256]{4,3,2,1,0:T(8,128)(2,1)} %get-tuple-element.84.refs_0_, ...), custom_call_target="tpu_custom_call" | custom-call | tf_op jit(solution)/shard_map/leave/pallas_call | solution.py:1842
  300.0 0.8 constant_dynamic-slice_fusion
  300.8 0.6 fusion.4
  301.4 2.1 pack.1
  303.5 4.6 %copy.22 = f32[8,256,512]{2,1,0:T(8,128)} copy(f32[8,256,512]{2,1,0:T(8,128)} %get-tuple-element.139) | data formatting | bytes 8388608
  (4 shorter events, 0.0 us)
Async XLA Ops:
  2.4 2.9 copy-start
